TPU v7x, 128 devices: a whole 4x4x4 slice. The times are simulated.
128 devices in a mesh: blk: 64 (over x, y_hi, z, core), rep: 2 (over y_lo).
Axes of the slice: x: 4, y: 4 (y_hi: 2, y_lo: 2; y = y_hi * 2 + y_lo), z: 4, core: 2. Of those that a mesh axis runs over, the one named last changes fastest.
Arguments:
- captions: bfloat16 [24576, 768], P(('blk', 'rep')), may hold values from -512 to 512
- images: bfloat16 [24576, 768], P(('blk', 'rep')), may hold values from -512 to 512
- positives: int32 [24576], P(('blk', 'rep')), may hold values from 0 to 24575, each once
- valid: int32 [24576], P(('blk', 'rep')), may hold values from 0 to 1, as said below
Outputs:
- caption_loss: float32 [24576], P(('blk', 'rep'))
- image_loss: float32 [24576], P(('blk', 'rep'))
- loss: float32 [], replicated
Inputs may be any that keep to these rules, and one draw needn't show every extreme that they name: `positives`: each image row is the positive of exactly one caption; a program may pack several of these indices into one sent element. `valid`: the last image row is always real; a program may pack several of these flags into one sent element.
All inputs are finite; a program needn't handle non-finite values.
Results may differ from a plain program's by a relative error of at most 0.0003.
Values may be sent and summed in bfloat16 or wider, within the bound.
No kernel may reach another device: no remote copies, remote signals or barrier semaphores. Data moves between devices by JAX's collectives and lax.ppermute only.
A program may use at most 128 MiB of HBM per device.

v0:
```python
import itertools

import jax
import jax.numpy as jnp
from jax import lax
from jax.experimental import pallas as pl
from jax.experimental.pallas import tpu as pltpu
from jax.sharding import Mesh
from jax.sharding import PartitionSpec as P


SIZES = {"x": 4, "h": 2, "z": 4, "c": 2, "l": 2}
AXES = tuple(SIZES)
LOG2E = 1.4426950408889634
LN2 = 0.6931471805599453
LOW = -1.0e30

B = 192
E = 768
MET = ((0, 0), (0, 1), (3, 0), (1, 0), (3, 1), (1, 1), (2, 0), (2, 1))
EARLY = 6
CAPS = len(MET)
IMGS = 2 * len(MET)
C = IMGS * B
RC = 448
R = -(-CAPS * B // RC) * RC
NC = 256
COUNTS = (2, 4, 5, 6, 7, 8, 10, 12)
PIECE = 64
GRAIN = 16
OK_BIT = 15
ABSENT = 9999.0

F32 = jnp.float32
BF16 = jnp.bfloat16
VMEM = pl.BlockSpec(memory_space=pltpu.VMEM)
SMEM = pl.BlockSpec(memory_space=pltpu.SMEM)


def send(value, to):
    pairs = []
    for at in itertools.product(*map(range, SIZES.values())):
        p = dict(zip(AXES, at))
        pairs.append((flat(p), flat({**p, **to(p)})))
    return lax.ppermute(value, AXES, pairs)


def other_core(p):
    return {"c": 1 - p["c"]}


def partner(p):
    return {"l": 1 - p["l"], "h": p["h"] ^ p["c"]}


def along(step):
    def to(p):
        axis = "x" if p["c"] else "z"
        return {axis: (p[axis] + step) % 4}

    return to


def place():
    return {a: lax.axis_index(a) for a in AXES}


def flat(p):
    at = 0
    for a in AXES:
        at = at * SIZES[a] + p[a]
    return at


def moved(p, off):
    q = dict(p)
    for a, d in off.items():
        q[a] = lax.rem(p[a] + d, SIZES[a])
    return q


def cap_place(p, k):
    step, y = MET[k]
    return moved(p, {"z": step, "l": y})


def img_place(p, m):
    step, y = MET[m // 2]
    return {**moved(p, {"x": step, "h": y, "l": y}), "c": m % 2}


def iota(shape, dim):
    return lax.broadcasted_iota(jnp.int32, shape, dim).astype(F32)


def dot(a, b):
    return jnp.dot(a, b, preferred_element_type=F32)


def earlier():
    return jnp.where(iota((B, B), 0) < iota((B, B), 1), 1.0, 0.0).astype(BF16)


def grains(n):
    return lax.shift_left(lax.shift_right_logical(n + (GRAIN - 1), 4), 4)


def pair_kernel(
    cap, img, positives, valid, cap_other, img_other, valid_other,
    carried, kept, words, ranks,
):
    first = lax.axis_index("c") == 0
    ok = jnp.concatenate([valid[...], valid_other[...]], axis=0)
    order = dot(jnp.broadcast_to(ok[:, None], (2, 8, B)).reshape(16, B).astype(F32).astype(BF16), earlier())
    found = jnp.where(ok > 0, jnp.concatenate([order[0:1], order[8:9]], axis=0), ABSENT)
    ranks[...] = found[0:1, :]
    words[...] = jnp.broadcast_to(
        positives[...] + valid[...] * (1 << OK_BIT), (128, B)
    ).reshape(128, 1, B)
    packed = []
    for i, block in enumerate((img, img_other)):
        pick = jnp.where(iota((B, B), 0) == found[i:i + 1, :], 1.0, 0.0).astype(BF16)
        packed.append(dot(pick, block[...]).astype(BF16))
    carried[0:B, :] = jnp.where(first, cap[...], packed[1])
    carried[B:2 * B, :] = jnp.where(first, cap_other[...], packed[0])
    kept[0:B, :] = jnp.where(first, packed[0], cap_other[...])
    kept[B:2 * B, :] = jnp.where(first, packed[1], cap[...])


def lookup_kernel(table, ranks, columns, counts, real, pos, words_v):
    p = place()
    words = table[...].reshape(128, B)
    words_v[...] = words
    ok = (lax.shift_right_logical(words, OK_BIT) & 1).astype(F32)
    rank = dot(ok.astype(BF16), earlier())
    real[...] = jnp.full((8, 128), jnp.sum(ok), F32)
    known = jnp.transpose(jnp.where(ok > 0, rank + 1.0, 0.0)).astype(BF16)
    for k in range(CAPS):
        row = words_v[pl.ds(flat(cap_place(p, k)), 1), :]
        pos[k:k + 1, :] = (row & ((1 << OK_BIT) - 1)).astype(F32)
    at = pos[...]
    hi = jnp.floor((at + 0.5) * (1.0 / B))
    lo = at - hi * B
    block = iota((128, B), 0)
    inner = iota((B, B), 0)
    for k in range(CAPS):
        pick = jnp.where(block == hi[k:k + 1, :], 1.0, 0.0).astype(BF16)
        column = dot(known, pick)
        pos[k:k + 1, :] = jnp.sum(
            jnp.where(inner == lo[k:k + 1, :], column, 0.0), axis=0, keepdims=True
        )
    value = pos[...]
    live = value > 0.0
    marks = jnp.where(live, 1.0, 0.0)
    order = dot(marks.astype(BF16), earlier())
    ranks[...] = jnp.where(live, order, ABSENT)
    start = jnp.zeros((1, 1), F32)
    base = jnp.full((CAPS, B), -ABSENT, F32)
    counts[0:CAPS, :] = jnp.broadcast_to(
        jnp.sum(marks, axis=1, keepdims=True).astype(jnp.int32), (CAPS, 128)
    )
    for m in range(IMGS):
        number = flat(img_place(p, m))
        row = words_v[pl.ds(number, 1), :]
        row = lax.shift_right_logical(row, OK_BIT) & 1
        count = jnp.sum(row.astype(F32), axis=1, keepdims=True)
        base = jnp.where(hi == number.astype(F32), start, base)
        start = start + jnp.floor((count + (GRAIN - 1.0)) * (1.0 / GRAIN)) * GRAIN
        counts[CAPS + m:CAPS + m + 1, :] = jnp.broadcast_to(count.astype(jnp.int32), (1, 128))
    targets = jnp.where(live, base + value - 1.0, -ABSENT)
    order = ranks[...]
    lane = iota((B, 128), 1)
    result = jnp.zeros((B, 128), F32)
    for k in range(CAPS):
        hit = inner == order[k:k + 1, :]
        target = jnp.sum(jnp.where(hit, targets[k:k + 1, :], 0.0), axis=1, keepdims=True)
        result = jnp.where(lane == float(k), target, result)
    columns[...] = result


def starts_of(counts, first, number):
    found, at = [], jnp.int32(0)
    for k in range(number):
        found.append(pl.multiple_of(at, GRAIN))
        at = at + grains(counts[first + k, 0])
    return found + [pl.multiple_of(at, GRAIN)]


def compact(counts, ranks, carried, kept, cap_out, img_out, first):
    core = lax.axis_index("c")
    slot = iota((B, B), 0)
    at = starts_of(counts, 0, CAPS)
    for k, (a, b) in enumerate(zip(carried, kept), first):
        block = jnp.where(core == 0, a[0:B, :], b[B:2 * B, :])
        pick = jnp.where(slot == ranks[k:k + 1, :], 1.0, 0.0).astype(BF16)
        cap_out[pl.ds(at[k], B), :] = dot(pick, block).astype(BF16)
    at = starts_of(counts, CAPS, IMGS)
    for k, (a, b) in enumerate(zip(carried, kept), first):
        for side in range(2):
            rows = pl.ds(side * B, B)
            img_out[pl.ds(at[2 * k + side], B), :] = jnp.where(core == 0, b[rows, :], a[rows, :])


def early_kernel(counts, ranks, *refs):
    cap_out, img_out = refs[2 * EARLY:]
    cap_out[...] = jnp.zeros(cap_out.shape, BF16)
    img_out[...] = jnp.zeros(img_out.shape, BF16)
    compact(counts, ranks, refs[:EARLY], refs[EARLY:2 * EARLY], cap_out, img_out, 0)


def late_kernel(counts, ranks, cap_in, img_in, *refs):
    del cap_in, img_in
    late = CAPS - EARLY
    cap_out, img_out = refs[2 * late:]
    compact(counts, ranks, refs[:late], refs[late:2 * late], cap_out, img_out, EARLY)


def score_kernel(
    counts, columns, cap_v, img_v, out, own_row,
    t_v, pos_b, bias_b, rmax, rmatch, rsum, col_bias, cmax, cmatch, csum, lines_v,
):
    img_at = starts_of(counts, CAPS, IMGS)
    column = iota((8, C), 1)
    bias = jnp.full((8, C), LOW, F32)
    for m in range(IMGS):
        begin = img_at[m].astype(F32)
        end = begin + counts[CAPS + m, 0].astype(F32)
        bias = jnp.where((column >= begin) & (column < end), 0.0, bias)
    col_bias[...] = bias
    cap_at = starts_of(counts, 0, CAPS)
    slot = iota((B, 128), 0)
    for k in range(CAPS):
        rows = pl.ds(cap_at[k], B)
        pos_b[rows, :] = jnp.broadcast_to(columns[:, k:k + 1], (B, 128))
        bias_b[rows, :] = jnp.where(slot < counts[k, 0].astype(F32), 0.0, LOW)
    rows_used = cap_at[CAPS]
    tail = pl.ds(rows_used, RC)
    bias_b[tail, :] = jnp.full((RC, 128), LOW, F32)
    pos_b[tail, :] = jnp.full((RC, 128), -ABSENT, F32)
    cmax[...] = jnp.full(cmax.shape, 4.0 * LOW, F32)
    cmatch[...] = jnp.zeros(cmatch.shape, F32)
    csum[...] = jnp.zeros(csum.shape, F32)

    def tiles(count):
        @pl.loop(0, lax.div(rows_used + (RC - 1), RC))
        def _(i):
            rows = pl.ds(pl.multiple_of(i * RC, RC), RC)
            a = cap_v[rows, :]
            for n in range(count):
                s = lax.dot_general(
                    a, img_v[n * NC:(n + 1) * NC, :], (((1,), (1,)), ((), ())),
                    preferred_element_type=F32,
                )
                q = s * LOG2E
                highest, found = None, None
                for half in range(2):
                    span = pl.ds(n * NC + half * 128, 128)
                    qh = q[:, half * 128:(half + 1) * 128]
                    t = (qh + bias_b[rows, :]) + col_bias[0:1, span]
                    t_v[rows, span] = t
                    number = iota((1, 128), 1) + float(n * NC + half * 128)
                    w = jnp.where(pos_b[rows, :] == number, qh, 0.0)
                    highest = t if half == 0 else jnp.maximum(highest, t)
                    found = w if half == 0 else found + w
                    cmax[:, span] = jnp.maximum(
                        cmax[:, span], jnp.max(t.reshape(-1, 8, 128), axis=0)
                    )
                    cmatch[:, span] += jnp.sum(w.reshape(-1, 8, 128), axis=0)
                if n == 0:
                    rmax[rows, :] = highest
                    rmatch[rows, :] = found
                else:
                    rmax[rows, :] = jnp.maximum(rmax[rows, :], highest)
                    rmatch[rows, :] += found
            rmax[rows, :] = jnp.broadcast_to(
                jnp.max(rmax[rows, :], axis=1, keepdims=True), (RC, 128)
            )

        top = jnp.max(cmax[...], axis=0, keepdims=True)
        cmax[...] = jnp.broadcast_to(top, cmax.shape)

        def piece(r, totals):
            rows = pl.ds(pl.multiple_of(r * PIECE, PIECE), PIECE)
            peak = rmax[rows, :]
            acc = jnp.zeros((PIECE, 128), F32)
            out = []
            for n in range(2 * count):
                t = t_v[rows, n * 128:(n + 1) * 128]
                acc = acc + jnp.exp2(t - peak)
                f = jnp.exp2(t.reshape(-1, 8, 128) - cmax[:, n * 128:(n + 1) * 128][None])
                out.append(totals[n] + jnp.sum(f, axis=0))
            rsum[rows, :] = acc
            return tuple(out)

        totals = lax.fori_loop(
            0, lax.div(rows_used + (PIECE - 1), PIECE), piece,
            tuple(jnp.zeros((8, 128), F32) for _ in range(2 * count)),
        )
        for n in range(2 * count):
            csum[:, n * 128:(n + 1) * 128] = totals[n]

    used = jnp.maximum(lax.div(img_at[IMGS] + (NC - 1), NC), 1)
    for below, count in zip((0, *COUNTS), COUNTS):
        pl.when((used > below) & (used <= count))(lambda count=count: tiles(count))

    p = place()
    lanes = lax.broadcasted_iota(jnp.int32, (B, 128), 1)
    for k in range(CAPS):
        rows = pl.ds(cap_at[k], B)
        total = jnp.sum(rsum[rows, :], axis=1, keepdims=True)
        match = jnp.sum(rmatch[rows, :], axis=1, keepdims=True)
        packed = jnp.where(lanes == 0, rmax[rows, :] + jnp.log2(total), match)
        lines = jnp.transpose(packed)
        if k:
            put(out, flat(cap_place(p, k)), lines)
        else:
            put(own_row, 0, lines)
    line = lax.broadcasted_iota(jnp.int32, (8, C), 0)
    total = jnp.sum(csum[...], axis=0, keepdims=True)
    match = jnp.sum(cmatch[...], axis=0, keepdims=True)
    lines_v[:, :C] = jnp.where(line == 0, cmax[0:1, :] + jnp.log2(total), match)
    lines_v[:, C:] = jnp.zeros((8, 384), F32)
    for m in range(IMGS):
        whole = lax.shift_left(lax.shift_right_logical(img_at[m], 7), 7)
        slab = lines_v[:, pl.ds(pl.multiple_of(whole, 128), 384)]
        slab = pltpu.roll(slab, lax.rem(384 - (img_at[m] - whole), 384), 1)
        put(out, flat(img_place(p, m)), slab)


def put(out, at, lines):
    for i in range(2):
        out[at, 0:1, i * B:(i + 1) * B] = lines[i:i + 1, :B]


def joined(parts, ranks):
    sums, matches = parts[:, :B], parts[:, B:]
    peak = jnp.max(sums, axis=0, keepdims=True)
    total = jnp.sum(jnp.exp2(sums - peak), axis=0, keepdims=True)
    match = jnp.sum(matches, axis=0, keepdims=True)
    packed = jnp.broadcast_to(LN2 * (peak - match + jnp.log2(total)), (8, B))
    packed = jnp.concatenate([packed, jnp.zeros((8, 256 - B), F32)], axis=1)
    column = jnp.transpose(packed)[:B, 0:1]
    return jnp.sum(jnp.where(iota((B, B), 0) == ranks, column, 0.0), axis=0, keepdims=True)


def loss_kernel(
    parts, own_row, row_ranks, col_ranks, real, caption_loss, image_loss, total, rows, cols
):
    p = place()
    rows[0:1, :] = own_row[0, :, :]
    for k in range(1, CAPS):
        rows[k:k + 1, :] = parts[flat(cap_place(p, k)), :, :]
    for m in range(IMGS):
        cols[m:m + 1, :] = parts[flat(img_place(p, m)), :, :]
    caption = joined(rows[...], row_ranks[0:1, :])
    image = joined(cols[...], col_ranks[...])
    caption_loss[...] = caption
    image_loss[...] = image
    both = jnp.sum(caption, axis=1, keepdims=True) + jnp.sum(image, axis=1, keepdims=True)
    share = both / (2.0 * real[0:1, 0:1])
    total[...] = jnp.broadcast_to(share, (128, 8)).reshape(128, 1, 8)


def small(mib, flops):
    return dict(
        compiler_params=pltpu.CompilerParams(vmem_limit_bytes=mib * 1024 * 1024),
        cost_estimate=pl.CostEstimate(flops=flops, bytes_accessed=10**6, transcendentals=0),
    )


def step(captions, images, positives, valid):
    shape = jax.ShapeDtypeStruct
    pair = shape((2 * B, E), BF16)
    others = [send(value, other_core) for value in (captions, images, valid[None])]
    carried, kept, words, image_ranks = pl.pallas_call(
        pair_kernel,
        out_shape=[pair, pair, shape((128, 1, B), jnp.int32), shape((1, B), F32)],
        in_specs=[VMEM] * 7,
        out_specs=[VMEM] * 4,
        **small(8, 10**8),
    )(captions, images, positives[None], valid[None], *others)
    near = send(carried, partner)
    a1, a3 = (send(carried, along(s)) for s in (1, 3))
    b1, b3 = (send(near, along(s)) for s in (1, 3))
    c1, c3 = send(a1, along(1)), send(b3, along(3))
    met = dict(y=near, a1=a1, a3=a3, b1=b1, b3=b3, c1=c1, c3=c3)
    swapped = [kept] + [send(v, other_core) for v in met.values()]
    carried = [carried, *met.values()]
    table = lax.all_to_all(words, AXES, 0, 0, tiled=True)
    ranks, columns, counts, real = pl.pallas_call(
        lookup_kernel,
        out_shape=[
            shape((CAPS, B), F32), shape((B, 128), F32),
            shape((CAPS + IMGS, 128), jnp.int32), shape((8, 128), F32),
        ],
        in_specs=[VMEM],
        out_specs=[VMEM] * 4,
        scratch_shapes=[pltpu.VMEM((CAPS, B), F32), pltpu.VMEM((128, B), jnp.int32)],
        **small(4, 3 * 10**9),
    )(table)
    packed_shapes = [shape((R, E), BF16), shape((C, E), BF16)]
    cap_v, img_v = pl.pallas_call(
        early_kernel,
        out_shape=packed_shapes,
        in_specs=[SMEM] + [VMEM] * (1 + 2 * EARLY),
        out_specs=[VMEM] * 2,
        **small(12, 2 * 10**9),
    )(counts, ranks, *carried[:EARLY], *swapped[:EARLY])
    cap_v, img_v = pl.pallas_call(
        late_kernel,
        out_shape=packed_shapes,
        in_specs=[SMEM] + [VMEM] * (3 + 2 * (CAPS - EARLY)),
        out_specs=[VMEM] * 2,
        input_output_aliases={2: 0, 3: 1},
        **small(12, 5 * 10**8),
    )(counts, ranks, cap_v, img_v, *carried[EARLY:], *swapped[EARLY:])
    out, own_row = pl.pallas_call(
        score_kernel,
        out_shape=[shape((n, 1, 2 * B), F32) for n in (128, 1)],
        in_specs=[SMEM] + [VMEM] * 3,
        out_specs=[VMEM] * 2,
        scratch_shapes=[
            pltpu.VMEM((R, C), F32),
            *[pltpu.VMEM((R + RC, 128), F32)] * 5,
            *[pltpu.VMEM((8, C), F32)] * 4,
            pltpu.VMEM((8, C + 384), F32),
        ],
        compiler_params=pltpu.CompilerParams(vmem_limit_bytes=36 * 1024 * 1024),
        cost_estimate=pl.CostEstimate(
            flops=R * C * E, bytes_accessed=2 * (R + C) * E, transcendentals=R * C
        ),
    )(counts, columns, cap_v, img_v)
    parts = lax.all_to_all(out, AXES, 0, 0, tiled=True)
    caption_loss, image_loss, total = pl.pallas_call(
        loss_kernel,
        out_shape=[shape((1, B), F32), shape((1, B), F32), shape((128, 1, 8), F32)],
        in_specs=[VMEM] * 5,
        out_specs=[VMEM] * 3,
        scratch_shapes=[pltpu.VMEM((CAPS, 2 * B), F32), pltpu.VMEM((IMGS, 2 * B), F32)],
        **small(4, 10**8),
    )(parts, own_row, ranks, image_ranks, real)
    totals = lax.all_to_all(total, AXES, 0, 0, tiled=True)
    return caption_loss.reshape(B), image_loss.reshape(B), jnp.sum(totals[:, 0, 0])


def solution(mesh):
    torus = Mesh(mesh.devices.reshape(*SIZES.values()), AXES)
    return jax.shard_map(
        step,
        mesh=torus,
        in_specs=(P(AXES, None), P(AXES, None), P(AXES), P(AXES)),
        out_specs=(P(AXES), P(AXES), P()),
        check_vma=False,
    )
```

profile of v0, /device:TPU:0, one launch (start us, length us, event | category | flops | bytes accessed | tf_op | source)
XLA Modules:
  0.0 103.6 jit_solution(13393746206578719717)
XLA Ops:
  0.6 0.1 collective-permute-start
  0.7 0.5 collective-permute-start.1
  1.2 0.1 collective-permute-start.2
  1.3 1.6 %collective-permute-done.2.valid_other = s32[1,192]{1,0:T(1,128)S(1)} collective-permute-done((s32[1,192]{1,0:T(1,128)}, s32[1,192]{1,0:T(1,128)S(1)}, u32[]{:S(2)}, u32[]{:S(2)}) %collective-permute-start.2) | collective-permute-done | bytes 800 | tf_op jit(solution)/shard_map/ppermute | solution.py:45
  2.9 1.0 copy-done
  3.9 1.0 copy-done.1
  4.9 0.7 copy-done.2
  5.5 0.7 copy-done.3
  6.2 0.5 shard_map.67
  6.7 1.8 %collective-permute-start.3 = (bf16[384,768]{1,0:T(8,128)(2,1)S(1)}, bf16[384,768]{1,0:T(8,128)(2,1)S(1)}, u32[]{:S(2)}, u32[]{:S(2)}) collective-permute-start(bf16[384,768]{1,0:T(8,128)(2,1)S(1)} %get-tuple-element.24.refs_0_), channel_id=1, source_target_pairs={{0,1},{1,0},{2,19},{3,18},{4,5},{5,4},{6,23},{7,22},{8,9},{9,8},{1... | collective-permute-start | bytes 1769480 | tf_op jit(solution)/shard_map/ppermute | solution.py:45
  8.5 4.0 %collective-permute-start.5 = (bf16[384,768]{1,0:T(8,128)(2,1)S(1)}, bf16[384,768]{1,0:T(8,128)(2,1)S(1)}, u32[]{:S(2)}, u32[]{:S(2)}) collective-permute-start(bf16[384,768]{1,0:T(8,128)(2,1)S(1)} %get-tuple-element.24.refs_0_), channel_id=1, source_target_pairs={{0,12},{1,13},{2,98},{3,99},{4,0},{5,1},{6,102},{7,103},{8,4},{9,5... | collective-permute-start | bytes 1769480 | tf_op jit(solution)/shard_map/ppermute | solution.py:45
  12.5 0.0 collective-permute-start.4
  12.5 4.2 %collective-permute-done.3.refs_1_ = bf16[384,768]{1,0:T(8,128)(2,1)S(1)} collective-permute-done((bf16[384,768]{1,0:T(8,128)(2,1)S(1)}, bf16[384,768]{1,0:T(8,128)(2,1)S(1)}, u32[]{:S(2)}, u32[]{:S(2)}) %collective-permute-start.3) | collective-permute-done | bytes 589856 | tf_op jit(solution)/shard_map/ppermute | solution.py:45
  16.7 4.1 %collective-permute-start.7 = (bf16[384,768]{1,0:T(8,128)(2,1)S(1)}, bf16[384,768]{1,0:T(8,128)(2,1)S(1)}, u32[]{:S(2)}, u32[]{:S(2)}) collective-permute-start(bf16[384,768]{1,0:T(8,128)(2,1)S(1)} %collective-permute-done.3.refs_1_), channel_id=1, source_target_pairs={{0,12},{1,13},{2,98},{3,99},{4,0},{5,1},{6,102},{7,103},{8,4},{9,5... | collective-permute-start | bytes 1769480 | tf_op jit(solution)/shard_map/ppermute | solution.py:45
  20.8 0.0 collective-permute-start.10
  20.8 2.8 %collective-permute-done.4.refs_2_ = bf16[384,768]{1,0:T(8,128)(2,1)S(1)} collective-permute-done((bf16[384,768]{1,0:T(8,128)(2,1)S(1)}, bf16[384,768]{1,0:T(8,128)(2,1)S(1)}, u32[]{:S(2)}, u32[]{:S(2)}) %collective-permute-start.4) | collective-permute-done | bytes 589856 | tf_op jit(solution)/shard_map/ppermute | solution.py:45
  23.6 0.2 collective-permute-start.9
  23.8 4.5 %collective-permute-done.7.refs_5_ = bf16[384,768]{1,0:T(8,128)(2,1)S(1)} collective-permute-done((bf16[384,768]{1,0:T(8,128)(2,1)S(1)}, bf16[384,768]{1,0:T(8,128)(2,1)S(1)}, u32[]{:S(2)}, u32[]{:S(2)}) %collective-permute-start.7) | collective-permute-done | bytes 589856 | tf_op jit(solution)/shard_map/ppermute | solution.py:45
  28.2 3.7 %collective-permute-start.14 = (bf16[384,768]{1,0:T(8,128)(2,1)S(1)}, bf16[384,768]{1,0:T(8,128)(2,1)S(1)}, u32[]{:S(2)}, u32[]{:S(2)}) collective-permute-start(bf16[384,768]{1,0:T(8,128)(2,1)S(1)} %collective-permute-done.7.refs_5_), channel_id=1, source_target_pairs={{0,12},{1,13},{2,98},{3,99},{4,0},{5,1},{6,102},{7,103},{8,4},{9,5... | collective-permute-start | bytes 1769480 | tf_op jit(solution)/shard_map/ppermute | solution.py:45
  31.9 2.8 %collective-permute-done.13.refs_0_ = bf16[384,768]{1,0:T(8,128)(2,1)S(1)} collective-permute-done((bf16[384,768]{1,0:T(8,128)(2,1)S(1)}, bf16[384,768]{1,0:T(8,128)(2,1)S(1)}, u32[]{:S(2)}, u32[]{:S(2)}) %collective-permute-start.13) | collective-permute-done | bytes 589856 | tf_op jit(solution)/shard_map/ppermute | solution.py:45
  34.7 6.3 %collective-permute-done.6.refs_4_ = bf16[384,768]{1,0:T(8,128)(2,1)S(1)} collective-permute-done((bf16[384,768]{1,0:T(8,128)(2,1)S(1)}, bf16[384,768]{1,0:T(8,128)(2,1)S(1)}, u32[]{:S(2)}, u32[]{:S(2)}) %collective-permute-start.6) | collective-permute-done | bytes 589856 | tf_op jit(solution)/shard_map/ppermute | solution.py:45
  41.0 0.5 collective-permute-start.15
  41.5 0.1 collective-permute-start.16
  41.6 18.0 %all_to_all.15.table = s32[128,1,192]{2,1,0:T(1,128)S(1)} all-to-all(s32[128,1,192]{2,1,0:T(1,128)S(1)} %get-tuple-element.20), channel_id=1, replica_groups=mesh['x'=4,'h'=2,'z'=4,'c'=2,'l'=2] {'x','h','z','c','l'}, dimensions={0} | all-to-all | bytes 196608 | tf_op jit(solution)/shard_map/all_to_all | solution.py:389
  59.6 1.2 %shard_map.68 = (f32[8,192]{1,0:T(8,128)S(1)}, f32[192,128]{1,0:T(8,128)S(1)}, s32[24,128]{1,0:T(8,128)S(1)}, f32[8,128]{1,0:T(8,128)S(1)}) custom-call(s32[128,1,192]{2,1,0:T(1,128)S(1)} %all_to_all.15.table), custom_call_target="tpu_custom_call" | custom-call | flops 3000000000 | bytes 1000000 | tf_op jit(solution)/shard_map/pallas_call | solution.py:390
  60.9 2.2 %shard_map.69 = (bf16[1792,768]{1,0:T(8,128)(2,1)S(1)}, bf16[3072,768]{1,0:T(8,128)(2,1)S(1)}) custom-call(s32[24,128]{1,0:T(8,128)S(1)} %get-tuple-element.21.counts, f32[8,192]{1,0:T(8,128)S(1)} %get-tuple-element.23.ranks.row_ranks, bf16[384,768]{1,0:T(8,128)(2,1)S(1)} %get-tuple-element.24.refs_0_, bf16[384,768]{1,0:T(8,128)(2,1)S(1)} %collective-permute-done.3.refs_1_, ...), custom_call_target="tpu_custom_call" | custom-call | flops 2000000000 | bytes 1000000 | tf_op jit(solution)/shard_map/pallas_call | solution.py:402
  63.1 1.2 %shard_map.70 = (bf16[1792,768]{1,0:T(8,128)(2,1)S(1)}, bf16[3072,768]{1,0:T(8,128)(2,1)S(1)}) custom-call(s32[24,128]{1,0:T(8,128)S(1)} %get-tuple-element.21.counts, f32[8,192]{1,0:T(8,128)S(1)} %get-tuple-element.23.ranks.row_ranks, bf16[1792,768]{1,0:T(8,128)(2,1)S(1)} %get-tuple-element.26.cap_in, ...), custom_call_target="tpu_custom_call", output_to_operand_aliasing={{0}: (2, {}), {1}: (3, {})} | custom-call | flops 500000000 | bytes 1000000 | tf_op jit(solution)/shard_map/pallas_call | solution.py:409
  64.3 9.1 %shard_map.71 = (f32[128,1,384]{2,1,0:T(1,128)S(1)}, f32[1,1,384]{2,1,0:T(1,128)S(1)}) custom-call(s32[24,128]{1,0:T(8,128)S(1)} %get-tuple-element.21.counts, f32[192,128]{1,0:T(8,128)S(1)} %get-tuple-element.22.columns, bf16[1792,768]{1,0:T(8,128)(2,1)S(1)} %get-tuple-element.28.cap_v, bf16[3072,768]{1,0:T(8,128)(2,1)S(1)} %get-tuple-element.29.img_v), custom_call_target="tpu_custom_call" | custom-call | flops 4227858432 | bytes 7471104 | tf_op jit(solution)/shard_map/pallas_call | solution.py:417
  73.4 14.7 %all_to_all.16.parts = f32[128,1,384]{2,1,0:T(1,128)S(1)} all-to-all(f32[128,1,384]{2,1,0:T(1,128)S(1)} %get-tuple-element.30), channel_id=1, replica_groups=mesh['x'=4,'h'=2,'z'=4,'c'=2,'l'=2] {'x','h','z','c','l'}, dimensions={0} | all-to-all | bytes 393216 | tf_op jit(solution)/shard_map/all_to_all | solution.py:433
  88.1 0.9 shard_map.72
  89.0 13.9 %all_to_all.17 = f32[128,1,8]{2,1,0:T(1,128)S(1)} all-to-all(f32[128,1,8]{2,1,0:T(1,128)S(1)} %get-tuple-element.36), channel_id=1, replica_groups=mesh['x'=4,'h'=2,'z'=4,'c'=2,'l'=2] {'x','h','z','c','l'}, dimensions={0} | all-to-all | bytes 8192 | tf_op jit(solution)/shard_map/all_to_all | solution.py:442
  102.9 0.7 slice_reduce_fusion
  (20 shorter events, 0.0 us)
Async XLA Ops:
  0.6 2.3 %collective-permute-start = (bf16[192,768]{1,0:T(8,128)(2,1)}, bf16[192,768]{1,0:T(8,128)(2,1)S(1)}, u32[]{:S(2)}, u32[]{:S(2)}) collective-permute-start(bf16[192,768]{1,0:T(8,128)(2,1)} %cap.1), channel_id=1, source_target_pairs={{0,2},{1,3},{2,0},{3,1},{4,6},{5,7},{6,4},{7,5},{8,10},{9,11},{10,... | collective-permute-start | bytes 884744 | tf_op jit(solution)/shard_map/ppermute | solution.py:45
  0.7 2.2 %collective-permute-start.1 = (bf16[192,768]{1,0:T(8,128)(2,1)}, bf16[192,768]{1,0:T(8,128)(2,1)S(1)}, u32[]{:S(2)}, u32[]{:S(2)}) collective-permute-start(bf16[192,768]{1,0:T(8,128)(2,1)} %img.1), channel_id=1, source_target_pairs={{0,2},{1,3},{2,0},{3,1},{4,6},{5,7},{6,4},{7,5},{8,10},{9,11},{10,... | collective-permute-start | bytes 884744 | tf_op jit(solution)/shard_map/ppermute | solution.py:45
  1.2 1.7 %collective-permute-start.2 = (s32[1,192]{1,0:T(1,128)}, s32[1,192]{1,0:T(1,128)S(1)}, u32[]{:S(2)}, u32[]{:S(2)}) collective-permute-start(s32[1,192]{1,0:T(1,128)} %bitcast.5), channel_id=1, source_target_pairs={{0,2},{1,3},{2,0},{3,1},{4,6},{5,7},{6,4},{7,5},{8,10},{9,11},{10,... | collective-permute-start | bytes 2312 | tf_op jit(solution)/shard_map/ppermute | solution.py:45
  2.9 1.0 copy-start
  3.9 1.0 copy-start.1
  4.9 0.7 copy-start.2
  5.5 0.7 copy-start.3
  6.7 10.0 %collective-permute-start.3 = (bf16[384,768]{1,0:T(8,128)(2,1)S(1)}, bf16[384,768]{1,0:T(8,128)(2,1)S(1)}, u32[]{:S(2)}, u32[]{:S(2)}) collective-permute-start(bf16[384,768]{1,0:T(8,128)(2,1)S(1)} %get-tuple-element.24.refs_0_), channel_id=1, source_target_pairs={{0,1},{1,0},{2,19},{3,18},{4,5},{5,4},{6,23},{7,22},{8,9},{9,8},{1... | collective-permute-start | bytes 1769480 | tf_op jit(solution)/shard_map/ppermute | solution.py:45
  8.5 12.3 %collective-permute-start.5 = (bf16[384,768]{1,0:T(8,128)(2,1)S(1)}, bf16[384,768]{1,0:T(8,128)(2,1)S(1)}, u32[]{:S(2)}, u32[]{:S(2)}) collective-permute-start(bf16[384,768]{1,0:T(8,128)(2,1)S(1)} %get-tuple-element.24.refs_0_), channel_id=1, source_target_pairs={{0,12},{1,13},{2,98},{3,99},{4,0},{5,1},{6,102},{7,103},{8,4},{9,5... | collective-permute-start | bytes 1769480 | tf_op jit(solution)/shard_map/ppermute | solution.py:45
  12.5 11.1 %collective-permute-start.4 = (bf16[384,768]{1,0:T(8,128)(2,1)S(1)}, bf16[384,768]{1,0:T(8,128)(2,1)S(1)}, u32[]{:S(2)}, u32[]{:S(2)}) collective-permute-start(bf16[384,768]{1,0:T(8,128)(2,1)S(1)} %get-tuple-element.24.refs_0_), channel_id=1, source_target_pairs={{0,4},{1,5},{2,34},{3,35},{4,8},{5,9},{6,38},{7,39},{8,12},{9,13},... | collective-permute-start | bytes 1769480 | tf_op jit(solution)/shard_map/ppermute | solution.py:45
  16.7 11.5 %collective-permute-start.7 = (bf16[384,768]{1,0:T(8,128)(2,1)S(1)}, bf16[384,768]{1,0:T(8,128)(2,1)S(1)}, u32[]{:S(2)}, u32[]{:S(2)}) collective-permute-start(bf16[384,768]{1,0:T(8,128)(2,1)S(1)} %collective-permute-done.3.refs_1_), channel_id=1, source_target_pairs={{0,12},{1,13},{2,98},{3,99},{4,0},{5,1},{6,102},{7,103},{8,4},{9,5... | collective-permute-start | bytes 1769480 | tf_op jit(solution)/shard_map/ppermute | solution.py:45
  20.8 11.1 %collective-permute-start.10 = (bf16[384,768]{1,0:T(8,128)(2,1)S(1)}, bf16[384,768]{1,0:T(8,128)(2,1)S(1)}, u32[]{:S(2)}, u32[]{:S(2)}) collective-permute-start(bf16[384,768]{1,0:T(8,128)(2,1)S(1)} %collective-permute-done.5.refs_3_), channel_id=1, source_target_pairs={{0,2},{1,3},{2,0},{3,1},{4,6},{5,7},{6,4},{7,5},{8,10},{9,11},{10,... | collective-permute-start | bytes 1769480 | tf_op jit(solution)/shard_map/ppermute | solution.py:45
  23.6 11.1 %collective-permute-start.13 = (bf16[384,768]{1,0:T(8,128)(2,1)S(1)}, bf16[384,768]{1,0:T(8,128)(2,1)S(1)}, u32[]{:S(2)}, u32[]{:S(2)}) collective-permute-start(bf16[384,768]{1,0:T(8,128)(2,1)S(1)} %collective-permute-done.4.refs_2_), channel_id=1, source_target_pairs={{0,4},{1,5},{2,34},{3,35},{4,8},{5,9},{6,38},{7,39},{8,12},{9,13},... | collective-permute-start | bytes 1769480 | tf_op jit(solution)/shard_map/ppermute | solution.py:45
  23.6 17.4 %collective-permute-start.6 = (bf16[384,768]{1,0:T(8,128)(2,1)S(1)}, bf16[384,768]{1,0:T(8,128)(2,1)S(1)}, u32[]{:S(2)}, u32[]{:S(2)}) collective-permute-start(bf16[384,768]{1,0:T(8,128)(2,1)S(1)} %collective-permute-done.3.refs_1_), channel_id=1, source_target_pairs={{0,4},{1,5},{2,34},{3,35},{4,8},{5,9},{6,38},{7,39},{8,12},{9,13},... | collective-permute-start | bytes 1769480 | tf_op jit(solution)/shard_map/ppermute | solution.py:45
  23.6 17.4 %collective-permute-start.9 = (bf16[384,768]{1,0:T(8,128)(2,1)S(1)}, bf16[384,768]{1,0:T(8,128)(2,1)S(1)}, u32[]{:S(2)}, u32[]{:S(2)}) collective-permute-start(bf16[384,768]{1,0:T(8,128)(2,1)S(1)} %collective-permute-done.4.refs_2_), channel_id=1, source_target_pairs={{0,2},{1,3},{2,0},{3,1},{4,6},{5,7},{6,4},{7,5},{8,10},{9,11},{10,... | collective-permute-start | bytes 1769480 | tf_op jit(solution)/shard_map/ppermute | solution.py:45
  28.2 13.3 %collective-permute-start.14 = (bf16[384,768]{1,0:T(8,128)(2,1)S(1)}, bf16[384,768]{1,0:T(8,128)(2,1)S(1)}, u32[]{:S(2)}, u32[]{:S(2)}) collective-permute-start(bf16[384,768]{1,0:T(8,128)(2,1)S(1)} %collective-permute-done.7.refs_5_), channel_id=1, source_target_pairs={{0,12},{1,13},{2,98},{3,99},{4,0},{5,1},{6,102},{7,103},{8,4},{9,5... | collective-permute-start | bytes 1769480 | tf_op jit(solution)/shard_map/ppermute | solution.py:45
  31.9 29.0 %collective-permute-start.8 = (bf16[384,768]{1,0:T(8,128)(2,1)S(1)}, bf16[384,768]{1,0:T(8,128)(2,1)S(1)}, u32[]{:S(2)}, u32[]{:S(2)}) collective-permute-start(bf16[384,768]{1,0:T(8,128)(2,1)S(1)} %collective-permute-done.3.refs_1_), channel_id=1, source_target_pairs={{0,2},{1,3},{2,0},{3,1},{4,6},{5,7},{6,4},{7,5},{8,10},{9,11},{10,... | collective-permute-start | bytes 1769480 | tf_op jit(solution)/shard_map/ppermute | solution.py:45
  34.7 26.2 %collective-permute-start.12 = (bf16[384,768]{1,0:T(8,128)(2,1)S(1)}, bf16[384,768]{1,0:T(8,128)(2,1)S(1)}, u32[]{:S(2)}, u32[]{:S(2)}) collective-permute-start(bf16[384,768]{1,0:T(8,128)(2,1)S(1)} %collective-permute-done.7.refs_5_), channel_id=1, source_target_pairs={{0,2},{1,3},{2,0},{3,1},{4,6},{5,7},{6,4},{7,5},{8,10},{9,11},{10,... | collective-permute-start | bytes 1769480 | tf_op jit(solution)/shard_map/ppermute | solution.py:45
  41.0 19.9 %collective-permute-start.11 = (bf16[384,768]{1,0:T(8,128)(2,1)S(1)}, bf16[384,768]{1,0:T(8,128)(2,1)S(1)}, u32[]{:S(2)}, u32[]{:S(2)}) collective-permute-start(bf16[384,768]{1,0:T(8,128)(2,1)S(1)} %collective-permute-done.6.refs_4_), channel_id=1, source_target_pairs={{0,2},{1,3},{2,0},{3,1},{4,6},{5,7},{6,4},{7,5},{8,10},{9,11},{10,... | collective-permute-start | bytes 1769480 | tf_op jit(solution)/shard_map/ppermute | solution.py:45
  41.0 22.1 %collective-permute-start.15 = (bf16[384,768]{1,0:T(8,128)(2,1)S(1)}, bf16[384,768]{1,0:T(8,128)(2,1)S(1)}, u32[]{:S(2)}, u32[]{:S(2)}) collective-permute-start(bf16[384,768]{1,0:T(8,128)(2,1)S(1)} %collective-permute-done.13.refs_0_), channel_id=1, source_target_pairs={{0,2},{1,3},{2,0},{3,1},{4,6},{5,7},{6,4},{7,5},{8,10},{9,11},{10,... | collective-permute-start | bytes 1769480 | tf_op jit(solution)/shard_map/ppermute | solution.py:45
  41.5 21.6 %collective-permute-start.16 = (bf16[384,768]{1,0:T(8,128)(2,1)S(1)}, bf16[384,768]{1,0:T(8,128)(2,1)S(1)}, u32[]{:S(2)}, u32[]{:S(2)}) collective-permute-start(bf16[384,768]{1,0:T(8,128)(2,1)S(1)} %collective-permute-done.14.refs_1_), channel_id=1, source_target_pairs={{0,2},{1,3},{2,0},{3,1},{4,6},{5,7},{6,4},{7,5},{8,10},{9,11},{10,... | collective-permute-start | bytes 1769480 | tf_op jit(solution)/shard_map/ppermute | solution.py:45
where the time goes:
time: 105 us; the launch traced here: 104 us
  blocking collectives  46.6 us (44%)
  waiting for transfers between devices  22.1 us (21%)
  starting transfers between devices  15.1 us (14%)
  Pallas kernels  15.1 us (14%)
  local copies, waits for them, and re-layouts  3.28 us (3%)
    ppermute x17, waiting for transfers between devices, send(): return lax.ppermute(value, AXES, pairs)  22.1 us
    all_to_all x1, blocking collectives, step(): table = lax.all_to_all(words, AXES, 0, 0, tiled=True)  18 us
    ppermute x17, starting transfers between devices, send(): return lax.ppermute(value, AXES, pairs)  15.1 us
    all_to_all x1, blocking collectives, step(): parts = lax.all_to_all(out, AXES, 0, 0, tiled=True)  14.7 us
    all_to_all x1, blocking collectives, step(): totals = lax.all_to_all(total, AXES, 0, 0, tiled=True)  13.9 us
    pallas_call x1, Pallas kernels, step(): pl.pallas_call(score_kernel, out_shape=[shape((n, 1, 2 * B), F32) for n i...  9.11 us
    unnamed x8, local copies, waits for them, and re-layouts  3.28 us
    pallas_call x1, Pallas kernels, step(): pl.pallas_call(early_kernel, out_shape=packed_shapes, in_specs=[SMEM] + [...  2.17 us
  transfers between devices with their start and end apart: 17, of which 6 were waited for; matrix products, arithmetic and copies ran while one was open for 0% of the time, Pallas kernels for 3%

commit v1 on v0

--- a/solution.py
+++ b/solution.py
@@ -1,3 +1,4 @@
+import functools
 import itertools
 
 import jax
@@ -18,14 +19,17 @@
 B = 192
 E = 768
 MET = ((0, 0), (0, 1), (3, 0), (1, 0), (3, 1), (1, 1), (2, 0), (2, 1))
-EARLY = 6
+PARTS = ((0, 4), (4, 6), (6, 8))
 CAPS = len(MET)
 IMGS = 2 * len(MET)
 C = IMGS * B
 RC = 448
 R = -(-CAPS * B // RC) * RC
+CAP_ROWS = CAPS * B + RC
 NC = 256
 COUNTS = (2, 4, 5, 6, 7, 8, 10, 12)
+TAIL = 2 * NC
+IMG_ROWS = C + TAIL
 PIECE = 64
 GRAIN = 16
 OK_BIT = 15
@@ -106,17 +110,16 @@
 
 
 def pair_kernel(
-    cap, img, positives, valid, cap_other, img_other, valid_other,
-    carried, kept, words, ranks,
+    cap, img, word, cap_other, img_other, word_other, carried, kept, words, ranks
 ):
     first = lax.axis_index("c") == 0
-    ok = jnp.concatenate([valid[...], valid_other[...]], axis=0)
+    ok = lax.shift_right_logical(
+        jnp.concatenate([word[...], word_other[...]], axis=0), OK_BIT
+    )
     order = dot(jnp.broadcast_to(ok[:, None], (2, 8, B)).reshape(16, B).astype(F32).astype(BF16), earlier())
     found = jnp.where(ok > 0, jnp.concatenate([order[0:1], order[8:9]], axis=0), ABSENT)
     ranks[...] = found[0:1, :]
-    words[...] = jnp.broadcast_to(
-        positives[...] + valid[...] * (1 << OK_BIT), (128, B)
-    ).reshape(128, 1, B)
+    words[...] = jnp.broadcast_to(word[...], (128, B)).reshape(128, 1, B)
     packed = []
     for i, block in enumerate((img, img_other)):
         pick = jnp.where(iota((B, B), 0) == found[i:i + 1, :], 1.0, 0.0).astype(BF16)
@@ -201,18 +204,17 @@
             img_out[pl.ds(at[2 * k + side], B), :] = jnp.where(core == 0, b[rows, :], a[rows, :])
 
 
-def early_kernel(counts, ranks, *refs):
-    cap_out, img_out = refs[2 * EARLY:]
-    cap_out[...] = jnp.zeros(cap_out.shape, BF16)
-    img_out[...] = jnp.zeros(img_out.shape, BF16)
-    compact(counts, ranks, refs[:EARLY], refs[EARLY:2 * EARLY], cap_out, img_out, 0)
-
-
-def late_kernel(counts, ranks, cap_in, img_in, *refs):
-    del cap_in, img_in
-    late = CAPS - EARLY
-    cap_out, img_out = refs[2 * late:]
-    compact(counts, ranks, refs[:late], refs[late:2 * late], cap_out, img_out, EARLY)
+def compact_kernel(part, counts, ranks, *refs):
+    first, last = PARTS[part]
+    refs = refs[2 if part else 0:]
+    number = last - first
+    cap_out, img_out = refs[2 * number:]
+    compact(counts, ranks, refs[:number], refs[number:2 * number], cap_out, img_out, first)
+    if last == CAPS:
+        cap_end = starts_of(counts, 0, CAPS)[-1]
+        img_end = starts_of(counts, CAPS, IMGS)[-1]
+        cap_out[pl.ds(cap_end, RC), :] = jnp.zeros((RC, E), BF16)
+        img_out[pl.ds(img_end, TAIL), :] = jnp.zeros((TAIL, E), BF16)
 
 
 def score_kernel(
@@ -371,14 +373,15 @@
 def step(captions, images, positives, valid):
     shape = jax.ShapeDtypeStruct
     pair = shape((2 * B, E), BF16)
-    others = [send(value, other_core) for value in (captions, images, valid[None])]
+    word = (positives + valid * (1 << OK_BIT))[None]
+    others = [send(value, other_core) for value in (captions, images, word)]
     carried, kept, words, image_ranks = pl.pallas_call(
         pair_kernel,
         out_shape=[pair, pair, shape((128, 1, B), jnp.int32), shape((1, B), F32)],
-        in_specs=[VMEM] * 7,
+        in_specs=[VMEM] * 6,
         out_specs=[VMEM] * 4,
         **small(8, 10**8),
-    )(captions, images, positives[None], valid[None], *others)
+    )(captions, images, word, *others)
     near = send(carried, partner)
     a1, a3 = (send(carried, along(s)) for s in (1, 3))
     b1, b3 = (send(near, along(s)) for s in (1, 3))
@@ -398,22 +401,17 @@
         scratch_shapes=[pltpu.VMEM((CAPS, B), F32), pltpu.VMEM((128, B), jnp.int32)],
         **small(4, 3 * 10**9),
     )(table)
-    packed_shapes = [shape((R, E), BF16), shape((C, E), BF16)]
-    cap_v, img_v = pl.pallas_call(
-        early_kernel,
-        out_shape=packed_shapes,
-        in_specs=[SMEM] + [VMEM] * (1 + 2 * EARLY),
-        out_specs=[VMEM] * 2,
-        **small(12, 2 * 10**9),
-    )(counts, ranks, *carried[:EARLY], *swapped[:EARLY])
-    cap_v, img_v = pl.pallas_call(
-        late_kernel,
-        out_shape=packed_shapes,
-        in_specs=[SMEM] + [VMEM] * (3 + 2 * (CAPS - EARLY)),
-        out_specs=[VMEM] * 2,
-        input_output_aliases={2: 0, 3: 1},
-        **small(12, 5 * 10**8),
-    )(counts, ranks, cap_v, img_v, *carried[EARLY:], *swapped[EARLY:])
+    buffers = []
+    for part, (first, last) in enumerate(PARTS):
+        buffers = pl.pallas_call(
+            functools.partial(compact_kernel, part),
+            out_shape=[shape((CAP_ROWS, E), BF16), shape((IMG_ROWS, E), BF16)],
+            in_specs=[SMEM] + [VMEM] * (1 + len(buffers) + 2 * (last - first)),
+            out_specs=[VMEM] * 2,
+            input_output_aliases={2: 0, 3: 1} if part else {},
+            **small(10, 10**9),
+        )(counts, ranks, *buffers, *carried[first:last], *swapped[first:last])
+    cap_v, img_v = buffers
     out, own_row = pl.pallas_call(
         score_kernel,
         out_shape=[shape((n, 1, 2 * B), F32) for n in (128, 1)],
@@ -425,7 +423,7 @@
             *[pltpu.VMEM((8, C), F32)] * 4,
             pltpu.VMEM((8, C + 384), F32),
         ],
-        compiler_params=pltpu.CompilerParams(vmem_limit_bytes=36 * 1024 * 1024),
+        compiler_params=pltpu.CompilerParams(vmem_limit_bytes=31 * 1024 * 1024),
         cost_estimate=pl.CostEstimate(
             flops=R * C * E, bytes_accessed=2 * (R + C) * E, transcendentals=R * C
         ),

time: 105 us -> 104 us (level)
  waiting for transfers between devices: 22.1 us -> 16.7 us
  starting transfers between devices: 15.1 us -> 17.7 us
  blocking collectives: 46.6 us -> 48.9 us
  local copies, waits for them, and re-layouts: 3.28 us -> 1.92 us
    ppermute x17, waiting for transfers between devices: 22.1 us -> 16.7 us  [send(): return lax.ppermute(value, AXES, pairs)]
    ppermute x17, starting transfers between devices: 15.1 us -> 17.7 us  [send(): return lax.ppermute(value, AXES, pairs)]
    all_to_all x1, blocking collectives: 18 us -> 20.3 us  [step(): table = lax.all_to_all(words, AXES, 0, 0, tiled=True)]
    unnamed x8 -> x4, local copies, waits for them, and re-layouts: 3.28 us -> 1.92 us
    pallas_call x2 -> x3, Pallas kernels: 3.32 us -> 3.85 us  [step(): pl.pallas_call(functools.partial(compact_kernel, part), out_shape=[shape(...]
  transfers between devices with their start and end apart: 17 -> 17, of which waited for: 6 -> 5; matrix products, arithmetic and copies ran while one was open for 0% -> 1% of each run, Pallas kernels for 3% -> 4%
where the time goes in v1:
time: 104 us; the launch traced here: 103 us
  blocking collectives  48.9 us (47%)
  starting transfers between devices  17.7 us (17%)
  waiting for transfers between devices  16.7 us (16%)
  Pallas kernels  15.6 us (15%)
  local copies, waits for them, and re-layouts  1.92 us (2%)
  other arithmetic  1.43 us (1%)
    all_to_all x1, blocking collectives, step(): table = lax.all_to_all(words, AXES, 0, 0, tiled=True)  20.3 us
    ppermute x17, starting transfers between devices, send(): return lax.ppermute(value, AXES, pairs)  17.7 us
    ppermute x17, waiting for transfers between devices, send(): return lax.ppermute(value, AXES, pairs)  16.7 us
    all_to_all x1, blocking collectives, step(): parts = lax.all_to_all(out, AXES, 0, 0, tiled=True)  14.7 us
    all_to_all x1, blocking collectives, step(): totals = lax.all_to_all(total, AXES, 0, 0, tiled=True)  13.9 us
    pallas_call x1, Pallas kernels, step(): pl.pallas_call(score_kernel, out_shape=[shape((n, 1, 2 * B), F32) for n i...  9.11 us
    pallas_call x3, Pallas kernels, step(): pl.pallas_call(functools.partial(compact_kernel, part), out_shape=[shape(...  3.85 us
  transfers between devices with their start and end apart: 17, of which 5 were waited for; matrix products, arithmetic and copies ran while one was open for 1% of the time, Pallas kernels for 4%

profile of v1, /device:TPU:0, one launch (start us, length us, event | category | flops | bytes accessed | tf_op | source)
XLA Modules:
  0.0 102.9 jit_solution(15806523600305388873)
XLA Ops:
  0.6 0.1 collective-permute-start
  0.7 0.5 collective-permute-start.1
  1.2 0.7 multiply_add_fusion
  1.9 0.1 collective-permute-start.2
  2.0 1.1 %collective-permute-done.2.word_other = s32[1,192]{1,0:T(1,128)S(1)} collective-permute-done((s32[1,192]{1,0:T(1,128)S(1)}, s32[1,192]{1,0:T(1,128)S(1)}, u32[]{:S(2)}, u32[]{:S(2)}) %collective-permute-start.2) | collective-permute-done | bytes 800 | tf_op jit(solution)/shard_map/ppermute | solution.py:49
  3.1 1.0 copy-done
  4.1 1.0 copy-done.1
  5.0 0.5 shard_map.67
  5.5 1.8 %collective-permute-start.3 = (bf16[384,768]{1,0:T(8,128)(2,1)S(1)}, bf16[384,768]{1,0:T(8,128)(2,1)S(1)}, u32[]{:S(2)}, u32[]{:S(2)}) collective-permute-start(bf16[384,768]{1,0:T(8,128)(2,1)S(1)} %get-tuple-element.26.refs_0_), channel_id=1, source_target_pairs={{0,1},{1,0},{2,19},{3,18},{4,5},{5,4},{6,23},{7,22},{8,9},{9,8},{1... | collective-permute-start | bytes 1769480 | tf_op jit(solution)/shard_map/ppermute | solution.py:49
  7.3 1.9 %collective-permute-start.4 = (bf16[384,768]{1,0:T(8,128)(2,1)S(1)}, bf16[384,768]{1,0:T(8,128)(2,1)S(1)}, u32[]{:S(2)}, u32[]{:S(2)}) collective-permute-start(bf16[384,768]{1,0:T(8,128)(2,1)S(1)} %get-tuple-element.26.refs_0_), channel_id=1, source_target_pairs={{0,4},{1,5},{2,34},{3,35},{4,8},{5,9},{6,38},{7,39},{8,12},{9,13},... | collective-permute-start | bytes 1769480 | tf_op jit(solution)/shard_map/ppermute | solution.py:49
  9.2 2.1 %collective-permute-start.5 = (bf16[384,768]{1,0:T(8,128)(2,1)S(1)}, bf16[384,768]{1,0:T(8,128)(2,1)S(1)}, u32[]{:S(2)}, u32[]{:S(2)}) collective-permute-start(bf16[384,768]{1,0:T(8,128)(2,1)S(1)} %get-tuple-element.26.refs_0_), channel_id=1, source_target_pairs={{0,12},{1,13},{2,98},{3,99},{4,0},{5,1},{6,102},{7,103},{8,4},{9,5... | collective-permute-start | bytes 1769480 | tf_op jit(solution)/shard_map/ppermute | solution.py:49
  11.3 4.2 %collective-permute-done.3.refs_1_ = bf16[384,768]{1,0:T(8,128)(2,1)S(1)} collective-permute-done((bf16[384,768]{1,0:T(8,128)(2,1)S(1)}, bf16[384,768]{1,0:T(8,128)(2,1)S(1)}, u32[]{:S(2)}, u32[]{:S(2)}) %collective-permute-start.3) | collective-permute-done | bytes 589856 | tf_op jit(solution)/shard_map/ppermute | solution.py:49
  15.5 4.1 %collective-permute-start.10 = (bf16[384,768]{1,0:T(8,128)(2,1)S(1)}, bf16[384,768]{1,0:T(8,128)(2,1)S(1)}, u32[]{:S(2)}, u32[]{:S(2)}) collective-permute-start(bf16[384,768]{1,0:T(8,128)(2,1)S(1)} %collective-permute-done.3.refs_1_), channel_id=1, source_target_pairs={{0,12},{1,13},{2,98},{3,99},{4,0},{5,1},{6,102},{7,103},{8,4},{9,5... | collective-permute-start | bytes 1769480 | tf_op jit(solution)/shard_map/ppermute | solution.py:49
  19.6 0.5 collective-permute-start.7
  20.1 0.3 collective-permute-start.9
  20.5 1.9 %collective-permute-start.13 = (bf16[384,768]{1,0:T(8,128)(2,1)S(1)}, bf16[384,768]{1,0:T(8,128)(2,1)S(1)}, u32[]{:S(2)}, u32[]{:S(2)}) collective-permute-start(bf16[384,768]{1,0:T(8,128)(2,1)S(1)} %collective-permute-done.4.refs_2_), channel_id=1, source_target_pairs={{0,4},{1,5},{2,34},{3,35},{4,8},{5,9},{6,38},{7,39},{8,12},{9,13},... | collective-permute-start | bytes 1769480 | tf_op jit(solution)/shard_map/ppermute | solution.py:49
  22.4 4.6 %collective-permute-done.10.refs_3_ = bf16[384,768]{1,0:T(8,128)(2,1)S(1)} collective-permute-done((bf16[384,768]{1,0:T(8,128)(2,1)S(1)}, bf16[384,768]{1,0:T(8,128)(2,1)S(1)}, u32[]{:S(2)}, u32[]{:S(2)}) %collective-permute-start.10) | collective-permute-done | bytes 589856 | tf_op jit(solution)/shard_map/ppermute | solution.py:49
  27.0 3.7 %collective-permute-start.14 = (bf16[384,768]{1,0:T(8,128)(2,1)S(1)}, bf16[384,768]{1,0:T(8,128)(2,1)S(1)}, u32[]{:S(2)}, u32[]{:S(2)}) collective-permute-start(bf16[384,768]{1,0:T(8,128)(2,1)S(1)} %collective-permute-done.10.refs_3_), channel_id=1, source_target_pairs={{0,12},{1,13},{2,98},{3,99},{4,0},{5,1},{6,102},{7,103},{8,4},{9,5... | collective-permute-start | bytes 1769480 | tf_op jit(solution)/shard_map/ppermute | solution.py:49
  30.7 0.5 collective-permute-start.12
  31.2 0.1 collective-permute-start.11
  31.3 6.2 %collective-permute-done.13.refs_2_ = bf16[384,768]{1,0:T(8,128)(2,1)S(1)} collective-permute-done((bf16[384,768]{1,0:T(8,128)(2,1)S(1)}, bf16[384,768]{1,0:T(8,128)(2,1)S(1)}, u32[]{:S(2)}, u32[]{:S(2)}) %collective-permute-start.13) | collective-permute-done | bytes 589856 | tf_op jit(solution)/shard_map/ppermute | solution.py:49
  37.5 0.6 collective-permute-done.14.refs_3_
  38.1 20.3 %all_to_all.15.table = s32[128,1,192]{2,1,0:T(1,128)S(1)} all-to-all(s32[128,1,192]{2,1,0:T(1,128)S(1)} %get-tuple-element.22), channel_id=1, replica_groups=mesh['x'=4,'h'=2,'z'=4,'c'=2,'l'=2] {'x','h','z','c','l'}, dimensions={0} | all-to-all | bytes 196608 | tf_op jit(solution)/shard_map/all_to_all | solution.py:392
  58.4 1.2 %shard_map.68 = (f32[8,192]{1,0:T(8,128)S(1)}, f32[192,128]{1,0:T(8,128)S(1)}, s32[24,128]{1,0:T(8,128)S(1)}, f32[8,128]{1,0:T(8,128)S(1)}) custom-call(s32[128,1,192]{2,1,0:T(1,128)S(1)} %all_to_all.15.table), custom_call_target="tpu_custom_call" | custom-call | flops 3000000000 | bytes 1000000 | tf_op jit(solution)/shard_map/pallas_call | solution.py:393
  59.7 1.4 %shard_map.69 = (bf16[1984,768]{1,0:T(8,128)(2,1)S(1)}, bf16[3584,768]{1,0:T(8,128)(2,1)S(1)}) custom-call(s32[24,128]{1,0:T(8,128)S(1)} %get-tuple-element.23.counts, f32[8,192]{1,0:T(8,128)S(1)} %get-tuple-element.25.ranks.row_ranks, bf16[384,768]{1,0:T(8,128)(2,1)S(1)} %get-tuple-element.26.refs_0_, bf16[384,768]{1,0:T(8,128)(2,1)S(1)} %collective-permute-done.3.refs_1_, ...), custom_call_target="tpu_custom_call" | custom-call | flops 1000000000 | bytes 1000000 | tf_op jit(solution)/shard_map/pallas_call | solution.py:406
  61.1 1.2 %shard_map.70 = (bf16[1984,768]{1,0:T(8,128)(2,1)S(1)}, bf16[3584,768]{1,0:T(8,128)(2,1)S(1)}) custom-call(s32[24,128]{1,0:T(8,128)S(1)} %get-tuple-element.23.counts, f32[8,192]{1,0:T(8,128)S(1)} %get-tuple-element.25.ranks.row_ranks, bf16[1984,768]{1,0:T(8,128)(2,1)S(1)} %get-tuple-element.28.refs_0_, ...), custom_call_target="tpu_custom_call", output_to_operand_aliasing={{0}: (2, {}), {1}: (3, {})} | custom-call | flops 1000000000 | bytes 1000000 | tf_op jit(solution)/shard_map/pallas_call | solution.py:406
  62.3 1.3 %shard_map.71 = (bf16[1984,768]{1,0:T(8,128)(2,1)S(1)}, bf16[3584,768]{1,0:T(8,128)(2,1)S(1)}) custom-call(s32[24,128]{1,0:T(8,128)S(1)} %get-tuple-element.23.counts, f32[8,192]{1,0:T(8,128)S(1)} %get-tuple-element.25.ranks.row_ranks, bf16[1984,768]{1,0:T(8,128)(2,1)S(1)} %get-tuple-element.30.refs_0_, ...), custom_call_target="tpu_custom_call", output_to_operand_aliasing={{0}: (2, {}), {1}: (3, {})} | custom-call | flops 1000000000 | bytes 1000000 | tf_op jit(solution)/shard_map/pallas_call | solution.py:406
  63.6 9.1 %shard_map.72 = (f32[128,1,384]{2,1,0:T(1,128)S(1)}, f32[1,1,384]{2,1,0:T(1,128)S(1)}) custom-call(s32[24,128]{1,0:T(8,128)S(1)} %get-tuple-element.23.counts, f32[192,128]{1,0:T(8,128)S(1)} %get-tuple-element.24.columns, bf16[1984,768]{1,0:T(8,128)(2,1)S(1)} %get-tuple-element.32.cap_v, bf16[3584,768]{1,0:T(8,128)(2,1)S(1)} %get-tuple-element.33.img_v), custom_call_target="tpu_custom_call" | custom-call | flops 4227858432 | bytes 7471104 | tf_op jit(solution)/shard_map/pallas_call | solution.py:415
  72.7 14.7 %all_to_all.16.parts = f32[128,1,384]{2,1,0:T(1,128)S(1)} all-to-all(f32[128,1,384]{2,1,0:T(1,128)S(1)} %get-tuple-element.34), channel_id=1, replica_groups=mesh['x'=4,'h'=2,'z'=4,'c'=2,'l'=2] {'x','h','z','c','l'}, dimensions={0} | all-to-all | bytes 393216 | tf_op jit(solution)/shard_map/all_to_all | solution.py:431
  87.4 0.9 shard_map.73
  88.3 13.9 %all_to_all.17 = f32[128,1,8]{2,1,0:T(1,128)S(1)} all-to-all(f32[128,1,8]{2,1,0:T(1,128)S(1)} %get-tuple-element.40), channel_id=1, replica_groups=mesh['x'=4,'h'=2,'z'=4,'c'=2,'l'=2] {'x','h','z','c','l'}, dimensions={0} | all-to-all | bytes 8192 | tf_op jit(solution)/shard_map/all_to_all | solution.py:440
  102.2 0.7 slice_reduce_fusion
  (18 shorter events, 0.0 us)
Async XLA Ops:
  0.6 2.5 %collective-permute-start = (bf16[192,768]{1,0:T(8,128)(2,1)}, bf16[192,768]{1,0:T(8,128)(2,1)S(1)}, u32[]{:S(2)}, u32[]{:S(2)}) collective-permute-start(bf16[192,768]{1,0:T(8,128)(2,1)} %cap.1), channel_id=1, source_target_pairs={{0,2},{1,3},{2,0},{3,1},{4,6},{5,7},{6,4},{7,5},{8,10},{9,11},{10,... | collective-permute-start | bytes 884744 | tf_op jit(solution)/shard_map/ppermute | solution.py:49
  0.7 2.4 %collective-permute-start.1 = (bf16[192,768]{1,0:T(8,128)(2,1)}, bf16[192,768]{1,0:T(8,128)(2,1)S(1)}, u32[]{:S(2)}, u32[]{:S(2)}) collective-permute-start(bf16[192,768]{1,0:T(8,128)(2,1)} %img.1), channel_id=1, source_target_pairs={{0,2},{1,3},{2,0},{3,1},{4,6},{5,7},{6,4},{7,5},{8,10},{9,11},{10,... | collective-permute-start | bytes 884744 | tf_op jit(solution)/shard_map/ppermute | solution.py:49
  1.9 1.2 %collective-permute-start.2 = (s32[1,192]{1,0:T(1,128)S(1)}, s32[1,192]{1,0:T(1,128)S(1)}, u32[]{:S(2)}, u32[]{:S(2)}) collective-permute-start(s32[1,192]{1,0:T(1,128)S(1)} %bitcast.3), channel_id=1, source_target_pairs={{0,2},{1,3},{2,0},{3,1},{4,6},{5,7},{6,4},{7,5},{8,10},{9,11},{10,... | collective-permute-start | bytes 2312 | tf_op jit(solution)/shard_map/ppermute | solution.py:49
  3.1 1.0 copy-start
  4.1 1.0 copy-start.1
  5.5 10.0 %collective-permute-start.3 = (bf16[384,768]{1,0:T(8,128)(2,1)S(1)}, bf16[384,768]{1,0:T(8,128)(2,1)S(1)}, u32[]{:S(2)}, u32[]{:S(2)}) collective-permute-start(bf16[384,768]{1,0:T(8,128)(2,1)S(1)} %get-tuple-element.26.refs_0_), channel_id=1, source_target_pairs={{0,1},{1,0},{2,19},{3,18},{4,5},{5,4},{6,23},{7,22},{8,9},{9,8},{1... | collective-permute-start | bytes 1769480 | tf_op jit(solution)/shard_map/ppermute | solution.py:49
  7.3 12.3 %collective-permute-start.4 = (bf16[384,768]{1,0:T(8,128)(2,1)S(1)}, bf16[384,768]{1,0:T(8,128)(2,1)S(1)}, u32[]{:S(2)}, u32[]{:S(2)}) collective-permute-start(bf16[384,768]{1,0:T(8,128)(2,1)S(1)} %get-tuple-element.26.refs_0_), channel_id=1, source_target_pairs={{0,4},{1,5},{2,34},{3,35},{4,8},{5,9},{6,38},{7,39},{8,12},{9,13},... | collective-permute-start | bytes 1769480 | tf_op jit(solution)/shard_map/ppermute | solution.py:49
  9.2 11.3 %collective-permute-start.5 = (bf16[384,768]{1,0:T(8,128)(2,1)S(1)}, bf16[384,768]{1,0:T(8,128)(2,1)S(1)}, u32[]{:S(2)}, u32[]{:S(2)}) collective-permute-start(bf16[384,768]{1,0:T(8,128)(2,1)S(1)} %get-tuple-element.26.refs_0_), channel_id=1, source_target_pairs={{0,12},{1,13},{2,98},{3,99},{4,0},{5,1},{6,102},{7,103},{8,4},{9,5... | collective-permute-start | bytes 1769480 | tf_op jit(solution)/shard_map/ppermute | solution.py:49
  15.5 11.5 %collective-permute-start.10 = (bf16[384,768]{1,0:T(8,128)(2,1)S(1)}, bf16[384,768]{1,0:T(8,128)(2,1)S(1)}, u32[]{:S(2)}, u32[]{:S(2)}) collective-permute-start(bf16[384,768]{1,0:T(8,128)(2,1)S(1)} %collective-permute-done.3.refs_1_), channel_id=1, source_target_pairs={{0,12},{1,13},{2,98},{3,99},{4,0},{5,1},{6,102},{7,103},{8,4},{9,5... | collective-permute-start | bytes 1769480 | tf_op jit(solution)/shard_map/ppermute | solution.py:49
  19.6 11.1 %collective-permute-start.6 = (bf16[384,768]{1,0:T(8,128)(2,1)S(1)}, bf16[384,768]{1,0:T(8,128)(2,1)S(1)}, u32[]{:S(2)}, u32[]{:S(2)}) collective-permute-start(bf16[384,768]{1,0:T(8,128)(2,1)S(1)} %collective-permute-done.3.refs_1_), channel_id=1, source_target_pairs={{0,2},{1,3},{2,0},{3,1},{4,6},{5,7},{6,4},{7,5},{8,10},{9,11},{10,... | collective-permute-start | bytes 1769480 | tf_op jit(solution)/shard_map/ppermute | solution.py:49
  19.6 11.1 %collective-permute-start.7 = (bf16[384,768]{1,0:T(8,128)(2,1)S(1)}, bf16[384,768]{1,0:T(8,128)(2,1)S(1)}, u32[]{:S(2)}, u32[]{:S(2)}) collective-permute-start(bf16[384,768]{1,0:T(8,128)(2,1)S(1)} %collective-permute-done.4.refs_2_), channel_id=1, source_target_pairs={{0,2},{1,3},{2,0},{3,1},{4,6},{5,7},{6,4},{7,5},{8,10},{9,11},{10,... | collective-permute-start | bytes 1769480 | tf_op jit(solution)/shard_map/ppermute | solution.py:49
  20.1 11.1 %collective-permute-start.9 = (bf16[384,768]{1,0:T(8,128)(2,1)S(1)}, bf16[384,768]{1,0:T(8,128)(2,1)S(1)}, u32[]{:S(2)}, u32[]{:S(2)}) collective-permute-start(bf16[384,768]{1,0:T(8,128)(2,1)S(1)} %collective-permute-done.3.refs_1_), channel_id=1, source_target_pairs={{0,4},{1,5},{2,34},{3,35},{4,8},{5,9},{6,38},{7,39},{8,12},{9,13},... | collective-permute-start | bytes 1769480 | tf_op jit(solution)/shard_map/ppermute | solution.py:49
  20.5 17.1 %collective-permute-start.13 = (bf16[384,768]{1,0:T(8,128)(2,1)S(1)}, bf16[384,768]{1,0:T(8,128)(2,1)S(1)}, u32[]{:S(2)}, u32[]{:S(2)}) collective-permute-start(bf16[384,768]{1,0:T(8,128)(2,1)S(1)} %collective-permute-done.4.refs_2_), channel_id=1, source_target_pairs={{0,4},{1,5},{2,34},{3,35},{4,8},{5,9},{6,38},{7,39},{8,12},{9,13},... | collective-permute-start | bytes 1769480 | tf_op jit(solution)/shard_map/ppermute | solution.py:49
  27.0 11.1 %collective-permute-start.14 = (bf16[384,768]{1,0:T(8,128)(2,1)S(1)}, bf16[384,768]{1,0:T(8,128)(2,1)S(1)}, u32[]{:S(2)}, u32[]{:S(2)}) collective-permute-start(bf16[384,768]{1,0:T(8,128)(2,1)S(1)} %collective-permute-done.10.refs_3_), channel_id=1, source_target_pairs={{0,12},{1,13},{2,98},{3,99},{4,0},{5,1},{6,102},{7,103},{8,4},{9,5... | collective-permute-start | bytes 1769480 | tf_op jit(solution)/shard_map/ppermute | solution.py:49
  30.7 29.0 %collective-permute-start.8 = (bf16[384,768]{1,0:T(8,128)(2,1)S(1)}, bf16[384,768]{1,0:T(8,128)(2,1)S(1)}, u32[]{:S(2)}, u32[]{:S(2)}) collective-permute-start(bf16[384,768]{1,0:T(8,128)(2,1)S(1)} %collective-permute-done.5.refs_3_), channel_id=1, source_target_pairs={{0,2},{1,3},{2,0},{3,1},{4,6},{5,7},{6,4},{7,5},{8,10},{9,11},{10,... | collective-permute-start | bytes 1769480 | tf_op jit(solution)/shard_map/ppermute | solution.py:49
  30.7 30.4 %collective-permute-start.12 = (bf16[384,768]{1,0:T(8,128)(2,1)S(1)}, bf16[384,768]{1,0:T(8,128)(2,1)S(1)}, u32[]{:S(2)}, u32[]{:S(2)}) collective-permute-start(bf16[384,768]{1,0:T(8,128)(2,1)S(1)} %collective-permute-done.10.refs_3_), channel_id=1, source_target_pairs={{0,2},{1,3},{2,0},{3,1},{4,6},{5,7},{6,4},{7,5},{8,10},{9,11},{10,... | collective-permute-start | bytes 1769480 | tf_op jit(solution)/shard_map/ppermute | solution.py:49
  31.2 29.9 %collective-permute-start.11 = (bf16[384,768]{1,0:T(8,128)(2,1)S(1)}, bf16[384,768]{1,0:T(8,128)(2,1)S(1)}, u32[]{:S(2)}, u32[]{:S(2)}) collective-permute-start(bf16[384,768]{1,0:T(8,128)(2,1)S(1)} %collective-permute-done.9.refs_2_), channel_id=1, source_target_pairs={{0,2},{1,3},{2,0},{3,1},{4,6},{5,7},{6,4},{7,5},{8,10},{9,11},{10,... | collective-permute-start | bytes 1769480 | tf_op jit(solution)/shard_map/ppermute | solution.py:49
  37.5 24.8 %collective-permute-start.15 = (bf16[384,768]{1,0:T(8,128)(2,1)S(1)}, bf16[384,768]{1,0:T(8,128)(2,1)S(1)}, u32[]{:S(2)}, u32[]{:S(2)}) collective-permute-start(bf16[384,768]{1,0:T(8,128)(2,1)S(1)} %collective-permute-done.13.refs_2_), channel_id=1, source_target_pairs={{0,2},{1,3},{2,0},{3,1},{4,6},{5,7},{6,4},{7,5},{8,10},{9,11},{10,... | collective-permute-start | bytes 1769480 | tf_op jit(solution)/shard_map/ppermute | solution.py:49
  38.1 24.2 %collective-permute-start.16 = (bf16[384,768]{1,0:T(8,128)(2,1)S(1)}, bf16[384,768]{1,0:T(8,128)(2,1)S(1)}, u32[]{:S(2)}, u32[]{:S(2)}) collective-permute-start(bf16[384,768]{1,0:T(8,128)(2,1)S(1)} %collective-permute-done.14.refs_3_), channel_id=1, source_target_pairs={{0,2},{1,3},{2,0},{3,1},{4,6},{5,7},{6,4},{7,5},{8,10},{9,11},{10,... | collective-permute-start | bytes 1769480 | tf_op jit(solution)/shard_map/ppermute | solution.py:49

commit v2 on v1

--- a/solution.py
+++ b/solution.py
@@ -27,9 +27,8 @@
 R = -(-CAPS * B // RC) * RC
 CAP_ROWS = CAPS * B + RC
 NC = 256
-COUNTS = (2, 4, 5, 6, 7, 8, 10, 12)
-TAIL = 2 * NC
-IMG_ROWS = C + TAIL
+GROUP = 7 * NC
+IMG_ROWS = -(-C // GROUP) * GROUP
 PIECE = 64
 GRAIN = 16
 OK_BIT = 15
@@ -189,6 +188,10 @@
     return found + [pl.multiple_of(at, GRAIN)]
 
 
+def groups_of(columns):
+    return jnp.maximum(lax.div(columns + (GROUP - 1), GROUP), 1)
+
+
 def compact(counts, ranks, carried, kept, cap_out, img_out, first):
     core = lax.axis_index("c")
     slot = iota((B, B), 0)
@@ -214,7 +217,17 @@
         cap_end = starts_of(counts, 0, CAPS)[-1]
         img_end = starts_of(counts, CAPS, IMGS)[-1]
         cap_out[pl.ds(cap_end, RC), :] = jnp.zeros((RC, E), BF16)
-        img_out[pl.ds(img_end, TAIL), :] = jnp.zeros((TAIL, E), BF16)
+        blank = jnp.zeros((64, E), BF16)
+        goal = groups_of(img_end) * GROUP
+
+        @pl.loop(0, lax.div(goal - img_end, 64))
+        def _(i):
+            img_out[pl.ds(pl.multiple_of(img_end + i * 64, GRAIN), 64), :] = blank
+
+        img_out[pl.ds(pl.multiple_of(goal - 64, GRAIN), 64), :] = jnp.where(
+            iota((64, E), 0) + (goal - 64).astype(F32) < img_end.astype(F32),
+            img_out[pl.ds(pl.multiple_of(goal - 64, GRAIN), 64), :], blank,
+        )
 
 
 def score_kernel(
@@ -222,8 +235,8 @@
     t_v, pos_b, bias_b, rmax, rmatch, rsum, col_bias, cmax, cmatch, csum, lines_v,
 ):
     img_at = starts_of(counts, CAPS, IMGS)
-    column = iota((8, C), 1)
-    bias = jnp.full((8, C), LOW, F32)
+    column = iota((8, IMG_ROWS), 1)
+    bias = jnp.full((8, IMG_ROWS), LOW, F32)
     for m in range(IMGS):
         begin = img_at[m].astype(F32)
         end = begin + counts[CAPS + m, 0].astype(F32)
@@ -243,67 +256,82 @@
     cmatch[...] = jnp.zeros(cmatch.shape, F32)
     csum[...] = jnp.zeros(csum.shape, F32)
 
-    def tiles(count):
-        @pl.loop(0, lax.div(rows_used + (RC - 1), RC))
-        def _(i):
-            rows = pl.ds(pl.multiple_of(i * RC, RC), RC)
-            a = cap_v[rows, :]
-            for n in range(count):
-                s = lax.dot_general(
-                    a, img_v[n * NC:(n + 1) * NC, :], (((1,), (1,)), ((), ())),
-                    preferred_element_type=F32,
+    groups = groups_of(img_at[IMGS])
+    steps = lax.div(rows_used + (RC - 1), RC)
+
+    @pl.loop(0, steps)
+    def _(i):
+        rows = pl.ds(pl.multiple_of(i * RC, RC), RC)
+        rmax[rows, :] = jnp.full((RC, 128), 4.0 * LOW, F32)
+        rmatch[rows, :] = jnp.zeros((RC, 128), F32)
+        rsum[rows, :] = jnp.zeros((RC, 128), F32)
+
+    @pl.loop(0, groups * steps)
+    def _(at):
+        g = lax.div(at, steps)
+        first = pl.multiple_of(g * GROUP, GROUP)
+        rows = pl.ds(pl.multiple_of((at - g * steps) * RC, RC), RC)
+        a = cap_v[rows, :]
+        for n in range(GROUP // NC):
+            s = lax.dot_general(
+                a, img_v[pl.ds(pl.multiple_of(first + n * NC, NC), NC), :],
+                (((1,), (1,)), ((), ())), preferred_element_type=F32,
+            )
+            q = s * LOG2E
+            highest, found = None, None
+            for half in range(2):
+                column = first + (n * NC + half * 128)
+                span = pl.ds(pl.multiple_of(column, 128), 128)
+                qh = q[:, half * 128:(half + 1) * 128]
+                t = (qh + bias_b[rows, :]) + col_bias[0:1, span]
+                t_v[rows, span] = t
+                number = iota((1, 128), 1) + column.astype(F32)
+                w = jnp.where(pos_b[rows, :] == number, qh, 0.0)
+                highest = t if half == 0 else jnp.maximum(highest, t)
+                found = w if half == 0 else found + w
+                cmax[:, span] = jnp.maximum(
+                    cmax[:, span], jnp.max(t.reshape(-1, 8, 128), axis=0)
                 )
-                q = s * LOG2E
-                highest, found = None, None
-                for half in range(2):
-                    span = pl.ds(n * NC + half * 128, 128)
-                    qh = q[:, half * 128:(half + 1) * 128]
-                    t = (qh + bias_b[rows, :]) + col_bias[0:1, span]
-                    t_v[rows, span] = t
-                    number = iota((1, 128), 1) + float(n * NC + half * 128)
-                    w = jnp.where(pos_b[rows, :] == number, qh, 0.0)
-                    highest = t if half == 0 else jnp.maximum(highest, t)
-                    found = w if half == 0 else found + w
-                    cmax[:, span] = jnp.maximum(
-                        cmax[:, span], jnp.max(t.reshape(-1, 8, 128), axis=0)
-                    )
-                    cmatch[:, span] += jnp.sum(w.reshape(-1, 8, 128), axis=0)
-                if n == 0:
-                    rmax[rows, :] = highest
-                    rmatch[rows, :] = found
-                else:
-                    rmax[rows, :] = jnp.maximum(rmax[rows, :], highest)
-                    rmatch[rows, :] += found
-            rmax[rows, :] = jnp.broadcast_to(
-                jnp.max(rmax[rows, :], axis=1, keepdims=True), (RC, 128)
-            )
-
-        top = jnp.max(cmax[...], axis=0, keepdims=True)
-        cmax[...] = jnp.broadcast_to(top, cmax.shape)
+                cmatch[:, span] += jnp.sum(w.reshape(-1, 8, 128), axis=0)
+            rmax[rows, :] = jnp.maximum(rmax[rows, :], highest)
+            rmatch[rows, :] += found
+
+    @pl.loop(0, steps)
+    def _(i):
+        rows = pl.ds(pl.multiple_of(i * RC, RC), RC)
+        rmax[rows, :] = jnp.broadcast_to(
+            jnp.max(rmax[rows, :], axis=1, keepdims=True), (RC, 128)
+        )
+
+    top = jnp.max(cmax[...], axis=0, keepdims=True)
+    cmax[...] = jnp.broadcast_to(top, cmax.shape)
+    width = GROUP // 128
+
+    @pl.loop(0, groups)
+    def _(g):
+        spans = [
+            pl.ds(pl.multiple_of(g * GROUP + n * 128, 128), 128) for n in range(width)
+        ]
 
         def piece(r, totals):
             rows = pl.ds(pl.multiple_of(r * PIECE, PIECE), PIECE)
             peak = rmax[rows, :]
-            acc = jnp.zeros((PIECE, 128), F32)
+            acc = rsum[rows, :]
             out = []
-            for n in range(2 * count):
-                t = t_v[rows, n * 128:(n + 1) * 128]
+            for n, span in enumerate(spans):
+                t = t_v[rows, span]
                 acc = acc + jnp.exp2(t - peak)
-                f = jnp.exp2(t.reshape(-1, 8, 128) - cmax[:, n * 128:(n + 1) * 128][None])
+                f = jnp.exp2(t.reshape(-1, 8, 128) - cmax[:, span][None])
                 out.append(totals[n] + jnp.sum(f, axis=0))
             rsum[rows, :] = acc
             return tuple(out)
 
         totals = lax.fori_loop(
             0, lax.div(rows_used + (PIECE - 1), PIECE), piece,
-            tuple(jnp.zeros((8, 128), F32) for _ in range(2 * count)),
+            tuple(jnp.zeros((8, 128), F32) for _ in range(width)),
         )
-        for n in range(2 * count):
-            csum[:, n * 128:(n + 1) * 128] = totals[n]
-
-    used = jnp.maximum(lax.div(img_at[IMGS] + (NC - 1), NC), 1)
-    for below, count in zip((0, *COUNTS), COUNTS):
-        pl.when((used > below) & (used <= count))(lambda count=count: tiles(count))
+        for n, span in enumerate(spans):
+            csum[:, span] = totals[n]
 
     p = place()
     lanes = lax.broadcasted_iota(jnp.int32, (B, 128), 1)
@@ -317,11 +345,11 @@
             put(out, flat(cap_place(p, k)), lines)
         else:
             put(own_row, 0, lines)
-    line = lax.broadcasted_iota(jnp.int32, (8, C), 0)
+    line = lax.broadcasted_iota(jnp.int32, (8, IMG_ROWS), 0)
     total = jnp.sum(csum[...], axis=0, keepdims=True)
     match = jnp.sum(cmatch[...], axis=0, keepdims=True)
-    lines_v[:, :C] = jnp.where(line == 0, cmax[0:1, :] + jnp.log2(total), match)
-    lines_v[:, C:] = jnp.zeros((8, 384), F32)
+    lines_v[:, :IMG_ROWS] = jnp.where(line == 0, cmax[0:1, :] + jnp.log2(total), match)
+    lines_v[:, IMG_ROWS:] = jnp.zeros((8, 384), F32)
     for m in range(IMGS):
         whole = lax.shift_left(lax.shift_right_logical(img_at[m], 7), 7)
         slab = lines_v[:, pl.ds(pl.multiple_of(whole, 128), 384)]
@@ -418,12 +446,12 @@
         in_specs=[SMEM] + [VMEM] * 3,
         out_specs=[VMEM] * 2,
         scratch_shapes=[
-            pltpu.VMEM((R, C), F32),
+            pltpu.VMEM((R, IMG_ROWS), F32),
             *[pltpu.VMEM((R + RC, 128), F32)] * 5,
-            *[pltpu.VMEM((8, C), F32)] * 4,
-            pltpu.VMEM((8, C + 384), F32),
+            *[pltpu.VMEM((8, IMG_ROWS), F32)] * 4,
+            pltpu.VMEM((8, IMG_ROWS + 384), F32),
         ],
-        compiler_params=pltpu.CompilerParams(vmem_limit_bytes=31 * 1024 * 1024),
+        compiler_params=pltpu.CompilerParams(vmem_limit_bytes=36 * 1024 * 1024),
         cost_estimate=pl.CostEstimate(
             flops=R * C * E, bytes_accessed=2 * (R + C) * E, transcendentals=R * C
         ),

time: 104 us -> 105 us (level)
  Pallas kernels: 15.6 us -> 16.9 us
    pallas_call x1, Pallas kernels: 9.11 us -> 10.4 us  [step(): pl.pallas_call(score_kernel, out_shape=[shape((n, 1, 2 * B), F32) for n i...]
where the time goes in v2:
time: 105 us; the launch traced here: 104 us
  blocking collectives  48.8 us (46%)
  starting transfers between devices  17.7 us (17%)
  Pallas kernels  16.9 us (16%)
  waiting for transfers between devices  16.7 us (16%)
  local copies, waits for them, and re-layouts  1.92 us (2%)
  other arithmetic  1.43 us (1%)
    all_to_all x1, blocking collectives, step(): table = lax.all_to_all(words, AXES, 0, 0, tiled=True)  20.3 us
    ppermute x17, starting transfers between devices, send(): return lax.ppermute(value, AXES, pairs)  17.7 us
    ppermute x17, waiting for transfers between devices, send(): return lax.ppermute(value, AXES, pairs)  16.7 us
    all_to_all x1, blocking collectives, step(): parts = lax.all_to_all(out, AXES, 0, 0, tiled=True)  14.6 us
    all_to_all x1, blocking collectives, step(): totals = lax.all_to_all(total, AXES, 0, 0, tiled=True)  13.9 us
    pallas_call x1, Pallas kernels, step(): pl.pallas_call(score_kernel, out_shape=[shape((n, 1, 2 * B), F32) for n i...  10.4 us
    pallas_call x3, Pallas kernels, step(): pl.pallas_call(functools.partial(compact_kernel, part), out_shape=[shape(...  3.85 us
  transfers between devices with their start and end apart: 17, of which 5 were waited for; matrix products, arithmetic and copies ran while one was open for 1% of the time, Pallas kernels for 4%

profile of v2, /device:TPU:0, one launch (start us, length us, event | category | flops | bytes accessed | tf_op | source)
XLA Modules:
  0.0 104.1 jit_solution(7651584618870358985)
XLA Ops:
  0.6 0.1 collective-permute-start
  0.7 0.5 collective-permute-start.1
  1.2 0.7 multiply_add_fusion
  1.9 0.1 collective-permute-start.2
  2.0 1.1 %collective-permute-done.2.word_other = s32[1,192]{1,0:T(1,128)S(1)} collective-permute-done((s32[1,192]{1,0:T(1,128)S(1)}, s32[1,192]{1,0:T(1,128)S(1)}, u32[]{:S(2)}, u32[]{:S(2)}) %collective-permute-start.2) | collective-permute-done | bytes 800 | tf_op jit(solution)/shard_map/ppermute | solution.py:48
  3.1 1.0 copy-done
  4.1 1.0 copy-done.1
  5.0 0.5 shard_map.67
  5.5 1.8 %collective-permute-start.3 = (bf16[384,768]{1,0:T(8,128)(2,1)S(1)}, bf16[384,768]{1,0:T(8,128)(2,1)S(1)}, u32[]{:S(2)}, u32[]{:S(2)}) collective-permute-start(bf16[384,768]{1,0:T(8,128)(2,1)S(1)} %get-tuple-element.26.refs_0_), channel_id=1, source_target_pairs={{0,1},{1,0},{2,19},{3,18},{4,5},{5,4},{6,23},{7,22},{8,9},{9,8},{1... | collective-permute-start | bytes 1769480 | tf_op jit(solution)/shard_map/ppermute | solution.py:48
  7.3 1.9 %collective-permute-start.4 = (bf16[384,768]{1,0:T(8,128)(2,1)S(1)}, bf16[384,768]{1,0:T(8,128)(2,1)S(1)}, u32[]{:S(2)}, u32[]{:S(2)}) collective-permute-start(bf16[384,768]{1,0:T(8,128)(2,1)S(1)} %get-tuple-element.26.refs_0_), channel_id=1, source_target_pairs={{0,4},{1,5},{2,34},{3,35},{4,8},{5,9},{6,38},{7,39},{8,12},{9,13},... | collective-permute-start | bytes 1769480 | tf_op jit(solution)/shard_map/ppermute | solution.py:48
  9.2 2.1 %collective-permute-start.5 = (bf16[384,768]{1,0:T(8,128)(2,1)S(1)}, bf16[384,768]{1,0:T(8,128)(2,1)S(1)}, u32[]{:S(2)}, u32[]{:S(2)}) collective-permute-start(bf16[384,768]{1,0:T(8,128)(2,1)S(1)} %get-tuple-element.26.refs_0_), channel_id=1, source_target_pairs={{0,12},{1,13},{2,98},{3,99},{4,0},{5,1},{6,102},{7,103},{8,4},{9,5... | collective-permute-start | bytes 1769480 | tf_op jit(solution)/shard_map/ppermute | solution.py:48
  11.3 4.2 %collective-permute-done.3.refs_1_ = bf16[384,768]{1,0:T(8,128)(2,1)S(1)} collective-permute-done((bf16[384,768]{1,0:T(8,128)(2,1)S(1)}, bf16[384,768]{1,0:T(8,128)(2,1)S(1)}, u32[]{:S(2)}, u32[]{:S(2)}) %collective-permute-start.3) | collective-permute-done | bytes 589856 | tf_op jit(solution)/shard_map/ppermute | solution.py:48
  15.5 4.1 %collective-permute-start.10 = (bf16[384,768]{1,0:T(8,128)(2,1)S(1)}, bf16[384,768]{1,0:T(8,128)(2,1)S(1)}, u32[]{:S(2)}, u32[]{:S(2)}) collective-permute-start(bf16[384,768]{1,0:T(8,128)(2,1)S(1)} %collective-permute-done.3.refs_1_), channel_id=1, source_target_pairs={{0,12},{1,13},{2,98},{3,99},{4,0},{5,1},{6,102},{7,103},{8,4},{9,5... | collective-permute-start | bytes 1769480 | tf_op jit(solution)/shard_map/ppermute | solution.py:48
  19.6 0.5 collective-permute-start.7
  20.1 0.3 collective-permute-start.9
  20.5 1.9 %collective-permute-start.13 = (bf16[384,768]{1,0:T(8,128)(2,1)S(1)}, bf16[384,768]{1,0:T(8,128)(2,1)S(1)}, u32[]{:S(2)}, u32[]{:S(2)}) collective-permute-start(bf16[384,768]{1,0:T(8,128)(2,1)S(1)} %collective-permute-done.4.refs_2_), channel_id=1, source_target_pairs={{0,4},{1,5},{2,34},{3,35},{4,8},{5,9},{6,38},{7,39},{8,12},{9,13},... | collective-permute-start | bytes 1769480 | tf_op jit(solution)/shard_map/ppermute | solution.py:48
  22.4 4.6 %collective-permute-done.10.refs_3_ = bf16[384,768]{1,0:T(8,128)(2,1)S(1)} collective-permute-done((bf16[384,768]{1,0:T(8,128)(2,1)S(1)}, bf16[384,768]{1,0:T(8,128)(2,1)S(1)}, u32[]{:S(2)}, u32[]{:S(2)}) %collective-permute-start.10) | collective-permute-done | bytes 589856 | tf_op jit(solution)/shard_map/ppermute | solution.py:48
  27.0 3.7 %collective-permute-start.14 = (bf16[384,768]{1,0:T(8,128)(2,1)S(1)}, bf16[384,768]{1,0:T(8,128)(2,1)S(1)}, u32[]{:S(2)}, u32[]{:S(2)}) collective-permute-start(bf16[384,768]{1,0:T(8,128)(2,1)S(1)} %collective-permute-done.10.refs_3_), channel_id=1, source_target_pairs={{0,12},{1,13},{2,98},{3,99},{4,0},{5,1},{6,102},{7,103},{8,4},{9,5... | collective-permute-start | bytes 1769480 | tf_op jit(solution)/shard_map/ppermute | solution.py:48
  30.7 0.5 collective-permute-start.12
  31.2 0.1 collective-permute-start.11
  31.3 6.2 %collective-permute-done.13.refs_2_ = bf16[384,768]{1,0:T(8,128)(2,1)S(1)} collective-permute-done((bf16[384,768]{1,0:T(8,128)(2,1)S(1)}, bf16[384,768]{1,0:T(8,128)(2,1)S(1)}, u32[]{:S(2)}, u32[]{:S(2)}) %collective-permute-start.13) | collective-permute-done | bytes 589856 | tf_op jit(solution)/shard_map/ppermute | solution.py:48
  37.5 0.6 collective-permute-done.14.refs_3_
  38.1 20.3 %all_to_all.15.table = s32[128,1,192]{2,1,0:T(1,128)S(1)} all-to-all(s32[128,1,192]{2,1,0:T(1,128)S(1)} %get-tuple-element.22), channel_id=1, replica_groups=mesh['x'=4,'h'=2,'z'=4,'c'=2,'l'=2] {'x','h','z','c','l'}, dimensions={0} | all-to-all | bytes 196608 | tf_op jit(solution)/shard_map/all_to_all | solution.py:420
  58.4 1.2 %shard_map.68 = (f32[8,192]{1,0:T(8,128)S(1)}, f32[192,128]{1,0:T(8,128)S(1)}, s32[24,128]{1,0:T(8,128)S(1)}, f32[8,128]{1,0:T(8,128)S(1)}) custom-call(s32[128,1,192]{2,1,0:T(1,128)S(1)} %all_to_all.15.table), custom_call_target="tpu_custom_call" | custom-call | flops 3000000000 | bytes 1000000 | tf_op jit(solution)/shard_map/pallas_call | solution.py:421
  59.7 1.4 %shard_map.69 = (bf16[1984,768]{1,0:T(8,128)(2,1)S(1)}, bf16[3584,768]{1,0:T(8,128)(2,1)S(1)}) custom-call(s32[24,128]{1,0:T(8,128)S(1)} %get-tuple-element.23.counts, f32[8,192]{1,0:T(8,128)S(1)} %get-tuple-element.25.ranks.row_ranks, bf16[384,768]{1,0:T(8,128)(2,1)S(1)} %get-tuple-element.26.refs_0_, bf16[384,768]{1,0:T(8,128)(2,1)S(1)} %collective-permute-done.3.refs_1_, ...), custom_call_target="tpu_custom_call" | custom-call | flops 1000000000 | bytes 1000000 | tf_op jit(solution)/shard_map/pallas_call | solution.py:434
  61.1 1.2 %shard_map.70 = (bf16[1984,768]{1,0:T(8,128)(2,1)S(1)}, bf16[3584,768]{1,0:T(8,128)(2,1)S(1)}) custom-call(s32[24,128]{1,0:T(8,128)S(1)} %get-tuple-element.23.counts, f32[8,192]{1,0:T(8,128)S(1)} %get-tuple-element.25.ranks.row_ranks, bf16[1984,768]{1,0:T(8,128)(2,1)S(1)} %get-tuple-element.28.refs_0_, ...), custom_call_target="tpu_custom_call", output_to_operand_aliasing={{0}: (2, {}), {1}: (3, {})} | custom-call | flops 1000000000 | bytes 1000000 | tf_op jit(solution)/shard_map/pallas_call | solution.py:434
  62.3 1.3 %shard_map.71 = (bf16[1984,768]{1,0:T(8,128)(2,1)S(1)}, bf16[3584,768]{1,0:T(8,128)(2,1)S(1)}) custom-call(s32[24,128]{1,0:T(8,128)S(1)} %get-tuple-element.23.counts, f32[8,192]{1,0:T(8,128)S(1)} %get-tuple-element.25.ranks.row_ranks, bf16[1984,768]{1,0:T(8,128)(2,1)S(1)} %get-tuple-element.30.refs_0_, ...), custom_call_target="tpu_custom_call", output_to_operand_aliasing={{0}: (2, {}), {1}: (3, {})} | custom-call | flops 1000000000 | bytes 1000000 | tf_op jit(solution)/shard_map/pallas_call | solution.py:434
  63.6 10.4 %shard_map.72 = (f32[128,1,384]{2,1,0:T(1,128)S(1)}, f32[1,1,384]{2,1,0:T(1,128)S(1)}) custom-call(s32[24,128]{1,0:T(8,128)S(1)} %get-tuple-element.23.counts, f32[192,128]{1,0:T(8,128)S(1)} %get-tuple-element.24.columns, bf16[1984,768]{1,0:T(8,128)(2,1)S(1)} %get-tuple-element.32.cap_v, bf16[3584,768]{1,0:T(8,128)(2,1)S(1)} %get-tuple-element.33.img_v), custom_call_target="tpu_custom_call" | custom-call | flops 4227858432 | bytes 7471104 | tf_op jit(solution)/shard_map/pallas_call | solution.py:443
  74.0 14.6 %all_to_all.16.parts = f32[128,1,384]{2,1,0:T(1,128)S(1)} all-to-all(f32[128,1,384]{2,1,0:T(1,128)S(1)} %get-tuple-element.34), channel_id=1, replica_groups=mesh['x'=4,'h'=2,'z'=4,'c'=2,'l'=2] {'x','h','z','c','l'}, dimensions={0} | all-to-all | bytes 393216 | tf_op jit(solution)/shard_map/all_to_all | solution.py:459
  88.6 0.9 shard_map.73
  89.5 13.9 %all_to_all.17 = f32[128,1,8]{2,1,0:T(1,128)S(1)} all-to-all(f32[128,1,8]{2,1,0:T(1,128)S(1)} %get-tuple-element.40), channel_id=1, replica_groups=mesh['x'=4,'h'=2,'z'=4,'c'=2,'l'=2] {'x','h','z','c','l'}, dimensions={0} | all-to-all | bytes 8192 | tf_op jit(solution)/shard_map/all_to_all | solution.py:468
  103.4 0.7 slice_reduce_fusion
  (18 shorter events, 0.0 us)
Async XLA Ops:
  0.6 2.5 %collective-permute-start = (bf16[192,768]{1,0:T(8,128)(2,1)}, bf16[192,768]{1,0:T(8,128)(2,1)S(1)}, u32[]{:S(2)}, u32[]{:S(2)}) collective-permute-start(bf16[192,768]{1,0:T(8,128)(2,1)} %cap.1), channel_id=1, source_target_pairs={{0,2},{1,3},{2,0},{3,1},{4,6},{5,7},{6,4},{7,5},{8,10},{9,11},{10,... | collective-permute-start | bytes 884744 | tf_op jit(solution)/shard_map/ppermute | solution.py:48
  0.7 2.4 %collective-permute-start.1 = (bf16[192,768]{1,0:T(8,128)(2,1)}, bf16[192,768]{1,0:T(8,128)(2,1)S(1)}, u32[]{:S(2)}, u32[]{:S(2)}) collective-permute-start(bf16[192,768]{1,0:T(8,128)(2,1)} %img.1), channel_id=1, source_target_pairs={{0,2},{1,3},{2,0},{3,1},{4,6},{5,7},{6,4},{7,5},{8,10},{9,11},{10,... | collective-permute-start | bytes 884744 | tf_op jit(solution)/shard_map/ppermute | solution.py:48
  1.9 1.2 %collective-permute-start.2 = (s32[1,192]{1,0:T(1,128)S(1)}, s32[1,192]{1,0:T(1,128)S(1)}, u32[]{:S(2)}, u32[]{:S(2)}) collective-permute-start(s32[1,192]{1,0:T(1,128)S(1)} %bitcast.3), channel_id=1, source_target_pairs={{0,2},{1,3},{2,0},{3,1},{4,6},{5,7},{6,4},{7,5},{8,10},{9,11},{10,... | collective-permute-start | bytes 2312 | tf_op jit(solution)/shard_map/ppermute | solution.py:48
  3.1 1.0 copy-start
  4.1 1.0 copy-start.1
  5.5 10.0 %collective-permute-start.3 = (bf16[384,768]{1,0:T(8,128)(2,1)S(1)}, bf16[384,768]{1,0:T(8,128)(2,1)S(1)}, u32[]{:S(2)}, u32[]{:S(2)}) collective-permute-start(bf16[384,768]{1,0:T(8,128)(2,1)S(1)} %get-tuple-element.26.refs_0_), channel_id=1, source_target_pairs={{0,1},{1,0},{2,19},{3,18},{4,5},{5,4},{6,23},{7,22},{8,9},{9,8},{1... | collective-permute-start | bytes 1769480 | tf_op jit(solution)/shard_map/ppermute | solution.py:48
  7.3 12.3 %collective-permute-start.4 = (bf16[384,768]{1,0:T(8,128)(2,1)S(1)}, bf16[384,768]{1,0:T(8,128)(2,1)S(1)}, u32[]{:S(2)}, u32[]{:S(2)}) collective-permute-start(bf16[384,768]{1,0:T(8,128)(2,1)S(1)} %get-tuple-element.26.refs_0_), channel_id=1, source_target_pairs={{0,4},{1,5},{2,34},{3,35},{4,8},{5,9},{6,38},{7,39},{8,12},{9,13},... | collective-permute-start | bytes 1769480 | tf_op jit(solution)/shard_map/ppermute | solution.py:48
  9.2 11.3 %collective-permute-start.5 = (bf16[384,768]{1,0:T(8,128)(2,1)S(1)}, bf16[384,768]{1,0:T(8,128)(2,1)S(1)}, u32[]{:S(2)}, u32[]{:S(2)}) collective-permute-start(bf16[384,768]{1,0:T(8,128)(2,1)S(1)} %get-tuple-element.26.refs_0_), channel_id=1, source_target_pairs={{0,12},{1,13},{2,98},{3,99},{4,0},{5,1},{6,102},{7,103},{8,4},{9,5... | collective-permute-start | bytes 1769480 | tf_op jit(solution)/shard_map/ppermute | solution.py:48
  15.5 11.5 %collective-permute-start.10 = (bf16[384,768]{1,0:T(8,128)(2,1)S(1)}, bf16[384,768]{1,0:T(8,128)(2,1)S(1)}, u32[]{:S(2)}, u32[]{:S(2)}) collective-permute-start(bf16[384,768]{1,0:T(8,128)(2,1)S(1)} %collective-permute-done.3.refs_1_), channel_id=1, source_target_pairs={{0,12},{1,13},{2,98},{3,99},{4,0},{5,1},{6,102},{7,103},{8,4},{9,5... | collective-permute-start | bytes 1769480 | tf_op jit(solution)/shard_map/ppermute | solution.py:48
  19.6 11.1 %collective-permute-start.6 = (bf16[384,768]{1,0:T(8,128)(2,1)S(1)}, bf16[384,768]{1,0:T(8,128)(2,1)S(1)}, u32[]{:S(2)}, u32[]{:S(2)}) collective-permute-start(bf16[384,768]{1,0:T(8,128)(2,1)S(1)} %collective-permute-done.3.refs_1_), channel_id=1, source_target_pairs={{0,2},{1,3},{2,0},{3,1},{4,6},{5,7},{6,4},{7,5},{8,10},{9,11},{10,... | collective-permute-start | bytes 1769480 | tf_op jit(solution)/shard_map/ppermute | solution.py:48
  19.6 11.1 %collective-permute-start.7 = (bf16[384,768]{1,0:T(8,128)(2,1)S(1)}, bf16[384,768]{1,0:T(8,128)(2,1)S(1)}, u32[]{:S(2)}, u32[]{:S(2)}) collective-permute-start(bf16[384,768]{1,0:T(8,128)(2,1)S(1)} %collective-permute-done.4.refs_2_), channel_id=1, source_target_pairs={{0,2},{1,3},{2,0},{3,1},{4,6},{5,7},{6,4},{7,5},{8,10},{9,11},{10,... | collective-permute-start | bytes 1769480 | tf_op jit(solution)/shard_map/ppermute | solution.py:48
  20.1 11.1 %collective-permute-start.9 = (bf16[384,768]{1,0:T(8,128)(2,1)S(1)}, bf16[384,768]{1,0:T(8,128)(2,1)S(1)}, u32[]{:S(2)}, u32[]{:S(2)}) collective-permute-start(bf16[384,768]{1,0:T(8,128)(2,1)S(1)} %collective-permute-done.3.refs_1_), channel_id=1, source_target_pairs={{0,4},{1,5},{2,34},{3,35},{4,8},{5,9},{6,38},{7,39},{8,12},{9,13},... | collective-permute-start | bytes 1769480 | tf_op jit(solution)/shard_map/ppermute | solution.py:48
  20.5 17.1 %collective-permute-start.13 = (bf16[384,768]{1,0:T(8,128)(2,1)S(1)}, bf16[384,768]{1,0:T(8,128)(2,1)S(1)}, u32[]{:S(2)}, u32[]{:S(2)}) collective-permute-start(bf16[384,768]{1,0:T(8,128)(2,1)S(1)} %collective-permute-done.4.refs_2_), channel_id=1, source_target_pairs={{0,4},{1,5},{2,34},{3,35},{4,8},{5,9},{6,38},{7,39},{8,12},{9,13},... | collective-permute-start | bytes 1769480 | tf_op jit(solution)/shard_map/ppermute | solution.py:48
  27.0 11.1 %collective-permute-start.14 = (bf16[384,768]{1,0:T(8,128)(2,1)S(1)}, bf16[384,768]{1,0:T(8,128)(2,1)S(1)}, u32[]{:S(2)}, u32[]{:S(2)}) collective-permute-start(bf16[384,768]{1,0:T(8,128)(2,1)S(1)} %collective-permute-done.10.refs_3_), channel_id=1, source_target_pairs={{0,12},{1,13},{2,98},{3,99},{4,0},{5,1},{6,102},{7,103},{8,4},{9,5... | collective-permute-start | bytes 1769480 | tf_op jit(solution)/shard_map/ppermute | solution.py:48
  30.7 29.0 %collective-permute-start.8 = (bf16[384,768]{1,0:T(8,128)(2,1)S(1)}, bf16[384,768]{1,0:T(8,128)(2,1)S(1)}, u32[]{:S(2)}, u32[]{:S(2)}) collective-permute-start(bf16[384,768]{1,0:T(8,128)(2,1)S(1)} %collective-permute-done.5.refs_3_), channel_id=1, source_target_pairs={{0,2},{1,3},{2,0},{3,1},{4,6},{5,7},{6,4},{7,5},{8,10},{9,11},{10,... | collective-permute-start | bytes 1769480 | tf_op jit(solution)/shard_map/ppermute | solution.py:48
  30.7 30.4 %collective-permute-start.12 = (bf16[384,768]{1,0:T(8,128)(2,1)S(1)}, bf16[384,768]{1,0:T(8,128)(2,1)S(1)}, u32[]{:S(2)}, u32[]{:S(2)}) collective-permute-start(bf16[384,768]{1,0:T(8,128)(2,1)S(1)} %collective-permute-done.10.refs_3_), channel_id=1, source_target_pairs={{0,2},{1,3},{2,0},{3,1},{4,6},{5,7},{6,4},{7,5},{8,10},{9,11},{10,... | collective-permute-start | bytes 1769480 | tf_op jit(solution)/shard_map/ppermute | solution.py:48
  31.2 29.9 %collective-permute-start.11 = (bf16[384,768]{1,0:T(8,128)(2,1)S(1)}, bf16[384,768]{1,0:T(8,128)(2,1)S(1)}, u32[]{:S(2)}, u32[]{:S(2)}) collective-permute-start(bf16[384,768]{1,0:T(8,128)(2,1)S(1)} %collective-permute-done.9.refs_2_), channel_id=1, source_target_pairs={{0,2},{1,3},{2,0},{3,1},{4,6},{5,7},{6,4},{7,5},{8,10},{9,11},{10,... | collective-permute-start | bytes 1769480 | tf_op jit(solution)/shard_map/ppermute | solution.py:48
  37.5 24.8 %collective-permute-start.15 = (bf16[384,768]{1,0:T(8,128)(2,1)S(1)}, bf16[384,768]{1,0:T(8,128)(2,1)S(1)}, u32[]{:S(2)}, u32[]{:S(2)}) collective-permute-start(bf16[384,768]{1,0:T(8,128)(2,1)S(1)} %collective-permute-done.13.refs_2_), channel_id=1, source_target_pairs={{0,2},{1,3},{2,0},{3,1},{4,6},{5,7},{6,4},{7,5},{8,10},{9,11},{10,... | collective-permute-start | bytes 1769480 | tf_op jit(solution)/shard_map/ppermute | solution.py:48
  38.1 24.2 %collective-permute-start.16 = (bf16[384,768]{1,0:T(8,128)(2,1)S(1)}, bf16[384,768]{1,0:T(8,128)(2,1)S(1)}, u32[]{:S(2)}, u32[]{:S(2)}) collective-permute-start(bf16[384,768]{1,0:T(8,128)(2,1)S(1)} %collective-permute-done.14.refs_3_), channel_id=1, source_target_pairs={{0,2},{1,3},{2,0},{3,1},{4,6},{5,7},{6,4},{7,5},{8,10},{9,11},{10,... | collective-permute-start | bytes 1769480 | tf_op jit(solution)/shard_map/ppermute | solution.py:48

commit v3 on v1

--- a/solution.py
+++ b/solution.py
@@ -30,7 +30,7 @@
 COUNTS = (2, 4, 5, 6, 7, 8, 10, 12)
 TAIL = 2 * NC
 IMG_ROWS = C + TAIL
-PIECE = 64
+PIECE = 32
 GRAIN = 16
 OK_BIT = 15
 ABSENT = 9999.0
@@ -119,7 +119,10 @@
     order = dot(jnp.broadcast_to(ok[:, None], (2, 8, B)).reshape(16, B).astype(F32).astype(BF16), earlier())
     found = jnp.where(ok > 0, jnp.concatenate([order[0:1], order[8:9]], axis=0), ABSENT)
     ranks[...] = found[0:1, :]
-    words[...] = jnp.broadcast_to(word[...], (128, B)).reshape(128, 1, B)
+    both = jnp.where(
+        first == (lax.broadcasted_iota(jnp.int32, (2, B), 0) == 0), word[...], word_other[...]
+    )
+    words[...] = jnp.broadcast_to(both[None], (8, 2, B))
     packed = []
     for i, block in enumerate((img, img_other)):
         pick = jnp.where(iota((B, B), 0) == found[i:i + 1, :], 1.0, 0.0).astype(BF16)
@@ -128,6 +131,10 @@
     carried[B:2 * B, :] = jnp.where(first, cap_other[...], packed[0])
     kept[0:B, :] = jnp.where(first, packed[0], cap_other[...])
     kept[B:2 * B, :] = jnp.where(first, packed[1], cap[...])
+
+
+def table_row(p):
+    return ((p["z"] * 2 + p["l"]) * 8 + p["x"] * 2 + p["h"]) * 2 + p["c"]
 
 
 def lookup_kernel(table, ranks, columns, counts, real, pos, words_v):
@@ -139,12 +146,14 @@
     real[...] = jnp.full((8, 128), jnp.sum(ok), F32)
     known = jnp.transpose(jnp.where(ok > 0, rank + 1.0, 0.0)).astype(BF16)
     for k in range(CAPS):
-        row = words_v[pl.ds(flat(cap_place(p, k)), 1), :]
+        row = words_v[pl.ds(table_row(cap_place(p, k)), 1), :]
         pos[k:k + 1, :] = (row & ((1 << OK_BIT) - 1)).astype(F32)
     at = pos[...]
     hi = jnp.floor((at + 0.5) * (1.0 / B))
     lo = at - hi * B
-    block = iota((128, B), 0)
+    line = lax.broadcasted_iota(jnp.int32, (128, B), 0)
+    bits = lambda low, mask: lax.shift_right_logical(line, low) & mask
+    block = (bits(1, 7) * 16 + bits(5, 3) * 4 + bits(0, 1) * 2 + bits(4, 1)).astype(F32)
     inner = iota((B, B), 0)
     for k in range(CAPS):
         pick = jnp.where(block == hi[k:k + 1, :], 1.0, 0.0).astype(BF16)
@@ -164,7 +173,7 @@
     )
     for m in range(IMGS):
         number = flat(img_place(p, m))
-        row = words_v[pl.ds(number, 1), :]
+        row = words_v[pl.ds(table_row(img_place(p, m)), 1), :]
         row = lax.shift_right_logical(row, OK_BIT) & 1
         count = jnp.sum(row.astype(F32), axis=1, keepdims=True)
         base = jnp.where(hi == number.astype(F32), start, base)
@@ -222,13 +231,15 @@
     t_v, pos_b, bias_b, rmax, rmatch, rsum, col_bias, cmax, cmatch, csum, lines_v,
 ):
     img_at = starts_of(counts, CAPS, IMGS)
-    column = iota((8, C), 1)
-    bias = jnp.full((8, C), LOW, F32)
+    col_bias[...] = jnp.full((8, C + 384), LOW, F32)
+    column = iota((8, 384), 1)
     for m in range(IMGS):
-        begin = img_at[m].astype(F32)
+        whole = lax.shift_left(lax.shift_right_logical(img_at[m], 7), 7)
+        span = pl.ds(pl.multiple_of(whole, 128), 384)
+        begin = (img_at[m] - whole).astype(F32)
         end = begin + counts[CAPS + m, 0].astype(F32)
-        bias = jnp.where((column >= begin) & (column < end), 0.0, bias)
-    col_bias[...] = bias
+        inside = (column >= begin) & (column < end)
+        col_bias[:, span] = jnp.where(inside, 0.0, col_bias[:, span])
     cap_at = starts_of(counts, 0, CAPS)
     slot = iota((B, 128), 0)
     for k in range(CAPS):
@@ -377,7 +388,7 @@
     others = [send(value, other_core) for value in (captions, images, word)]
     carried, kept, words, image_ranks = pl.pallas_call(
         pair_kernel,
-        out_shape=[pair, pair, shape((128, 1, B), jnp.int32), shape((1, B), F32)],
+        out_shape=[pair, pair, shape((8, 2, B), jnp.int32), shape((1, B), F32)],
         in_specs=[VMEM] * 6,
         out_specs=[VMEM] * 4,
         **small(8, 10**8),
@@ -389,7 +400,9 @@
     met = dict(y=near, a1=a1, a3=a3, b1=b1, b3=b3, c1=c1, c3=c3)
     swapped = [kept] + [send(v, other_core) for v in met.values()]
     carried = [carried, *met.values()]
-    table = lax.all_to_all(words, AXES, 0, 0, tiled=True)
+    part = lax.all_to_all(words, ("x", "h"), 0, 0, tiled=True)
+    part = jnp.broadcast_to(part.reshape(1, 16, B), (8, 16, B))
+    table = lax.all_to_all(part, ("z", "l"), 0, 0, tiled=True)
     ranks, columns, counts, real = pl.pallas_call(
         lookup_kernel,
         out_shape=[
@@ -420,7 +433,8 @@
         scratch_shapes=[
             pltpu.VMEM((R, C), F32),
             *[pltpu.VMEM((R + RC, 128), F32)] * 5,
-            *[pltpu.VMEM((8, C), F32)] * 4,
+            pltpu.VMEM((8, C + 384), F32),
+            *[pltpu.VMEM((8, C), F32)] * 3,
             pltpu.VMEM((8, C + 384), F32),
         ],
         compiler_params=pltpu.CompilerParams(vmem_limit_bytes=31 * 1024 * 1024),

time: 104 us -> 115 us (1.11)
  local copies, waits for them, and re-layouts: 1.92 us -> 9.81 us
  blocking collectives: 48.9 us -> 54.5 us
  waiting for transfers between devices: 16.7 us -> 12.7 us
    unnamed x4 -> x28, local copies, waits for them, and re-layouts: 1.92 us -> 7.75 us
    all_to_all x1 -> x2, blocking collectives: 20.3 us -> 26.1 us  [the longest x1 14.5 us: step(): part = lax.all_to_all(words, ('x', 'h'), 0, 0, tiled=True)]
    ppermute x17, waiting for transfers between devices: 16.7 us -> 12.7 us  [send(): return lax.ppermute(value, AXES, pairs)]
    broadcast_in_dim x0 -> x2, local copies, waits for them, and re-layouts: none -> 2.05 us  [step(): part = jnp.broadcast_to(part.reshape(1, 16, B), (8, 16, B))]
  transfers between devices with their start and end apart: 17 -> 17, of which waited for: 5 -> 5; matrix products, arithmetic and copies ran while one was open for 1% -> 2% of each run, Pallas kernels for 4% -> 4%
where the time goes in v3:
time: 115 us; the launch traced here: 113 us
  blocking collectives  54.5 us (47%)
  starting transfers between devices  17.5 us (15%)
  Pallas kernels  16.6 us (14%)
  waiting for transfers between devices  12.7 us (11%)
  local copies, waits for them, and re-layouts  9.81 us (9%)
  other arithmetic  1.43 us (1%)
    ppermute x17, starting transfers between devices, send(): return lax.ppermute(value, AXES, pairs)  17.5 us
    all_to_all x1, blocking collectives, step(): parts = lax.all_to_all(out, AXES, 0, 0, tiled=True)  14.6 us
    all_to_all x1, blocking collectives, step(): part = lax.all_to_all(words, ('x', 'h'), 0, 0, tiled=True)  14.5 us
    all_to_all x1, blocking collectives, step(): totals = lax.all_to_all(total, AXES, 0, 0, tiled=True)  13.9 us
    ppermute x17, waiting for transfers between devices, send(): return lax.ppermute(value, AXES, pairs)  12.7 us
    all_to_all x1, blocking collectives, step(): table = lax.all_to_all(part, ('z', 'l'), 0, 0, tiled=True)  11.6 us
    pallas_call x1, Pallas kernels, step(): pl.pallas_call(score_kernel, out_shape=[shape((n, 1, 2 * B), F32) for n i...  9.2 us
    unnamed x28, local copies, waits for them, and re-layouts  7.75 us
  transfers between devices with their start and end apart: 17, of which 5 were waited for; matrix products, arithmetic and copies ran while one was open for 2% of the time, Pallas kernels for 4%

profile of v3, /device:TPU:0, one launch (start us, length us, event | category | flops | bytes accessed | tf_op | source)
XLA Modules:
  0.0 113.3 jit_solution(9922940365239476063)
XLA Ops:
  1.2 0.7 multiply_add_fusion
  2.0 1.1 collective-permute-done.2.word_other
  3.1 1.0 copy-done.12
  4.1 1.0 copy-done.13
  5.5 0.8 copy-done.2
  6.3 1.7 %collective-permute-start.3 = (bf16[384,768]{1,0:T(8,128)(2,1)S(1)}, bf16[384,768]{1,0:T(8,128)(2,1)S(1)}, u32[]{:S(2)}, u32[]{:S(2)}) collective-permute-start(bf16[384,768]{1,0:T(8,128)(2,1)S(1)} %get-tuple-element.26.refs_0_), channel_id=1, source_target_pairs={{0,1},{1,0},{2,19},{3,18},{4,5},{5,4},{6,23},{7,22},{8,9},{9,8},{1... | collective-permute-start | bytes 1769480 | tf_op jit(solution)/shard_map/ppermute | solution.py:49
  8.0 1.9 %collective-permute-start.4 = (bf16[384,768]{1,0:T(8,128)(2,1)S(1)}, bf16[384,768]{1,0:T(8,128)(2,1)S(1)}, u32[]{:S(2)}, u32[]{:S(2)}) collective-permute-start(bf16[384,768]{1,0:T(8,128)(2,1)S(1)} %get-tuple-element.26.refs_0_), channel_id=1, source_target_pairs={{0,4},{1,5},{2,34},{3,35},{4,8},{5,9},{6,38},{7,39},{8,12},{9,13},... | collective-permute-start | bytes 1769480 | tf_op jit(solution)/shard_map/ppermute | solution.py:49
  9.9 2.1 %collective-permute-start.5 = (bf16[384,768]{1,0:T(8,128)(2,1)S(1)}, bf16[384,768]{1,0:T(8,128)(2,1)}, u32[]{:S(2)}, u32[]{:S(2)}) collective-permute-start(bf16[384,768]{1,0:T(8,128)(2,1)S(1)} %get-tuple-element.26.refs_0_), channel_id=1, source_target_pairs={{0,12},{1,13},{2,98},{3,99},{4,0},{5,1},{6,102},{7,103},{8,4},{9,5... | collective-permute-start | bytes 1769480 | tf_op jit(solution)/shard_map/ppermute | solution.py:49
  12.1 0.8 copy-done
  12.9 3.3 %collective-permute-done.3.refs_1_ = bf16[384,768]{1,0:T(8,128)(2,1)S(1)} collective-permute-done((bf16[384,768]{1,0:T(8,128)(2,1)S(1)}, bf16[384,768]{1,0:T(8,128)(2,1)S(1)}, u32[]{:S(2)}, u32[]{:S(2)}) %collective-permute-start.3) | collective-permute-done | bytes 589856 | tf_op jit(solution)/shard_map/ppermute | solution.py:49
  16.2 4.1 %collective-permute-start.10 = (bf16[384,768]{1,0:T(8,128)(2,1)S(1)}, bf16[384,768]{1,0:T(8,128)(2,1)S(1)}, u32[]{:S(2)}, u32[]{:S(2)}) collective-permute-start(bf16[384,768]{1,0:T(8,128)(2,1)S(1)} %collective-permute-done.3.refs_1_), channel_id=1, source_target_pairs={{0,12},{1,13},{2,98},{3,99},{4,0},{5,1},{6,102},{7,103},{8,4},{9,5... | collective-permute-start | bytes 1769480 | tf_op jit(solution)/shard_map/ppermute | solution.py:49
  21.2 0.8 copy-done.4
  22.0 1.9 %collective-permute-start.13 = (bf16[384,768]{1,0:T(8,128)(2,1)S(1)}, bf16[384,768]{1,0:T(8,128)(2,1)S(1)}, u32[]{:S(2)}, u32[]{:S(2)}) collective-permute-start(bf16[384,768]{1,0:T(8,128)(2,1)S(1)} %collective-permute-done.4.refs_2_), channel_id=1, source_target_pairs={{0,4},{1,5},{2,34},{3,35},{4,8},{5,9},{6,38},{7,39},{8,12},{9,13},... | collective-permute-start | bytes 1769480 | tf_op jit(solution)/shard_map/ppermute | solution.py:49
  23.9 0.8 copy-done.6
  24.7 3.0 %collective-permute-done.10.refs_3_ = bf16[384,768]{1,0:T(8,128)(2,1)S(1)} collective-permute-done((bf16[384,768]{1,0:T(8,128)(2,1)S(1)}, bf16[384,768]{1,0:T(8,128)(2,1)S(1)}, u32[]{:S(2)}, u32[]{:S(2)}) %collective-permute-start.10) | collective-permute-done | bytes 589856 | tf_op jit(solution)/shard_map/ppermute | solution.py:49
  27.8 3.7 %collective-permute-start.14 = (bf16[384,768]{1,0:T(8,128)(2,1)S(1)}, bf16[384,768]{1,0:T(8,128)(2,1)S(1)}, u32[]{:S(2)}, u32[]{:S(2)}) collective-permute-start(bf16[384,768]{1,0:T(8,128)(2,1)S(1)} %collective-permute-done.10.refs_3_), channel_id=1, source_target_pairs={{0,12},{1,13},{2,98},{3,99},{4,0},{5,1},{6,102},{7,103},{8,4},{9,5... | collective-permute-start | bytes 1769480 | tf_op jit(solution)/shard_map/ppermute | solution.py:49
  31.5 0.8 copy-done.8
  32.3 0.8 copy-done.10
  33.6 4.7 %collective-permute-done.13.refs_2_ = bf16[384,768]{1,0:T(8,128)(2,1)S(1)} collective-permute-done((bf16[384,768]{1,0:T(8,128)(2,1)S(1)}, bf16[384,768]{1,0:T(8,128)(2,1)S(1)}, u32[]{:S(2)}, u32[]{:S(2)}) %collective-permute-start.13) | collective-permute-done | bytes 589856 | tf_op jit(solution)/shard_map/ppermute | solution.py:49
  38.9 14.5 %all_to_all.20 = s32[8,2,192]{2,1,0:T(2,128)} all-to-all(s32[8,2,192]{2,1,0:T(2,128)S(1)} %get-tuple-element.22), channel_id=1, replica_groups=mesh['x'=4,'h'=2,'z'=4,'c'=2,'l'=2] {'x','h'}, dimensions={0} | all-to-all | bytes 24576 | tf_op jit(solution)/shard_map/all_to_all | solution.py:403
  53.4 1.3 %broadcast_in_dim.11 = s32[16,192]{1,0:T(8,128)} reshape(s32[8,2,192]{2,1,0:T(2,128)} %all_to_all.20) | data formatting | bytes 24576 | tf_op jit(solution)/shard_map/broadcast_in_dim | solution.py:404
  54.7 0.7 broadcast_in_dim.12
  55.4 11.6 %all_to_all.21.table = s32[8,16,192]{2,1,0:T(8,128)S(1)} all-to-all(s32[8,16,192]{2,1,0:T(8,128)S(1)} %broadcast_in_dim.12), channel_id=1, replica_groups=mesh['x'=4,'h'=2,'z'=4,'c'=2,'l'=2] {'z','l'}, dimensions={0} | all-to-all | bytes 196608 | tf_op jit(solution)/shard_map/all_to_all | solution.py:405
  67.0 1.0 shard_map.68
  69.0 1.9 %shard_map.69 = (bf16[1984,768]{1,0:T(8,128)(2,1)S(1)}, bf16[3584,768]{1,0:T(8,128)(2,1)S(1)}) custom-call(s32[24,128]{1,0:T(8,128)S(1)} %get-tuple-element.23.counts, f32[8,192]{1,0:T(8,128)S(1)} %get-tuple-element.25.ranks.row_ranks, bf16[384,768]{1,0:T(8,128)(2,1)S(1)} %copy-done.1, bf16[384,768]{1,0:T(8,128)(2,1)S(1)} %copy-done.5, ...), custom_call_target="tpu_custom_call" | custom-call | flops 1000000000 | bytes 1000000 | tf_op jit(solution)/shard_map/pallas_call | solution.py:419
  70.9 1.5 %shard_map.70 = (bf16[1984,768]{1,0:T(8,128)(2,1)S(1)}, bf16[3584,768]{1,0:T(8,128)(2,1)S(1)}) custom-call(s32[24,128]{1,0:T(8,128)S(1)} %get-tuple-element.23.counts, f32[8,192]{1,0:T(8,128)S(1)} %get-tuple-element.25.ranks.row_ranks, bf16[1984,768]{1,0:T(8,128)(2,1)S(1)} %get-tuple-element.28.refs_0_, ...), custom_call_target="tpu_custom_call", output_to_operand_aliasing={{0}: (2, {}), {1}: (3, {})} | custom-call | flops 1000000000 | bytes 1000000 | tf_op jit(solution)/shard_map/pallas_call | solution.py:419
  72.4 1.6 %shard_map.71 = (bf16[1984,768]{1,0:T(8,128)(2,1)S(1)}, bf16[3584,768]{1,0:T(8,128)(2,1)S(1)}) custom-call(s32[24,128]{1,0:T(8,128)S(1)} %get-tuple-element.23.counts, f32[8,192]{1,0:T(8,128)S(1)} %get-tuple-element.25.ranks.row_ranks, bf16[1984,768]{1,0:T(8,128)(2,1)S(1)} %get-tuple-element.30.refs_0_, ...), custom_call_target="tpu_custom_call", output_to_operand_aliasing={{0}: (2, {}), {1}: (3, {})} | custom-call | flops 1000000000 | bytes 1000000 | tf_op jit(solution)/shard_map/pallas_call | solution.py:419
  74.0 9.2 %shard_map.72 = (f32[128,1,384]{2,1,0:T(1,128)S(1)}, f32[1,1,384]{2,1,0:T(1,128)S(1)}) custom-call(s32[24,128]{1,0:T(8,128)S(1)} %get-tuple-element.23.counts, f32[192,128]{1,0:T(8,128)S(1)} %get-tuple-element.24.columns, bf16[1984,768]{1,0:T(8,128)(2,1)S(1)} %get-tuple-element.32.cap_v, bf16[3584,768]{1,0:T(8,128)(2,1)S(1)} %get-tuple-element.33.img_v), custom_call_target="tpu_custom_call" | custom-call | flops 4227858432 | bytes 7471104 | tf_op jit(solution)/shard_map/pallas_call | solution.py:428
  83.2 14.6 %all_to_all.22.parts = f32[128,1,384]{2,1,0:T(1,128)S(1)} all-to-all(f32[128,1,384]{2,1,0:T(1,128)S(1)} %get-tuple-element.34), channel_id=1, replica_groups=mesh['x'=4,'h'=2,'z'=4,'c'=2,'l'=2] {'x','h','z','c','l'}, dimensions={0} | all-to-all | bytes 393216 | tf_op jit(solution)/shard_map/all_to_all | solution.py:445
  97.8 0.9 shard_map.73
  98.7 13.9 %all_to_all.23 = f32[128,1,8]{2,1,0:T(1,128)S(1)} all-to-all(f32[128,1,8]{2,1,0:T(1,128)S(1)} %get-tuple-element.40), channel_id=1, replica_groups=mesh['x'=4,'h'=2,'z'=4,'c'=2,'l'=2] {'x','h','z','c','l'}, dimensions={0} | all-to-all | bytes 8192 | tf_op jit(solution)/shard_map/all_to_all | solution.py:454
  112.6 0.7 slice_reduce_fusion
  (45 shorter events, 4.0 us)
Async XLA Ops:
  0.6 2.5 %collective-permute-start = (bf16[192,768]{1,0:T(8,128)(2,1)}, bf16[192,768]{1,0:T(8,128)(2,1)S(1)}, u32[]{:S(2)}, u32[]{:S(2)}) collective-permute-start(bf16[192,768]{1,0:T(8,128)(2,1)} %cap.1), channel_id=1, source_target_pairs={{0,2},{1,3},{2,0},{3,1},{4,6},{5,7},{6,4},{7,5},{8,10},{9,11},{10,... | collective-permute-start | bytes 884744 | tf_op jit(solution)/shard_map/ppermute | solution.py:49
  0.7 2.4 %collective-permute-start.1 = (bf16[192,768]{1,0:T(8,128)(2,1)}, bf16[192,768]{1,0:T(8,128)(2,1)S(1)}, u32[]{:S(2)}, u32[]{:S(2)}) collective-permute-start(bf16[192,768]{1,0:T(8,128)(2,1)} %img.1), channel_id=1, source_target_pairs={{0,2},{1,3},{2,0},{3,1},{4,6},{5,7},{6,4},{7,5},{8,10},{9,11},{10,... | collective-permute-start | bytes 884744 | tf_op jit(solution)/shard_map/ppermute | solution.py:49
  1.9 1.2 %collective-permute-start.2 = (s32[1,192]{1,0:T(1,128)S(1)}, s32[1,192]{1,0:T(1,128)S(1)}, u32[]{:S(2)}, u32[]{:S(2)}) collective-permute-start(s32[1,192]{1,0:T(1,128)S(1)} %bitcast.3), channel_id=1, source_target_pairs={{0,2},{1,3},{2,0},{3,1},{4,6},{5,7},{6,4},{7,5},{8,10},{9,11},{10,... | collective-permute-start | bytes 2312 | tf_op jit(solution)/shard_map/ppermute | solution.py:49
  3.1 1.0 copy-start.12
  4.1 1.0 copy-start.13
  5.5 0.8 copy-start.2
  6.3 9.9 %collective-permute-start.3 = (bf16[384,768]{1,0:T(8,128)(2,1)S(1)}, bf16[384,768]{1,0:T(8,128)(2,1)S(1)}, u32[]{:S(2)}, u32[]{:S(2)}) collective-permute-start(bf16[384,768]{1,0:T(8,128)(2,1)S(1)} %get-tuple-element.26.refs_0_), channel_id=1, source_target_pairs={{0,1},{1,0},{2,19},{3,18},{4,5},{5,4},{6,23},{7,22},{8,9},{9,8},{1... | collective-permute-start | bytes 1769480 | tf_op jit(solution)/shard_map/ppermute | solution.py:49
  8.0 12.4 %collective-permute-start.4 = (bf16[384,768]{1,0:T(8,128)(2,1)S(1)}, bf16[384,768]{1,0:T(8,128)(2,1)S(1)}, u32[]{:S(2)}, u32[]{:S(2)}) collective-permute-start(bf16[384,768]{1,0:T(8,128)(2,1)S(1)} %get-tuple-element.26.refs_0_), channel_id=1, source_target_pairs={{0,4},{1,5},{2,34},{3,35},{4,8},{5,9},{6,38},{7,39},{8,12},{9,13},... | collective-permute-start | bytes 1769480 | tf_op jit(solution)/shard_map/ppermute | solution.py:49
  9.9 12.1 %collective-permute-start.5 = (bf16[384,768]{1,0:T(8,128)(2,1)S(1)}, bf16[384,768]{1,0:T(8,128)(2,1)}, u32[]{:S(2)}, u32[]{:S(2)}) collective-permute-start(bf16[384,768]{1,0:T(8,128)(2,1)S(1)} %get-tuple-element.26.refs_0_), channel_id=1, source_target_pairs={{0,12},{1,13},{2,98},{3,99},{4,0},{5,1},{6,102},{7,103},{8,4},{9,5... | collective-permute-start | bytes 1769480 | tf_op jit(solution)/shard_map/ppermute | solution.py:49
  12.0 0.8 copy-start
  16.2 11.6 %collective-permute-start.10 = (bf16[384,768]{1,0:T(8,128)(2,1)S(1)}, bf16[384,768]{1,0:T(8,128)(2,1)S(1)}, u32[]{:S(2)}, u32[]{:S(2)}) collective-permute-start(bf16[384,768]{1,0:T(8,128)(2,1)S(1)} %collective-permute-done.3.refs_1_), channel_id=1, source_target_pairs={{0,12},{1,13},{2,98},{3,99},{4,0},{5,1},{6,102},{7,103},{8,4},{9,5... | collective-permute-start | bytes 1769480 | tf_op jit(solution)/shard_map/ppermute | solution.py:49
  20.4 11.1 %collective-permute-start.6 = (bf16[384,768]{1,0:T(8,128)(2,1)S(1)}, bf16[384,768]{1,0:T(8,128)(2,1)S(1)}, u32[]{:S(2)}, u32[]{:S(2)}) collective-permute-start(bf16[384,768]{1,0:T(8,128)(2,1)S(1)} %collective-permute-done.3.refs_1_), channel_id=1, source_target_pairs={{0,2},{1,3},{2,0},{3,1},{4,6},{5,7},{6,4},{7,5},{8,10},{9,11},{10,... | collective-permute-start | bytes 1769480 | tf_op jit(solution)/shard_map/ppermute | solution.py:49
  20.4 11.9 %collective-permute-start.7 = (bf16[384,768]{1,0:T(8,128)(2,1)S(1)}, bf16[384,768]{1,0:T(8,128)(2,1)S(1)}, u32[]{:S(2)}, u32[]{:S(2)}) collective-permute-start(bf16[384,768]{1,0:T(8,128)(2,1)S(1)} %collective-permute-done.4.refs_2_), channel_id=1, source_target_pairs={{0,2},{1,3},{2,0},{3,1},{4,6},{5,7},{6,4},{7,5},{8,10},{9,11},{10,... | collective-permute-start | bytes 1769480 | tf_op jit(solution)/shard_map/ppermute | solution.py:49
  20.9 12.7 %collective-permute-start.9 = (bf16[384,768]{1,0:T(8,128)(2,1)S(1)}, bf16[384,768]{1,0:T(8,128)(2,1)S(1)}, u32[]{:S(2)}, u32[]{:S(2)}) collective-permute-start(bf16[384,768]{1,0:T(8,128)(2,1)S(1)} %collective-permute-done.3.refs_1_), channel_id=1, source_target_pairs={{0,4},{1,5},{2,34},{3,35},{4,8},{5,9},{6,38},{7,39},{8,12},{9,13},... | collective-permute-start | bytes 1769480 | tf_op jit(solution)/shard_map/ppermute | solution.py:49
  21.2 0.8 copy-start.4
  22.0 16.3 %collective-permute-start.13 = (bf16[384,768]{1,0:T(8,128)(2,1)S(1)}, bf16[384,768]{1,0:T(8,128)(2,1)S(1)}, u32[]{:S(2)}, u32[]{:S(2)}) collective-permute-start(bf16[384,768]{1,0:T(8,128)(2,1)S(1)} %collective-permute-done.4.refs_2_), channel_id=1, source_target_pairs={{0,4},{1,5},{2,34},{3,35},{4,8},{5,9},{6,38},{7,39},{8,12},{9,13},... | collective-permute-start | bytes 1769480 | tf_op jit(solution)/shard_map/ppermute | solution.py:49
  23.9 0.8 copy-start.6
  27.8 11.1 %collective-permute-start.14 = (bf16[384,768]{1,0:T(8,128)(2,1)S(1)}, bf16[384,768]{1,0:T(8,128)(2,1)S(1)}, u32[]{:S(2)}, u32[]{:S(2)}) collective-permute-start(bf16[384,768]{1,0:T(8,128)(2,1)S(1)} %collective-permute-done.10.refs_3_), channel_id=1, source_target_pairs={{0,12},{1,13},{2,98},{3,99},{4,0},{5,1},{6,102},{7,103},{8,4},{9,5... | collective-permute-start | bytes 1769480 | tf_op jit(solution)/shard_map/ppermute | solution.py:49
  31.5 0.8 copy-start.8
  32.3 35.8 %collective-permute-start.8 = (bf16[384,768]{1,0:T(8,128)(2,1)}, bf16[384,768]{1,0:T(8,128)(2,1)}, u32[]{:S(2)}, u32[]{:S(2)}) collective-permute-start(bf16[384,768]{1,0:T(8,128)(2,1)} %collective-permute-done.5.refs_3_), channel_id=1, source_target_pairs={{0,2},{1,3},{2,0},{3,1},{4,6},{5,7},{6,4},{7,5},{8,10},{9,11},{10,... | collective-permute-start | bytes 1769480 | tf_op jit(solution)/shard_map/ppermute | solution.py:49
  32.3 0.8 copy-start.10
  33.1 37.8 %collective-permute-start.12 = (bf16[384,768]{1,0:T(8,128)(2,1)S(1)}, bf16[384,768]{1,0:T(8,128)(2,1)S(1)}, u32[]{:S(2)}, u32[]{:S(2)}) collective-permute-start(bf16[384,768]{1,0:T(8,128)(2,1)S(1)} %collective-permute-done.10.refs_3_), channel_id=1, source_target_pairs={{0,2},{1,3},{2,0},{3,1},{4,6},{5,7},{6,4},{7,5},{8,10},{9,11},{10,... | collective-permute-start | bytes 1769480 | tf_op jit(solution)/shard_map/ppermute | solution.py:49
  33.6 37.3 %collective-permute-start.11 = (bf16[384,768]{1,0:T(8,128)(2,1)S(1)}, bf16[384,768]{1,0:T(8,128)(2,1)}, u32[]{:S(2)}, u32[]{:S(2)}) collective-permute-start(bf16[384,768]{1,0:T(8,128)(2,1)S(1)} %collective-permute-done.9.refs_2_), channel_id=1, source_target_pairs={{0,2},{1,3},{2,0},{3,1},{4,6},{5,7},{6,4},{7,5},{8,10},{9,11},{10,... | collective-permute-start | bytes 1769480 | tf_op jit(solution)/shard_map/ppermute | solution.py:49
  38.3 34.1 %collective-permute-start.15 = (bf16[384,768]{1,0:T(8,128)(2,1)S(1)}, bf16[384,768]{1,0:T(8,128)(2,1)S(1)}, u32[]{:S(2)}, u32[]{:S(2)}) collective-permute-start(bf16[384,768]{1,0:T(8,128)(2,1)S(1)} %collective-permute-done.13.refs_2_), channel_id=1, source_target_pairs={{0,2},{1,3},{2,0},{3,1},{4,6},{5,7},{6,4},{7,5},{8,10},{9,11},{10,... | collective-permute-start | bytes 1769480 | tf_op jit(solution)/shard_map/ppermute | solution.py:49
  38.8 33.6 %collective-permute-start.16 = (bf16[384,768]{1,0:T(8,128)(2,1)S(1)}, bf16[384,768]{1,0:T(8,128)(2,1)}, u32[]{:S(2)}, u32[]{:S(2)}) collective-permute-start(bf16[384,768]{1,0:T(8,128)(2,1)S(1)} %collective-permute-done.14.refs_3_), channel_id=1, source_target_pairs={{0,2},{1,3},{2,0},{3,1},{4,6},{5,7},{6,4},{7,5},{8,10},{9,11},{10,... | collective-permute-start | bytes 1769480 | tf_op jit(solution)/shard_map/ppermute | solution.py:49
  67.0 1.1 copy-start.1
  67.0 1.2 %copy-start.3 = (bf16[384,768]{1,0:T(8,128)(2,1)S(1)}, bf16[384,768]{1,0:T(8,128)(2,1)}, u32[]{:S(2)}) copy-start(bf16[384,768]{1,0:T(8,128)(2,1)} %copy-done.2) | copy-start | bytes 1769476
  67.0 1.4 %copy-start.5 = (bf16[384,768]{1,0:T(8,128)(2,1)S(1)}, bf16[384,768]{1,0:T(8,128)(2,1)}, u32[]{:S(2)}) copy-start(bf16[384,768]{1,0:T(8,128)(2,1)} %copy-done.4) | copy-start | bytes 1769476
  67.0 1.6 %copy-start.7 = (bf16[384,768]{1,0:T(8,128)(2,1)S(1)}, bf16[384,768]{1,0:T(8,128)(2,1)}, u32[]{:S(2)}) copy-start(bf16[384,768]{1,0:T(8,128)(2,1)} %copy-done.6) | copy-start | bytes 1769476
  67.0 1.8 %copy-start.9 = (bf16[384,768]{1,0:T(8,128)(2,1)S(1)}, bf16[384,768]{1,0:T(8,128)(2,1)}, u32[]{:S(2)}) copy-start(bf16[384,768]{1,0:T(8,128)(2,1)} %copy-done.8) | copy-start | bytes 1769476
  67.0 1.9 %copy-start.11 = (bf16[384,768]{1,0:T(8,128)(2,1)S(1)}, bf16[384,768]{1,0:T(8,128)(2,1)}, u32[]{:S(2)}) copy-start(bf16[384,768]{1,0:T(8,128)(2,1)} %copy-done.10) | copy-start | bytes 1769476

commit v4 on v3

--- a/solution.py
+++ b/solution.py
@@ -19,7 +19,7 @@
 B = 192
 E = 768
 MET = ((0, 0), (0, 1), (3, 0), (1, 0), (3, 1), (1, 1), (2, 0), (2, 1))
-PARTS = ((0, 4), (4, 6), (6, 8))
+PARTS = ((0, 6), (6, 8))
 CAPS = len(MET)
 IMGS = 2 * len(MET)
 C = IMGS * B
@@ -109,14 +109,13 @@
     return lax.shift_left(lax.shift_right_logical(n + (GRAIN - 1), 4), 4)
 
 
-def pair_kernel(
-    cap, img, word, cap_other, img_other, word_other, carried, kept, words, ranks
-):
+def pair_kernel(own, cap_other, img_other, word, word_other, carried, words, ranks):
     first = lax.axis_index("c") == 0
     ok = lax.shift_right_logical(
         jnp.concatenate([word[...], word_other[...]], axis=0), OK_BIT
     )
-    order = dot(jnp.broadcast_to(ok[:, None], (2, 8, B)).reshape(16, B).astype(F32).astype(BF16), earlier())
+    marks = jnp.broadcast_to(ok[:, None], (2, 8, B)).reshape(16, B).astype(F32).astype(BF16)
+    order = dot(marks, earlier())
     found = jnp.where(ok > 0, jnp.concatenate([order[0:1], order[8:9]], axis=0), ABSENT)
     ranks[...] = found[0:1, :]
     both = jnp.where(
@@ -124,13 +123,11 @@
     )
     words[...] = jnp.broadcast_to(both[None], (8, 2, B))
     packed = []
-    for i, block in enumerate((img, img_other)):
+    for i, block in enumerate((own, img_other)):
         pick = jnp.where(iota((B, B), 0) == found[i:i + 1, :], 1.0, 0.0).astype(BF16)
         packed.append(dot(pick, block[...]).astype(BF16))
-    carried[0:B, :] = jnp.where(first, cap[...], packed[1])
+    carried[0:B, :] = jnp.where(first, own[...], packed[1])
     carried[B:2 * B, :] = jnp.where(first, cap_other[...], packed[0])
-    kept[0:B, :] = jnp.where(first, packed[0], cap_other[...])
-    kept[B:2 * B, :] = jnp.where(first, packed[1], cap[...])
 
 
 def table_row(p):
@@ -386,20 +383,21 @@
     pair = shape((2 * B, E), BF16)
     word = (positives + valid * (1 << OK_BIT))[None]
     others = [send(value, other_core) for value in (captions, images, word)]
-    carried, kept, words, image_ranks = pl.pallas_call(
+    own = jnp.where(lax.axis_index("c") == 0, captions, images)
+    carried, words, image_ranks = pl.pallas_call(
         pair_kernel,
-        out_shape=[pair, pair, shape((8, 2, B), jnp.int32), shape((1, B), F32)],
-        in_specs=[VMEM] * 6,
-        out_specs=[VMEM] * 4,
+        out_shape=[pair, shape((8, 2, B), jnp.int32), shape((1, B), F32)],
+        in_specs=[VMEM] * 5,
+        out_specs=[VMEM] * 3,
         **small(8, 10**8),
-    )(captions, images, word, *others)
+    )(own, others[0], others[1], word, others[2])
     near = send(carried, partner)
     a1, a3 = (send(carried, along(s)) for s in (1, 3))
     b1, b3 = (send(near, along(s)) for s in (1, 3))
     c1, c3 = send(a1, along(1)), send(b3, along(3))
-    met = dict(y=near, a1=a1, a3=a3, b1=b1, b3=b3, c1=c1, c3=c3)
-    swapped = [kept] + [send(v, other_core) for v in met.values()]
-    carried = [carried, *met.values()]
+    met = dict(own=carried, y=near, a1=a1, a3=a3, b1=b1, b3=b3, c1=c1, c3=c3)
+    swapped = [send(v, other_core) for v in met.values()]
+    carried = list(met.values())
     part = lax.all_to_all(words, ("x", "h"), 0, 0, tiled=True)
     part = jnp.broadcast_to(part.reshape(1, 16, B), (8, 16, B))
     table = lax.all_to_all(part, ("z", "l"), 0, 0, tiled=True)

time: 115 us -> 111 us (0.965)
  waiting for transfers between devices: 12.7 us -> 19.7 us
  local copies, waits for them, and re-layouts: 9.81 us -> 3.89 us
  blocking collectives: 54.5 us -> 51.8 us
  starting transfers between devices: 17.5 us -> 15.1 us
    ppermute x17 -> x18, waiting for transfers between devices: 12.7 us -> 19.7 us  [send(): return lax.ppermute(value, AXES, pairs)]
    unnamed x28 -> x8, local copies, waits for them, and re-layouts: 7.75 us -> 1.84 us
    all_to_all x1, blocking collectives: 11.6 us -> 9.14 us  [step(): table = lax.all_to_all(part, ('z', 'l'), 0, 0, tiled=True)]
    ppermute x17 -> x18, starting transfers between devices: 17.5 us -> 15.1 us  [send(): return lax.ppermute(value, AXES, pairs)]
    pallas_call x3 -> x2, Pallas kernels: 4.98 us -> 4.67 us  [step(): pl.pallas_call(functools.partial(compact_kernel, part), out_shape=[shape(...]
  transfers between devices with their start and end apart: 17 -> 18, of which waited for: 5 -> 6; matrix products, arithmetic and copies ran while one was open for 2% -> 3% of each run, Pallas kernels for 4% -> 3%
where the time goes in v4:
time: 111 us; the launch traced here: 110 us
  blocking collectives  51.8 us (47%)
  waiting for transfers between devices  19.7 us (18%)
  Pallas kernels  16.2 us (15%)
  starting transfers between devices  15.1 us (14%)
  local copies, waits for them, and re-layouts  3.89 us (4%)
  other arithmetic  2.43 us (2%)
    ppermute x18, waiting for transfers between devices, send(): return lax.ppermute(value, AXES, pairs)  19.7 us
    ppermute x18, starting transfers between devices, send(): return lax.ppermute(value, AXES, pairs)  15.1 us
    all_to_all x1, blocking collectives, step(): parts = lax.all_to_all(out, AXES, 0, 0, tiled=True)  14.6 us
    all_to_all x1, blocking collectives, step(): part = lax.all_to_all(words, ('x', 'h'), 0, 0, tiled=True)  14.2 us
    all_to_all x1, blocking collectives, step(): totals = lax.all_to_all(total, AXES, 0, 0, tiled=True)  13.9 us
    pallas_call x1, Pallas kernels, step(): pl.pallas_call(score_kernel, out_shape=[shape((n, 1, 2 * B), F32) for n i...  9.22 us
    all_to_all x1, blocking collectives, step(): table = lax.all_to_all(part, ('z', 'l'), 0, 0, tiled=True)  9.14 us
    pallas_call x2, Pallas kernels, step(): pl.pallas_call(functools.partial(compact_kernel, part), out_shape=[shape(...  4.67 us
  transfers between devices with their start and end apart: 18, of which 6 were waited for; matrix products, arithmetic and copies ran while one was open for 3% of the time, Pallas kernels for 3%

profile of v4, /device:TPU:0, one launch (start us, length us, event | category | flops | bytes accessed | tf_op | source)
XLA Modules:
  0.0 110.0 jit_solution(6921066812853698151)
XLA Ops:
  0.6 0.1 collective-permute-start
  0.7 0.5 collective-permute-start.1
  1.2 0.7 multiply_add_fusion
  1.9 0.1 collective-permute-start.2
  2.0 1.0 broadcast_select_fusion.own
  3.1 0.4 shard_map.67
  3.5 1.8 %collective-permute-start.3 = (bf16[384,768]{1,0:T(8,128)(2,1)S(1)}, bf16[384,768]{1,0:T(8,128)(2,1)S(1)}, u32[]{:S(2)}, u32[]{:S(2)}) collective-permute-start(bf16[384,768]{1,0:T(8,128)(2,1)S(1)} %get-tuple-element.23.refs_0_), channel_id=1, source_target_pairs={{0,1},{1,0},{2,19},{3,18},{4,5},{5,4},{6,23},{7,22},{8,9},{9,8},{1... | collective-permute-start | bytes 1769480 | tf_op jit(solution)/shard_map/ppermute | solution.py:49
  5.3 4.0 %collective-permute-start.5 = (bf16[384,768]{1,0:T(8,128)(2,1)S(1)}, bf16[384,768]{1,0:T(8,128)(2,1)S(1)}, u32[]{:S(2)}, u32[]{:S(2)}) collective-permute-start(bf16[384,768]{1,0:T(8,128)(2,1)S(1)} %get-tuple-element.23.refs_0_), channel_id=1, source_target_pairs={{0,12},{1,13},{2,98},{3,99},{4,0},{5,1},{6,102},{7,103},{8,4},{9,5... | collective-permute-start | bytes 1769480 | tf_op jit(solution)/shard_map/ppermute | solution.py:49
  9.4 4.1 %collective-permute-done.3.refs_1_ = bf16[384,768]{1,0:T(8,128)(2,1)S(1)} collective-permute-done((bf16[384,768]{1,0:T(8,128)(2,1)S(1)}, bf16[384,768]{1,0:T(8,128)(2,1)S(1)}, u32[]{:S(2)}, u32[]{:S(2)}) %collective-permute-start.3) | collective-permute-done | bytes 589856 | tf_op jit(solution)/shard_map/ppermute | solution.py:49
  13.5 4.2 %collective-permute-start.7 = (bf16[384,768]{1,0:T(8,128)(2,1)S(1)}, bf16[384,768]{1,0:T(8,128)(2,1)}, u32[]{:S(2)}, u32[]{:S(2)}) collective-permute-start(bf16[384,768]{1,0:T(8,128)(2,1)S(1)} %collective-permute-done.3.refs_1_), channel_id=1, source_target_pairs={{0,12},{1,13},{2,98},{3,99},{4,0},{5,1},{6,102},{7,103},{8,4},{9,5... | collective-permute-start | bytes 1769480 | tf_op jit(solution)/shard_map/ppermute | solution.py:49
  17.7 2.8 %collective-permute-done.4.refs_2_ = bf16[384,768]{1,0:T(8,128)(2,1)S(1)} collective-permute-done((bf16[384,768]{1,0:T(8,128)(2,1)S(1)}, bf16[384,768]{1,0:T(8,128)(2,1)S(1)}, u32[]{:S(2)}, u32[]{:S(2)}) %collective-permute-start.4) | collective-permute-done | bytes 589856 | tf_op jit(solution)/shard_map/ppermute | solution.py:49
  20.5 0.1 collective-permute-start.10
  20.6 4.5 %collective-permute-done.7.refs_5_ = bf16[384,768]{1,0:T(8,128)(2,1)} collective-permute-done((bf16[384,768]{1,0:T(8,128)(2,1)S(1)}, bf16[384,768]{1,0:T(8,128)(2,1)}, u32[]{:S(2)}, u32[]{:S(2)}) %collective-permute-start.7) | collective-permute-done | bytes 589856 | tf_op jit(solution)/shard_map/ppermute | solution.py:49
  25.1 3.8 %collective-permute-start.15 = (bf16[384,768]{1,0:T(8,128)(2,1)}, bf16[384,768]{1,0:T(8,128)(2,1)}, u32[]{:S(2)}, u32[]{:S(2)}) collective-permute-start(bf16[384,768]{1,0:T(8,128)(2,1)} %collective-permute-done.7.refs_5_), channel_id=1, source_target_pairs={{0,12},{1,13},{2,98},{3,99},{4,0},{5,1},{6,102},{7,103},{8,4},{9,5... | collective-permute-start | bytes 1769480 | tf_op jit(solution)/shard_map/ppermute | solution.py:49
  28.9 0.8 copy-done
  29.7 1.8 %collective-permute-done.14.refs_2_ = bf16[384,768]{1,0:T(8,128)(2,1)S(1)} collective-permute-done((bf16[384,768]{1,0:T(8,128)(2,1)S(1)}, bf16[384,768]{1,0:T(8,128)(2,1)S(1)}, u32[]{:S(2)}, u32[]{:S(2)}) %collective-permute-start.14) | collective-permute-done | bytes 589856 | tf_op jit(solution)/shard_map/ppermute | solution.py:49
  31.5 6.4 %collective-permute-done.6.refs_4_ = bf16[384,768]{1,0:T(8,128)(2,1)} collective-permute-done((bf16[384,768]{1,0:T(8,128)(2,1)S(1)}, bf16[384,768]{1,0:T(8,128)(2,1)}, u32[]{:S(2)}, u32[]{:S(2)}) %collective-permute-start.6) | collective-permute-done | bytes 589856 | tf_op jit(solution)/shard_map/ppermute | solution.py:49
  38.0 0.8 copy-done.2
  38.8 0.5 collective-permute-start.16
  39.3 14.2 %all_to_all.20 = s32[8,2,192]{2,1,0:T(2,128)} all-to-all(s32[8,2,192]{2,1,0:T(2,128)S(1)} %get-tuple-element.19), channel_id=1, replica_groups=mesh['x'=4,'h'=2,'z'=4,'c'=2,'l'=2] {'x','h'}, dimensions={0} | all-to-all | bytes 24576 | tf_op jit(solution)/shard_map/all_to_all | solution.py:401
  53.5 1.3 %broadcast_in_dim.11 = s32[16,192]{1,0:T(8,128)} reshape(s32[8,2,192]{2,1,0:T(2,128)} %all_to_all.20) | data formatting | bytes 24576 | tf_op jit(solution)/shard_map/broadcast_in_dim | solution.py:402
  54.9 0.7 broadcast_in_dim.12
  55.6 9.1 %all_to_all.21.table = s32[8,16,192]{2,1,0:T(8,128)S(1)} all-to-all(s32[8,16,192]{2,1,0:T(8,128)S(1)} %broadcast_in_dim.12), channel_id=1, replica_groups=mesh['x'=4,'h'=2,'z'=4,'c'=2,'l'=2] {'z','l'}, dimensions={0} | all-to-all | bytes 196608 | tf_op jit(solution)/shard_map/all_to_all | solution.py:403
  64.7 1.0 shard_map.68
  65.8 0.2 copy-done.3
  66.0 2.7 %shard_map.69 = (bf16[1984,768]{1,0:T(8,128)(2,1)S(1)}, bf16[3584,768]{1,0:T(8,128)(2,1)S(1)}) custom-call(s32[24,128]{1,0:T(8,128)S(1)} %get-tuple-element.20.counts, f32[8,192]{1,0:T(8,128)S(1)} %get-tuple-element.22.ranks.row_ranks, bf16[384,768]{1,0:T(8,128)(2,1)S(1)} %get-tuple-element.23.refs_0_, bf16[384,768]{1,0:T(8,128)(2,1)S(1)} %collective-permute-done.3.refs_1_, ...), custom_call_target="tpu_custom_call" | custom-call | flops 1000000000 | bytes 1000000 | tf_op jit(solution)/shard_map/pallas_call | solution.py:417
  68.7 1.9 %shard_map.70 = (bf16[1984,768]{1,0:T(8,128)(2,1)S(1)}, bf16[3584,768]{1,0:T(8,128)(2,1)S(1)}) custom-call(s32[24,128]{1,0:T(8,128)S(1)} %get-tuple-element.20.counts, f32[8,192]{1,0:T(8,128)S(1)} %get-tuple-element.22.ranks.row_ranks, bf16[1984,768]{1,0:T(8,128)(2,1)S(1)} %get-tuple-element.24.refs_0_, ...), custom_call_target="tpu_custom_call", output_to_operand_aliasing={{0}: (2, {}), {1}: (3, {})} | custom-call | flops 1000000000 | bytes 1000000 | tf_op jit(solution)/shard_map/pallas_call | solution.py:417
  70.7 9.2 %shard_map.71 = (f32[128,1,384]{2,1,0:T(1,128)S(1)}, f32[1,1,384]{2,1,0:T(1,128)S(1)}) custom-call(s32[24,128]{1,0:T(8,128)S(1)} %get-tuple-element.20.counts, f32[192,128]{1,0:T(8,128)S(1)} %get-tuple-element.21.columns, bf16[1984,768]{1,0:T(8,128)(2,1)S(1)} %get-tuple-element.26.cap_v, bf16[3584,768]{1,0:T(8,128)(2,1)S(1)} %get-tuple-element.27.img_v), custom_call_target="tpu_custom_call" | custom-call | flops 4227858432 | bytes 7471104 | tf_op jit(solution)/shard_map/pallas_call | solution.py:426
  79.9 14.6 %all_to_all.22.parts = f32[128,1,384]{2,1,0:T(1,128)S(1)} all-to-all(f32[128,1,384]{2,1,0:T(1,128)S(1)} %get-tuple-element.28), channel_id=1, replica_groups=mesh['x'=4,'h'=2,'z'=4,'c'=2,'l'=2] {'x','h','z','c','l'}, dimensions={0} | all-to-all | bytes 393216 | tf_op jit(solution)/shard_map/all_to_all | solution.py:443
  94.5 0.9 shard_map.72
  95.4 13.9 %all_to_all.23 = f32[128,1,8]{2,1,0:T(1,128)S(1)} all-to-all(f32[128,1,8]{2,1,0:T(1,128)S(1)} %get-tuple-element.34), channel_id=1, replica_groups=mesh['x'=4,'h'=2,'z'=4,'c'=2,'l'=2] {'x','h','z','c','l'}, dimensions={0} | all-to-all | bytes 8192 | tf_op jit(solution)/shard_map/all_to_all | solution.py:452
  109.3 0.7 slice_reduce_fusion
  (27 shorter events, 0.1 us)
Async XLA Ops:
  0.6 2.5 %collective-permute-start = (bf16[192,768]{1,0:T(8,128)(2,1)}, bf16[192,768]{1,0:T(8,128)(2,1)S(1)}, u32[]{:S(2)}, u32[]{:S(2)}) collective-permute-start(bf16[192,768]{1,0:T(8,128)(2,1)} %param.4), channel_id=1, source_target_pairs={{0,2},{1,3},{2,0},{3,1},{4,6},{5,7},{6,4},{7,5},{8,10},{9,11},{10,... | collective-permute-start | bytes 884744 | tf_op jit(solution)/shard_map/ppermute | solution.py:49
  0.7 2.4 %collective-permute-start.1 = (bf16[192,768]{1,0:T(8,128)(2,1)}, bf16[192,768]{1,0:T(8,128)(2,1)S(1)}, u32[]{:S(2)}, u32[]{:S(2)}) collective-permute-start(bf16[192,768]{1,0:T(8,128)(2,1)} %param.5), channel_id=1, source_target_pairs={{0,2},{1,3},{2,0},{3,1},{4,6},{5,7},{6,4},{7,5},{8,10},{9,11},{10,... | collective-permute-start | bytes 884744 | tf_op jit(solution)/shard_map/ppermute | solution.py:49
  1.9 1.2 %collective-permute-start.2 = (s32[1,192]{1,0:T(1,128)S(1)}, s32[1,192]{1,0:T(1,128)S(1)}, u32[]{:S(2)}, u32[]{:S(2)}) collective-permute-start(s32[1,192]{1,0:T(1,128)S(1)} %bitcast.3), channel_id=1, source_target_pairs={{0,2},{1,3},{2,0},{3,1},{4,6},{5,7},{6,4},{7,5},{8,10},{9,11},{10,... | collective-permute-start | bytes 2312 | tf_op jit(solution)/shard_map/ppermute | solution.py:49
  3.5 10.0 %collective-permute-start.3 = (bf16[384,768]{1,0:T(8,128)(2,1)S(1)}, bf16[384,768]{1,0:T(8,128)(2,1)S(1)}, u32[]{:S(2)}, u32[]{:S(2)}) collective-permute-start(bf16[384,768]{1,0:T(8,128)(2,1)S(1)} %get-tuple-element.23.refs_0_), channel_id=1, source_target_pairs={{0,1},{1,0},{2,19},{3,18},{4,5},{5,4},{6,23},{7,22},{8,9},{9,8},{1... | collective-permute-start | bytes 1769480 | tf_op jit(solution)/shard_map/ppermute | solution.py:49
  5.3 12.4 %collective-permute-start.5 = (bf16[384,768]{1,0:T(8,128)(2,1)S(1)}, bf16[384,768]{1,0:T(8,128)(2,1)S(1)}, u32[]{:S(2)}, u32[]{:S(2)}) collective-permute-start(bf16[384,768]{1,0:T(8,128)(2,1)S(1)} %get-tuple-element.23.refs_0_), channel_id=1, source_target_pairs={{0,12},{1,13},{2,98},{3,99},{4,0},{5,1},{6,102},{7,103},{8,4},{9,5... | collective-permute-start | bytes 1769480 | tf_op jit(solution)/shard_map/ppermute | solution.py:49
  9.3 11.1 %collective-permute-start.4 = (bf16[384,768]{1,0:T(8,128)(2,1)S(1)}, bf16[384,768]{1,0:T(8,128)(2,1)S(1)}, u32[]{:S(2)}, u32[]{:S(2)}) collective-permute-start(bf16[384,768]{1,0:T(8,128)(2,1)S(1)} %get-tuple-element.23.refs_0_), channel_id=1, source_target_pairs={{0,4},{1,5},{2,34},{3,35},{4,8},{5,9},{6,38},{7,39},{8,12},{9,13},... | collective-permute-start | bytes 1769480 | tf_op jit(solution)/shard_map/ppermute | solution.py:49
  9.3 11.1 %collective-permute-start.8 = (bf16[384,768]{1,0:T(8,128)(2,1)S(1)}, bf16[384,768]{1,0:T(8,128)(2,1)S(1)}, u32[]{:S(2)}, u32[]{:S(2)}) collective-permute-start(bf16[384,768]{1,0:T(8,128)(2,1)S(1)} %get-tuple-element.23.refs_0_), channel_id=1, source_target_pairs={{0,2},{1,3},{2,0},{3,1},{4,6},{5,7},{6,4},{7,5},{8,10},{9,11},{10,... | collective-permute-start | bytes 1769480 | tf_op jit(solution)/shard_map/ppermute | solution.py:49
  13.5 11.6 %collective-permute-start.7 = (bf16[384,768]{1,0:T(8,128)(2,1)S(1)}, bf16[384,768]{1,0:T(8,128)(2,1)}, u32[]{:S(2)}, u32[]{:S(2)}) collective-permute-start(bf16[384,768]{1,0:T(8,128)(2,1)S(1)} %collective-permute-done.3.refs_1_), channel_id=1, source_target_pairs={{0,12},{1,13},{2,98},{3,99},{4,0},{5,1},{6,102},{7,103},{8,4},{9,5... | collective-permute-start | bytes 1769480 | tf_op jit(solution)/shard_map/ppermute | solution.py:49
  17.7 11.2 %collective-permute-start.11 = (bf16[384,768]{1,0:T(8,128)(2,1)S(1)}, bf16[384,768]{1,0:T(8,128)(2,1)S(1)}, u32[]{:S(2)}, u32[]{:S(2)}) collective-permute-start(bf16[384,768]{1,0:T(8,128)(2,1)S(1)} %collective-permute-done.5.refs_3_), channel_id=1, source_target_pairs={{0,2},{1,3},{2,0},{3,1},{4,6},{5,7},{6,4},{7,5},{8,10},{9,11},{10,... | collective-permute-start | bytes 1769480 | tf_op jit(solution)/shard_map/ppermute | solution.py:49
  20.4 11.1 %collective-permute-start.14 = (bf16[384,768]{1,0:T(8,128)(2,1)S(1)}, bf16[384,768]{1,0:T(8,128)(2,1)S(1)}, u32[]{:S(2)}, u32[]{:S(2)}) collective-permute-start(bf16[384,768]{1,0:T(8,128)(2,1)S(1)} %collective-permute-done.4.refs_2_), channel_id=1, source_target_pairs={{0,4},{1,5},{2,34},{3,35},{4,8},{5,9},{6,38},{7,39},{8,12},{9,13},... | collective-permute-start | bytes 1769480 | tf_op jit(solution)/shard_map/ppermute | solution.py:49
  20.4 17.5 %collective-permute-start.6 = (bf16[384,768]{1,0:T(8,128)(2,1)S(1)}, bf16[384,768]{1,0:T(8,128)(2,1)}, u32[]{:S(2)}, u32[]{:S(2)}) collective-permute-start(bf16[384,768]{1,0:T(8,128)(2,1)S(1)} %collective-permute-done.3.refs_1_), channel_id=1, source_target_pairs={{0,4},{1,5},{2,34},{3,35},{4,8},{5,9},{6,38},{7,39},{8,12},{9,13},... | collective-permute-start | bytes 1769480 | tf_op jit(solution)/shard_map/ppermute | solution.py:49
  20.5 17.5 %collective-permute-start.10 = (bf16[384,768]{1,0:T(8,128)(2,1)S(1)}, bf16[384,768]{1,0:T(8,128)(2,1)S(1)}, u32[]{:S(2)}, u32[]{:S(2)}) collective-permute-start(bf16[384,768]{1,0:T(8,128)(2,1)S(1)} %collective-permute-done.4.refs_2_), channel_id=1, source_target_pairs={{0,2},{1,3},{2,0},{3,1},{4,6},{5,7},{6,4},{7,5},{8,10},{9,11},{10,... | collective-permute-start | bytes 1769480 | tf_op jit(solution)/shard_map/ppermute | solution.py:49
  25.1 14.2 %collective-permute-start.15 = (bf16[384,768]{1,0:T(8,128)(2,1)}, bf16[384,768]{1,0:T(8,128)(2,1)}, u32[]{:S(2)}, u32[]{:S(2)}) collective-permute-start(bf16[384,768]{1,0:T(8,128)(2,1)} %collective-permute-done.7.refs_5_), channel_id=1, source_target_pairs={{0,12},{1,13},{2,98},{3,99},{4,0},{5,1},{6,102},{7,103},{8,4},{9,5... | collective-permute-start | bytes 1769480 | tf_op jit(solution)/shard_map/ppermute | solution.py:49
  28.9 0.8 copy-start
  29.7 36.1 %collective-permute-start.9 = (bf16[384,768]{1,0:T(8,128)(2,1)S(1)}, bf16[384,768]{1,0:T(8,128)(2,1)}, u32[]{:S(2)}, u32[]{:S(2)}) collective-permute-start(bf16[384,768]{1,0:T(8,128)(2,1)S(1)} %collective-permute-done.3.refs_1_), channel_id=1, source_target_pairs={{0,2},{1,3},{2,0},{3,1},{4,6},{5,7},{6,4},{7,5},{8,10},{9,11},{10,... | collective-permute-start | bytes 1769480 | tf_op jit(solution)/shard_map/ppermute | solution.py:49
  31.5 34.2 %collective-permute-start.13 = (bf16[384,768]{1,0:T(8,128)(2,1)}, bf16[384,768]{1,0:T(8,128)(2,1)}, u32[]{:S(2)}, u32[]{:S(2)}) collective-permute-start(bf16[384,768]{1,0:T(8,128)(2,1)} %collective-permute-done.7.refs_5_), channel_id=1, source_target_pairs={{0,2},{1,3},{2,0},{3,1},{4,6},{5,7},{6,4},{7,5},{8,10},{9,11},{10,... | collective-permute-start | bytes 1769480 | tf_op jit(solution)/shard_map/ppermute | solution.py:49
  38.0 27.8 %collective-permute-start.12 = (bf16[384,768]{1,0:T(8,128)(2,1)}, bf16[384,768]{1,0:T(8,128)(2,1)}, u32[]{:S(2)}, u32[]{:S(2)}) collective-permute-start(bf16[384,768]{1,0:T(8,128)(2,1)} %collective-permute-done.6.refs_4_), channel_id=1, source_target_pairs={{0,2},{1,3},{2,0},{3,1},{4,6},{5,7},{6,4},{7,5},{8,10},{9,11},{10,... | collective-permute-start | bytes 1769480 | tf_op jit(solution)/shard_map/ppermute | solution.py:49
  38.0 0.8 copy-start.2
  38.8 29.9 %collective-permute-start.16 = (bf16[384,768]{1,0:T(8,128)(2,1)S(1)}, bf16[384,768]{1,0:T(8,128)(2,1)}, u32[]{:S(2)}, u32[]{:S(2)}) collective-permute-start(bf16[384,768]{1,0:T(8,128)(2,1)S(1)} %collective-permute-done.14.refs_2_), channel_id=1, source_target_pairs={{0,2},{1,3},{2,0},{3,1},{4,6},{5,7},{6,4},{7,5},{8,10},{9,11},{10,... | collective-permute-start | bytes 1769480 | tf_op jit(solution)/shard_map/ppermute | solution.py:49
  39.3 29.4 %collective-permute-start.17 = (bf16[384,768]{1,0:T(8,128)(2,1)}, bf16[384,768]{1,0:T(8,128)(2,1)}, u32[]{:S(2)}, u32[]{:S(2)}) collective-permute-start(bf16[384,768]{1,0:T(8,128)(2,1)} %collective-permute-done.15.refs_3_), channel_id=1, source_target_pairs={{0,2},{1,3},{2,0},{3,1},{4,6},{5,7},{6,4},{7,5},{8,10},{9,11},{10,... | collective-permute-start | bytes 1769480 | tf_op jit(solution)/shard_map/ppermute | solution.py:49
  64.7 1.1 copy-start.1
  64.7 1.2 %copy-start.3 = (bf16[384,768]{1,0:T(8,128)(2,1)S(1)}, bf16[384,768]{1,0:T(8,128)(2,1)}, u32[]{:S(2)}) copy-start(bf16[384,768]{1,0:T(8,128)(2,1)} %copy-done.2) | copy-start | bytes 1769476

commit v5 on v4

--- a/solution.py
+++ b/solution.py
@@ -128,6 +128,10 @@
         packed.append(dot(pick, block[...]).astype(BF16))
     carried[0:B, :] = jnp.where(first, own[...], packed[1])
     carried[B:2 * B, :] = jnp.where(first, cap_other[...], packed[0])
+
+
+def spread_kernel(part, words):
+    words[...] = jnp.broadcast_to(part[...].reshape(1, 16, B), (8, 16, B))
 
 
 def table_row(p):
@@ -215,12 +219,12 @@
     refs = refs[2 if part else 0:]
     number = last - first
     cap_out, img_out = refs[2 * number:]
-    compact(counts, ranks, refs[:number], refs[number:2 * number], cap_out, img_out, first)
-    if last == CAPS:
+    if part == 0:
         cap_end = starts_of(counts, 0, CAPS)[-1]
         img_end = starts_of(counts, CAPS, IMGS)[-1]
         cap_out[pl.ds(cap_end, RC), :] = jnp.zeros((RC, E), BF16)
         img_out[pl.ds(img_end, TAIL), :] = jnp.zeros((TAIL, E), BF16)
+    compact(counts, ranks, refs[:number], refs[number:2 * number], cap_out, img_out, first)
 
 
 def score_kernel(
@@ -399,7 +403,10 @@
     swapped = [send(v, other_core) for v in met.values()]
     carried = list(met.values())
     part = lax.all_to_all(words, ("x", "h"), 0, 0, tiled=True)
-    part = jnp.broadcast_to(part.reshape(1, 16, B), (8, 16, B))
+    part = pl.pallas_call(
+        spread_kernel, out_shape=shape((8, 16, B), jnp.int32), in_specs=[VMEM],
+        out_specs=VMEM, **small(62, 10**8),
+    )(part)
     table = lax.all_to_all(part, ("z", "l"), 0, 0, tiled=True)
     ranks, columns, counts, real = pl.pallas_call(
         lookup_kernel,

time: 111 us -> 112 us (level)
  Pallas kernels: 16.2 us -> 17.8 us
  waiting for transfers between devices: 19.7 us -> 18.1 us
    broadcast_in_dim x2 -> x0, local copies, waits for them, and re-layouts: 2.05 us -> none  [step(): part = jnp.broadcast_to(part.reshape(1, 16, B), (8, 16, B))]
    unnamed x8 -> x16, local copies, waits for them, and re-layouts: 1.84 us -> 3.81 us
    ppermute x18, waiting for transfers between devices: 19.7 us -> 18.1 us  [send(): return lax.ppermute(value, AXES, pairs)]
    pallas_call x0 -> x1, Pallas kernels: none -> 1.37 us  [step(): pl.pallas_call(spread_kernel, out_shape=shape((8, 16, B), jnp.int32), in_...]
  transfers between devices with their start and end apart: 18 -> 18, of which waited for: 6 -> 6; matrix products, arithmetic and copies ran while one was open for 3% -> 2% of each run, Pallas kernels for 3% -> 5%
where the time goes in v5:
time: 112 us; the launch traced here: 110 us
  blocking collectives  52.3 us (47%)
  waiting for transfers between devices  18.1 us (16%)
  Pallas kernels  17.8 us (16%)
  starting transfers between devices  15.1 us (13%)
  local copies, waits for them, and re-layouts  3.81 us (3%)
  other arithmetic  2.43 us (2%)
    ppermute x18, waiting for transfers between devices, send(): return lax.ppermute(value, AXES, pairs)  18.1 us
    ppermute x18, starting transfers between devices, send(): return lax.ppermute(value, AXES, pairs)  15.1 us
    all_to_all x1, blocking collectives, step(): part = lax.all_to_all(words, ('x', 'h'), 0, 0, tiled=True)  14.2 us
    all_to_all x1, blocking collectives, step(): parts = lax.all_to_all(out, AXES, 0, 0, tiled=True)  14.2 us
    all_to_all x1, blocking collectives, step(): totals = lax.all_to_all(total, AXES, 0, 0, tiled=True)  13.9 us
    all_to_all x1, blocking collectives, step(): table = lax.all_to_all(part, ('z', 'l'), 0, 0, tiled=True)  9.97 us
    pallas_call x1, Pallas kernels, step(): pl.pallas_call(score_kernel, out_shape=[shape((n, 1, 2 * B), F32) for n i...  9.2 us
    pallas_call x2, Pallas kernels, step(): pl.pallas_call(functools.partial(compact_kernel, part), out_shape=[shape(...  4.82 us
  transfers between devices with their start and end apart: 18, of which 6 were waited for; matrix products, arithmetic and copies ran while one was open for 2% of the time, Pallas kernels for 5%

profile of v5, /device:TPU:0, one launch (start us, length us, event | category | flops | bytes accessed | tf_op | source)
XLA Modules:
  0.0 110.2 jit_solution(16034962656248041884)
XLA Ops:
  0.7 0.5 collective-permute-start.1
  1.2 0.7 multiply_add_fusion
  2.0 1.0 broadcast_select_fusion.own
  3.1 0.4 shard_map.67
  3.5 1.8 %collective-permute-start.3 = (bf16[384,768]{1,0:T(8,128)(2,1)S(1)}, bf16[384,768]{1,0:T(8,128)(2,1)S(1)}, u32[]{:S(2)}, u32[]{:S(2)}) collective-permute-start(bf16[384,768]{1,0:T(8,128)(2,1)S(1)} %get-tuple-element.23.refs_0_), channel_id=1, source_target_pairs={{0,1},{1,0},{2,19},{3,18},{4,5},{5,4},{6,23},{7,22},{8,9},{9,8},{1... | collective-permute-start | bytes 1769480 | tf_op jit(solution)/shard_map/ppermute | solution.py:49
  5.3 4.0 %collective-permute-start.5 = (bf16[384,768]{1,0:T(8,128)(2,1)S(1)}, bf16[384,768]{1,0:T(8,128)(2,1)S(1)}, u32[]{:S(2)}, u32[]{:S(2)}) collective-permute-start(bf16[384,768]{1,0:T(8,128)(2,1)S(1)} %get-tuple-element.23.refs_0_), channel_id=1, source_target_pairs={{0,12},{1,13},{2,98},{3,99},{4,0},{5,1},{6,102},{7,103},{8,4},{9,5... | collective-permute-start | bytes 1769480 | tf_op jit(solution)/shard_map/ppermute | solution.py:49
  9.4 4.1 %collective-permute-done.3.refs_1_ = bf16[384,768]{1,0:T(8,128)(2,1)S(1)} collective-permute-done((bf16[384,768]{1,0:T(8,128)(2,1)S(1)}, bf16[384,768]{1,0:T(8,128)(2,1)S(1)}, u32[]{:S(2)}, u32[]{:S(2)}) %collective-permute-start.3) | collective-permute-done | bytes 589856 | tf_op jit(solution)/shard_map/ppermute | solution.py:49
  13.5 4.2 %collective-permute-start.7 = (bf16[384,768]{1,0:T(8,128)(2,1)S(1)}, bf16[384,768]{1,0:T(8,128)(2,1)}, u32[]{:S(2)}, u32[]{:S(2)}) collective-permute-start(bf16[384,768]{1,0:T(8,128)(2,1)S(1)} %collective-permute-done.3.refs_1_), channel_id=1, source_target_pairs={{0,12},{1,13},{2,98},{3,99},{4,0},{5,1},{6,102},{7,103},{8,4},{9,5... | collective-permute-start | bytes 1769480 | tf_op jit(solution)/shard_map/ppermute | solution.py:49
  17.7 2.8 %collective-permute-done.4.refs_2_ = bf16[384,768]{1,0:T(8,128)(2,1)S(1)} collective-permute-done((bf16[384,768]{1,0:T(8,128)(2,1)S(1)}, bf16[384,768]{1,0:T(8,128)(2,1)S(1)}, u32[]{:S(2)}, u32[]{:S(2)}) %collective-permute-start.4) | collective-permute-done | bytes 589856 | tf_op jit(solution)/shard_map/ppermute | solution.py:49
  20.5 0.8 copy-done.2
  21.4 0.8 copy-done
  22.3 2.8 %collective-permute-done.7.refs_5_ = bf16[384,768]{1,0:T(8,128)(2,1)} collective-permute-done((bf16[384,768]{1,0:T(8,128)(2,1)S(1)}, bf16[384,768]{1,0:T(8,128)(2,1)}, u32[]{:S(2)}, u32[]{:S(2)}) %collective-permute-start.7) | collective-permute-done | bytes 589856 | tf_op jit(solution)/shard_map/ppermute | solution.py:49
  25.1 3.8 %collective-permute-start.15 = (bf16[384,768]{1,0:T(8,128)(2,1)}, bf16[384,768]{1,0:T(8,128)(2,1)}, u32[]{:S(2)}, u32[]{:S(2)}) collective-permute-start(bf16[384,768]{1,0:T(8,128)(2,1)} %collective-permute-done.7.refs_5_), channel_id=1, source_target_pairs={{0,12},{1,13},{2,98},{3,99},{4,0},{5,1},{6,102},{7,103},{8,4},{9,5... | collective-permute-start | bytes 1769480 | tf_op jit(solution)/shard_map/ppermute | solution.py:49
  28.9 0.8 copy-done.4
  29.7 2.0 %collective-permute-done.14.refs_2_ = bf16[384,768]{1,0:T(8,128)(2,1)} collective-permute-done((bf16[384,768]{1,0:T(8,128)(2,1)S(1)}, bf16[384,768]{1,0:T(8,128)(2,1)}, u32[]{:S(2)}, u32[]{:S(2)}) %collective-permute-start.14) | collective-permute-done | bytes 589856 | tf_op jit(solution)/shard_map/ppermute | solution.py:49
  31.6 6.3 %collective-permute-done.6.refs_4_ = bf16[384,768]{1,0:T(8,128)(2,1)} collective-permute-done((bf16[384,768]{1,0:T(8,128)(2,1)S(1)}, bf16[384,768]{1,0:T(8,128)(2,1)}, u32[]{:S(2)}, u32[]{:S(2)}) %collective-permute-start.6) | collective-permute-done | bytes 589856 | tf_op jit(solution)/shard_map/ppermute | solution.py:49
  38.0 0.8 copy-done.6
  38.8 0.5 collective-permute-start.16
  39.3 14.2 %all_to_all.20.part = s32[8,2,192]{2,1,0:T(2,128)} all-to-all(s32[8,2,192]{2,1,0:T(2,128)S(1)} %get-tuple-element.19), channel_id=1, replica_groups=mesh['x'=4,'h'=2,'z'=4,'c'=2,'l'=2] {'x','h'}, dimensions={0} | all-to-all | bytes 24576 | tf_op jit(solution)/shard_map/all_to_all | solution.py:405
  53.5 1.4 %shard_map.68 = s32[8,16,192]{2,1,0:T(8,128)} custom-call(s32[8,2,192]{2,1,0:T(2,128)} %all_to_all.20.part), custom_call_target="tpu_custom_call" | custom-call | flops 100000000 | bytes 1000000 | tf_op jit(solution)/shard_map/pallas_call | solution.py:406
  54.9 10.0 %all_to_all.21.table = s32[8,16,192]{2,1,0:T(8,128)S(1)} all-to-all(s32[8,16,192]{2,1,0:T(8,128)} %shard_map.68), channel_id=1, replica_groups=mesh['x'=4,'h'=2,'z'=4,'c'=2,'l'=2] {'z','l'}, dimensions={0} | all-to-all | bytes 196608 | tf_op jit(solution)/shard_map/all_to_all | solution.py:410
  64.9 1.0 shard_map.69
  65.9 0.2 copy-done.3
  66.1 0.2 copy-done.5
  66.3 0.2 copy-done.7
  66.5 2.8 %shard_map.70 = (bf16[1984,768]{1,0:T(8,128)(2,1)S(1)}, bf16[3584,768]{1,0:T(8,128)(2,1)S(1)}) custom-call(s32[24,128]{1,0:T(8,128)S(1)} %get-tuple-element.20.counts, f32[8,192]{1,0:T(8,128)S(1)} %get-tuple-element.22.ranks.row_ranks, bf16[384,768]{1,0:T(8,128)(2,1)S(1)} %get-tuple-element.23.refs_0_, bf16[384,768]{1,0:T(8,128)(2,1)S(1)} %collective-permute-done.3.refs_1_, ...), custom_call_target="tpu_custom_call" | custom-call | flops 1000000000 | bytes 1000000 | tf_op jit(solution)/shard_map/pallas_call | solution.py:424
  69.3 2.0 %shard_map.71 = (bf16[1984,768]{1,0:T(8,128)(2,1)S(1)}, bf16[3584,768]{1,0:T(8,128)(2,1)S(1)}) custom-call(s32[24,128]{1,0:T(8,128)S(1)} %get-tuple-element.20.counts, f32[8,192]{1,0:T(8,128)S(1)} %get-tuple-element.22.ranks.row_ranks, bf16[1984,768]{1,0:T(8,128)(2,1)S(1)} %get-tuple-element.24.refs_0_, ...), custom_call_target="tpu_custom_call", output_to_operand_aliasing={{0}: (2, {}), {1}: (3, {})} | custom-call | flops 1000000000 | bytes 1000000 | tf_op jit(solution)/shard_map/pallas_call | solution.py:424
  71.3 9.2 %shard_map.72 = (f32[128,1,384]{2,1,0:T(1,128)S(1)}, f32[1,1,384]{2,1,0:T(1,128)S(1)}) custom-call(s32[24,128]{1,0:T(8,128)S(1)} %get-tuple-element.20.counts, f32[192,128]{1,0:T(8,128)S(1)} %get-tuple-element.21.columns, bf16[1984,768]{1,0:T(8,128)(2,1)S(1)} %get-tuple-element.26.cap_v, bf16[3584,768]{1,0:T(8,128)(2,1)S(1)} %get-tuple-element.27.img_v), custom_call_target="tpu_custom_call" | custom-call | flops 4227858432 | bytes 7471104 | tf_op jit(solution)/shard_map/pallas_call | solution.py:433
  80.5 14.2 %all_to_all.22.parts = f32[128,1,384]{2,1,0:T(1,128)S(1)} all-to-all(f32[128,1,384]{2,1,0:T(1,128)S(1)} %get-tuple-element.28), channel_id=1, replica_groups=mesh['x'=4,'h'=2,'z'=4,'c'=2,'l'=2] {'x','h','z','c','l'}, dimensions={0} | all-to-all | bytes 393216 | tf_op jit(solution)/shard_map/all_to_all | solution.py:450
  94.7 0.9 shard_map.73
  95.6 13.9 %all_to_all.23 = f32[128,1,8]{2,1,0:T(1,128)S(1)} all-to-all(f32[128,1,8]{2,1,0:T(1,128)S(1)} %get-tuple-element.34), channel_id=1, replica_groups=mesh['x'=4,'h'=2,'z'=4,'c'=2,'l'=2] {'x','h','z','c','l'}, dimensions={0} | all-to-all | bytes 8192 | tf_op jit(solution)/shard_map/all_to_all | solution.py:459
  109.5 0.7 slice_reduce_fusion
  (34 shorter events, 0.5 us)
Async XLA Ops:
  0.6 2.5 %collective-permute-start = (bf16[192,768]{1,0:T(8,128)(2,1)}, bf16[192,768]{1,0:T(8,128)(2,1)S(1)}, u32[]{:S(2)}, u32[]{:S(2)}) collective-permute-start(bf16[192,768]{1,0:T(8,128)(2,1)} %param.4), channel_id=1, source_target_pairs={{0,2},{1,3},{2,0},{3,1},{4,6},{5,7},{6,4},{7,5},{8,10},{9,11},{10,... | collective-permute-start | bytes 884744 | tf_op jit(solution)/shard_map/ppermute | solution.py:49
  0.7 2.4 %collective-permute-start.1 = (bf16[192,768]{1,0:T(8,128)(2,1)}, bf16[192,768]{1,0:T(8,128)(2,1)S(1)}, u32[]{:S(2)}, u32[]{:S(2)}) collective-permute-start(bf16[192,768]{1,0:T(8,128)(2,1)} %param.5), channel_id=1, source_target_pairs={{0,2},{1,3},{2,0},{3,1},{4,6},{5,7},{6,4},{7,5},{8,10},{9,11},{10,... | collective-permute-start | bytes 884744 | tf_op jit(solution)/shard_map/ppermute | solution.py:49
  1.9 1.2 %collective-permute-start.2 = (s32[1,192]{1,0:T(1,128)S(1)}, s32[1,192]{1,0:T(1,128)S(1)}, u32[]{:S(2)}, u32[]{:S(2)}) collective-permute-start(s32[1,192]{1,0:T(1,128)S(1)} %bitcast.3), channel_id=1, source_target_pairs={{0,2},{1,3},{2,0},{3,1},{4,6},{5,7},{6,4},{7,5},{8,10},{9,11},{10,... | collective-permute-start | bytes 2312 | tf_op jit(solution)/shard_map/ppermute | solution.py:49
  3.5 10.0 %collective-permute-start.3 = (bf16[384,768]{1,0:T(8,128)(2,1)S(1)}, bf16[384,768]{1,0:T(8,128)(2,1)S(1)}, u32[]{:S(2)}, u32[]{:S(2)}) collective-permute-start(bf16[384,768]{1,0:T(8,128)(2,1)S(1)} %get-tuple-element.23.refs_0_), channel_id=1, source_target_pairs={{0,1},{1,0},{2,19},{3,18},{4,5},{5,4},{6,23},{7,22},{8,9},{9,8},{1... | collective-permute-start | bytes 1769480 | tf_op jit(solution)/shard_map/ppermute | solution.py:49
  5.3 12.4 %collective-permute-start.5 = (bf16[384,768]{1,0:T(8,128)(2,1)S(1)}, bf16[384,768]{1,0:T(8,128)(2,1)S(1)}, u32[]{:S(2)}, u32[]{:S(2)}) collective-permute-start(bf16[384,768]{1,0:T(8,128)(2,1)S(1)} %get-tuple-element.23.refs_0_), channel_id=1, source_target_pairs={{0,12},{1,13},{2,98},{3,99},{4,0},{5,1},{6,102},{7,103},{8,4},{9,5... | collective-permute-start | bytes 1769480 | tf_op jit(solution)/shard_map/ppermute | solution.py:49
  9.3 11.1 %collective-permute-start.4 = (bf16[384,768]{1,0:T(8,128)(2,1)S(1)}, bf16[384,768]{1,0:T(8,128)(2,1)S(1)}, u32[]{:S(2)}, u32[]{:S(2)}) collective-permute-start(bf16[384,768]{1,0:T(8,128)(2,1)S(1)} %get-tuple-element.23.refs_0_), channel_id=1, source_target_pairs={{0,4},{1,5},{2,34},{3,35},{4,8},{5,9},{6,38},{7,39},{8,12},{9,13},... | collective-permute-start | bytes 1769480 | tf_op jit(solution)/shard_map/ppermute | solution.py:49
  9.3 11.1 %collective-permute-start.8 = (bf16[384,768]{1,0:T(8,128)(2,1)S(1)}, bf16[384,768]{1,0:T(8,128)(2,1)S(1)}, u32[]{:S(2)}, u32[]{:S(2)}) collective-permute-start(bf16[384,768]{1,0:T(8,128)(2,1)S(1)} %get-tuple-element.23.refs_0_), channel_id=1, source_target_pairs={{0,2},{1,3},{2,0},{3,1},{4,6},{5,7},{6,4},{7,5},{8,10},{9,11},{10,... | collective-permute-start | bytes 1769480 | tf_op jit(solution)/shard_map/ppermute | solution.py:49
  13.5 11.6 %collective-permute-start.7 = (bf16[384,768]{1,0:T(8,128)(2,1)S(1)}, bf16[384,768]{1,0:T(8,128)(2,1)}, u32[]{:S(2)}, u32[]{:S(2)}) collective-permute-start(bf16[384,768]{1,0:T(8,128)(2,1)S(1)} %collective-permute-done.3.refs_1_), channel_id=1, source_target_pairs={{0,12},{1,13},{2,98},{3,99},{4,0},{5,1},{6,102},{7,103},{8,4},{9,5... | collective-permute-start | bytes 1769480 | tf_op jit(solution)/shard_map/ppermute | solution.py:49
  17.7 11.2 %collective-permute-start.11 = (bf16[384,768]{1,0:T(8,128)(2,1)S(1)}, bf16[384,768]{1,0:T(8,128)(2,1)S(1)}, u32[]{:S(2)}, u32[]{:S(2)}) collective-permute-start(bf16[384,768]{1,0:T(8,128)(2,1)S(1)} %collective-permute-done.5.refs_3_), channel_id=1, source_target_pairs={{0,2},{1,3},{2,0},{3,1},{4,6},{5,7},{6,4},{7,5},{8,10},{9,11},{10,... | collective-permute-start | bytes 1769480 | tf_op jit(solution)/shard_map/ppermute | solution.py:49
  20.4 11.2 %collective-permute-start.14 = (bf16[384,768]{1,0:T(8,128)(2,1)S(1)}, bf16[384,768]{1,0:T(8,128)(2,1)}, u32[]{:S(2)}, u32[]{:S(2)}) collective-permute-start(bf16[384,768]{1,0:T(8,128)(2,1)S(1)} %collective-permute-done.4.refs_2_), channel_id=1, source_target_pairs={{0,4},{1,5},{2,34},{3,35},{4,8},{5,9},{6,38},{7,39},{8,12},{9,13},... | collective-permute-start | bytes 1769480 | tf_op jit(solution)/shard_map/ppermute | solution.py:49
  20.4 17.5 %collective-permute-start.6 = (bf16[384,768]{1,0:T(8,128)(2,1)S(1)}, bf16[384,768]{1,0:T(8,128)(2,1)}, u32[]{:S(2)}, u32[]{:S(2)}) collective-permute-start(bf16[384,768]{1,0:T(8,128)(2,1)S(1)} %collective-permute-done.3.refs_1_), channel_id=1, source_target_pairs={{0,4},{1,5},{2,34},{3,35},{4,8},{5,9},{6,38},{7,39},{8,12},{9,13},... | collective-permute-start | bytes 1769480 | tf_op jit(solution)/shard_map/ppermute | solution.py:49
  20.5 0.8 copy-start.2
  21.3 16.7 %collective-permute-start.10 = (bf16[384,768]{1,0:T(8,128)(2,1)S(1)}, bf16[384,768]{1,0:T(8,128)(2,1)S(1)}, u32[]{:S(2)}, u32[]{:S(2)}) collective-permute-start(bf16[384,768]{1,0:T(8,128)(2,1)S(1)} %collective-permute-done.4.refs_2_), channel_id=1, source_target_pairs={{0,2},{1,3},{2,0},{3,1},{4,6},{5,7},{6,4},{7,5},{8,10},{9,11},{10,... | collective-permute-start | bytes 1769480 | tf_op jit(solution)/shard_map/ppermute | solution.py:49
  21.4 0.8 copy-start
  25.1 14.2 %collective-permute-start.15 = (bf16[384,768]{1,0:T(8,128)(2,1)}, bf16[384,768]{1,0:T(8,128)(2,1)}, u32[]{:S(2)}, u32[]{:S(2)}) collective-permute-start(bf16[384,768]{1,0:T(8,128)(2,1)} %collective-permute-done.7.refs_5_), channel_id=1, source_target_pairs={{0,12},{1,13},{2,98},{3,99},{4,0},{5,1},{6,102},{7,103},{8,4},{9,5... | collective-permute-start | bytes 1769480 | tf_op jit(solution)/shard_map/ppermute | solution.py:49
  28.9 0.8 copy-start.4
  29.7 36.2 %collective-permute-start.9 = (bf16[384,768]{1,0:T(8,128)(2,1)S(1)}, bf16[384,768]{1,0:T(8,128)(2,1)}, u32[]{:S(2)}, u32[]{:S(2)}) collective-permute-start(bf16[384,768]{1,0:T(8,128)(2,1)S(1)} %collective-permute-done.3.refs_1_), channel_id=1, source_target_pairs={{0,2},{1,3},{2,0},{3,1},{4,6},{5,7},{6,4},{7,5},{8,10},{9,11},{10,... | collective-permute-start | bytes 1769480 | tf_op jit(solution)/shard_map/ppermute | solution.py:49
  31.6 34.3 %collective-permute-start.13 = (bf16[384,768]{1,0:T(8,128)(2,1)}, bf16[384,768]{1,0:T(8,128)(2,1)}, u32[]{:S(2)}, u32[]{:S(2)}) collective-permute-start(bf16[384,768]{1,0:T(8,128)(2,1)} %collective-permute-done.7.refs_5_), channel_id=1, source_target_pairs={{0,2},{1,3},{2,0},{3,1},{4,6},{5,7},{6,4},{7,5},{8,10},{9,11},{10,... | collective-permute-start | bytes 1769480 | tf_op jit(solution)/shard_map/ppermute | solution.py:49
  38.0 28.0 %collective-permute-start.12 = (bf16[384,768]{1,0:T(8,128)(2,1)}, bf16[384,768]{1,0:T(8,128)(2,1)}, u32[]{:S(2)}, u32[]{:S(2)}) collective-permute-start(bf16[384,768]{1,0:T(8,128)(2,1)} %collective-permute-done.6.refs_4_), channel_id=1, source_target_pairs={{0,2},{1,3},{2,0},{3,1},{4,6},{5,7},{6,4},{7,5},{8,10},{9,11},{10,... | collective-permute-start | bytes 1769480 | tf_op jit(solution)/shard_map/ppermute | solution.py:49
  38.0 0.8 copy-start.6
  38.8 30.5 %collective-permute-start.16 = (bf16[384,768]{1,0:T(8,128)(2,1)}, bf16[384,768]{1,0:T(8,128)(2,1)}, u32[]{:S(2)}, u32[]{:S(2)}) collective-permute-start(bf16[384,768]{1,0:T(8,128)(2,1)} %collective-permute-done.14.refs_2_), channel_id=1, source_target_pairs={{0,2},{1,3},{2,0},{3,1},{4,6},{5,7},{6,4},{7,5},{8,10},{9,11},{10,... | collective-permute-start | bytes 1769480 | tf_op jit(solution)/shard_map/ppermute | solution.py:49
  39.3 30.0 %collective-permute-start.17 = (bf16[384,768]{1,0:T(8,128)(2,1)}, bf16[384,768]{1,0:T(8,128)(2,1)}, u32[]{:S(2)}, u32[]{:S(2)}) collective-permute-start(bf16[384,768]{1,0:T(8,128)(2,1)} %collective-permute-done.15.refs_3_), channel_id=1, source_target_pairs={{0,2},{1,3},{2,0},{3,1},{4,6},{5,7},{6,4},{7,5},{8,10},{9,11},{10,... | collective-permute-start | bytes 1769480 | tf_op jit(solution)/shard_map/ppermute | solution.py:49
  64.9 1.1 copy-start.1
  64.9 1.2 %copy-start.3 = (bf16[384,768]{1,0:T(8,128)(2,1)S(1)}, bf16[384,768]{1,0:T(8,128)(2,1)}, u32[]{:S(2)}) copy-start(bf16[384,768]{1,0:T(8,128)(2,1)} %copy-done.2) | copy-start | bytes 1769476
  64.9 1.4 %copy-start.5 = (bf16[384,768]{1,0:T(8,128)(2,1)S(1)}, bf16[384,768]{1,0:T(8,128)(2,1)}, u32[]{:S(2)}) copy-start(bf16[384,768]{1,0:T(8,128)(2,1)} %copy-done.4) | copy-start | bytes 1769476
  64.9 1.6 %copy-start.7 = (bf16[384,768]{1,0:T(8,128)(2,1)S(1)}, bf16[384,768]{1,0:T(8,128)(2,1)}, u32[]{:S(2)}) copy-start(bf16[384,768]{1,0:T(8,128)(2,1)} %copy-done.6) | copy-start | bytes 1769476

commit v6 on v5

--- a/solution.py
+++ b/solution.py
@@ -31,6 +31,7 @@
 TAIL = 2 * NC
 IMG_ROWS = C + TAIL
 PIECE = 32
+SPAN = 7 * 128
 GRAIN = 16
 OK_BIT = 15
 ABSENT = 9999.0
@@ -229,7 +230,7 @@
 
 def score_kernel(
     counts, columns, cap_v, img_v, out, own_row,
-    t_v, pos_b, bias_b, rmax, rmatch, rsum, col_bias, cmax, cmatch, csum, lines_v,
+    t_v, pos_b, bias_b, rmax, rmatch, rsum, col_bias, cmax, cmatch, csum, lines_v, row_lines,
 ):
     img_at = starts_of(counts, CAPS, IMGS)
     col_bias[...] = jnp.full((8, C + 384), LOW, F32)
@@ -317,28 +318,36 @@
     for below, count in zip((0, *COUNTS), COUNTS):
         pl.when((used > below) & (used <= count))(lambda count=count: tiles(count))
 
-    p = place()
-    lanes = lax.broadcasted_iota(jnp.int32, (B, 128), 1)
-    for k in range(CAPS):
-        rows = pl.ds(cap_at[k], B)
-        total = jnp.sum(rsum[rows, :], axis=1, keepdims=True)
-        match = jnp.sum(rmatch[rows, :], axis=1, keepdims=True)
-        packed = jnp.where(lanes == 0, rmax[rows, :] + jnp.log2(total), match)
-        lines = jnp.transpose(packed)
-        if k:
-            put(out, flat(cap_place(p, k)), lines)
-        else:
-            put(own_row, 0, lines)
+    lanes = lax.broadcasted_iota(jnp.int32, (128, 128), 1)
+
+    @pl.loop(0, lax.div(rows_used + (SPAN - 1), SPAN))
+    def _(i):
+        for j in range(SPAN // 128):
+            rows = pl.ds(pl.multiple_of(i * SPAN + j * 128, 128), 128)
+            total = jnp.sum(rsum[rows, :], axis=1, keepdims=True)
+            match = jnp.sum(rmatch[rows, :], axis=1, keepdims=True)
+            packed = jnp.where(lanes == 0, rmax[rows, :] + jnp.log2(total), match)
+            row_lines[:, rows] = jnp.transpose(packed)[0:8, :]
+
     line = lax.broadcasted_iota(jnp.int32, (8, C), 0)
     total = jnp.sum(csum[...], axis=0, keepdims=True)
     match = jnp.sum(cmatch[...], axis=0, keepdims=True)
     lines_v[:, :C] = jnp.where(line == 0, cmax[0:1, :] + jnp.log2(total), match)
-    lines_v[:, C:] = jnp.zeros((8, 384), F32)
+    p = place()
+    for k in range(CAPS):
+        cut = cut_at(row_lines, cap_at[k])
+        if k:
+            put(out, flat(cap_place(p, k)), cut)
+        else:
+            put(own_row, 0, cut)
     for m in range(IMGS):
-        whole = lax.shift_left(lax.shift_right_logical(img_at[m], 7), 7)
-        slab = lines_v[:, pl.ds(pl.multiple_of(whole, 128), 384)]
-        slab = pltpu.roll(slab, lax.rem(384 - (img_at[m] - whole), 384), 1)
-        put(out, flat(img_place(p, m)), slab)
+        put(out, flat(img_place(p, m)), cut_at(lines_v, img_at[m]))
+
+
+def cut_at(lines, start):
+    whole = lax.shift_left(lax.shift_right_logical(start, 7), 7)
+    slab = lines[:, pl.ds(pl.multiple_of(whole, 128), 384)]
+    return pltpu.roll(slab, lax.rem(384 - (start - whole), 384), 1)
 
 
 def put(out, at, lines):
@@ -405,7 +414,7 @@
     part = lax.all_to_all(words, ("x", "h"), 0, 0, tiled=True)
     part = pl.pallas_call(
         spread_kernel, out_shape=shape((8, 16, B), jnp.int32), in_specs=[VMEM],
-        out_specs=VMEM, **small(62, 10**8),
+        out_specs=VMEM, **small(2, 10**8),
     )(part)
     table = lax.all_to_all(part, ("z", "l"), 0, 0, tiled=True)
     ranks, columns, counts, real = pl.pallas_call(
@@ -441,6 +450,7 @@
             pltpu.VMEM((8, C + 384), F32),
             *[pltpu.VMEM((8, C), F32)] * 3,
             pltpu.VMEM((8, C + 384), F32),
+            pltpu.VMEM((8, R + 384), F32),
         ],
         compiler_params=pltpu.CompilerParams(vmem_limit_bytes=31 * 1024 * 1024),
         cost_estimate=pl.CostEstimate(

time: 112 us -> 105 us (0.938)
  Pallas kernels: 17.8 us -> 12.8 us
  local copies, waits for them, and re-layouts: 3.81 us -> 0 us
  waiting for transfers between devices: 18.1 us -> 20.6 us
    unnamed x16 -> x0, local copies, waits for them, and re-layouts: 3.81 us -> none
    ppermute x18, waiting for transfers between devices: 18.1 us -> 20.6 us  [send(): return lax.ppermute(value, AXES, pairs)]
    pallas_call x1, Pallas kernels: 9.2 us -> 7.36 us  [step(): pl.pallas_call(score_kernel, out_shape=[shape((n, 1, 2 * B), F32) for n i...]
    pallas_call x2, Pallas kernels: 4.82 us -> 3.04 us  [step(): pl.pallas_call(functools.partial(compact_kernel, part), out_shape=[shape(...]
    pallas_call x1, Pallas kernels: 1.37 us -> 0.01 us  [step(): pl.pallas_call(spread_kernel, out_shape=shape((8, 16, B), jnp.int32), in_...]
  transfers between devices with their start and end apart: 18 -> 18, of which waited for: 6 -> 6; matrix products, arithmetic and copies ran while one was open for 2% -> 2% of each run, Pallas kernels for 5% -> 3%
where the time goes in v6:
time: 105 us; the launch traced here: 104 us
  blocking collectives  52 us (50%)
  waiting for transfers between devices  20.6 us (20%)
  starting transfers between devices  15.1 us (14%)
  Pallas kernels  12.8 us (12%)
  other arithmetic  2.43 us (2%)
    ppermute x18, waiting for transfers between devices, send(): return lax.ppermute(value, AXES, pairs)  20.6 us
    ppermute x18, starting transfers between devices, send(): return lax.ppermute(value, AXES, pairs)  15.1 us
    all_to_all x1, blocking collectives, step(): parts = lax.all_to_all(out, AXES, 0, 0, tiled=True)  14.4 us
    all_to_all x1, blocking collectives, step(): part = lax.all_to_all(words, ('x', 'h'), 0, 0, tiled=True)  14.1 us
    all_to_all x1, blocking collectives, step(): totals = lax.all_to_all(total, AXES, 0, 0, tiled=True)  13.9 us
    all_to_all x1, blocking collectives, step(): table = lax.all_to_all(part, ('z', 'l'), 0, 0, tiled=True)  9.57 us
    pallas_call x1, Pallas kernels, step(): pl.pallas_call(score_kernel, out_shape=[shape((n, 1, 2 * B), F32) for n i...  7.36 us
    pallas_call x2, Pallas kernels, step(): pl.pallas_call(functools.partial(compact_kernel, part), out_shape=[shape(...  3.04 us
  transfers between devices with their start and end apart: 18, of which 6 were waited for; matrix products, arithmetic and copies ran while one was open for 2% of the time, Pallas kernels for 3%

profile of v6, /device:TPU:0, one launch (start us, length us, event | category | flops | bytes accessed | tf_op | source)
XLA Modules:
  0.0 103.6 jit_solution(16536650012616105483)
XLA Ops:
  0.6 0.1 collective-permute-start
  0.7 0.5 collective-permute-start.1
  1.2 0.7 multiply_add_fusion
  1.9 0.1 collective-permute-start.2
  2.0 1.0 broadcast_select_fusion.own
  3.0 0.1 collective-permute-done.2.word_other
  3.1 0.0 collective-permute-done.cap_other
  3.1 0.4 shard_map.67
  3.5 1.8 %collective-permute-start.3 = (bf16[384,768]{1,0:T(8,128)(2,1)S(1)}, bf16[384,768]{1,0:T(8,128)(2,1)S(1)}, u32[]{:S(2)}, u32[]{:S(2)}) collective-permute-start(bf16[384,768]{1,0:T(8,128)(2,1)S(1)} %get-tuple-element.23.refs_0_), channel_id=1, source_target_pairs={{0,1},{1,0},{2,19},{3,18},{4,5},{5,4},{6,23},{7,22},{8,9},{9,8},{1... | collective-permute-start | bytes 1769480 | tf_op jit(solution)/shard_map/ppermute | solution.py:50
  5.3 4.0 %collective-permute-start.5 = (bf16[384,768]{1,0:T(8,128)(2,1)S(1)}, bf16[384,768]{1,0:T(8,128)(2,1)S(1)}, u32[]{:S(2)}, u32[]{:S(2)}) collective-permute-start(bf16[384,768]{1,0:T(8,128)(2,1)S(1)} %get-tuple-element.23.refs_0_), channel_id=1, source_target_pairs={{0,12},{1,13},{2,98},{3,99},{4,0},{5,1},{6,102},{7,103},{8,4},{9,5... | collective-permute-start | bytes 1769480 | tf_op jit(solution)/shard_map/ppermute | solution.py:50
  9.3 0.0 collective-permute-start.4
  9.4 0.0 collective-permute-start.8
  9.4 4.1 %collective-permute-done.3.refs_1_ = bf16[384,768]{1,0:T(8,128)(2,1)S(1)} collective-permute-done((bf16[384,768]{1,0:T(8,128)(2,1)S(1)}, bf16[384,768]{1,0:T(8,128)(2,1)S(1)}, u32[]{:S(2)}, u32[]{:S(2)}) %collective-permute-start.3) | collective-permute-done | bytes 589856 | tf_op jit(solution)/shard_map/ppermute | solution.py:50
  13.5 4.2 %collective-permute-start.7 = (bf16[384,768]{1,0:T(8,128)(2,1)S(1)}, bf16[384,768]{1,0:T(8,128)(2,1)S(1)}, u32[]{:S(2)}, u32[]{:S(2)}) collective-permute-start(bf16[384,768]{1,0:T(8,128)(2,1)S(1)} %collective-permute-done.3.refs_1_), channel_id=1, source_target_pairs={{0,12},{1,13},{2,98},{3,99},{4,0},{5,1},{6,102},{7,103},{8,4},{9,5... | collective-permute-start | bytes 1769480 | tf_op jit(solution)/shard_map/ppermute | solution.py:50
  17.7 2.8 %collective-permute-done.4.refs_2_ = bf16[384,768]{1,0:T(8,128)(2,1)S(1)} collective-permute-done((bf16[384,768]{1,0:T(8,128)(2,1)S(1)}, bf16[384,768]{1,0:T(8,128)(2,1)S(1)}, u32[]{:S(2)}, u32[]{:S(2)}) %collective-permute-start.4) | collective-permute-done | bytes 589856 | tf_op jit(solution)/shard_map/ppermute | solution.py:50
  20.5 0.1 collective-permute-start.10
  20.6 4.5 %collective-permute-done.7.refs_5_ = bf16[384,768]{1,0:T(8,128)(2,1)S(1)} collective-permute-done((bf16[384,768]{1,0:T(8,128)(2,1)S(1)}, bf16[384,768]{1,0:T(8,128)(2,1)S(1)}, u32[]{:S(2)}, u32[]{:S(2)}) %collective-permute-start.7) | collective-permute-done | bytes 589856 | tf_op jit(solution)/shard_map/ppermute | solution.py:50
  25.1 3.7 %collective-permute-start.15 = (bf16[384,768]{1,0:T(8,128)(2,1)S(1)}, bf16[384,768]{1,0:T(8,128)(2,1)S(1)}, u32[]{:S(2)}, u32[]{:S(2)}) collective-permute-start(bf16[384,768]{1,0:T(8,128)(2,1)S(1)} %collective-permute-done.7.refs_5_), channel_id=1, source_target_pairs={{0,12},{1,13},{2,98},{3,99},{4,0},{5,1},{6,102},{7,103},{8,4},{9,5... | collective-permute-start | bytes 1769480 | tf_op jit(solution)/shard_map/ppermute | solution.py:50
  28.8 2.8 %collective-permute-done.14.refs_2_ = bf16[384,768]{1,0:T(8,128)(2,1)S(1)} collective-permute-done((bf16[384,768]{1,0:T(8,128)(2,1)S(1)}, bf16[384,768]{1,0:T(8,128)(2,1)S(1)}, u32[]{:S(2)}, u32[]{:S(2)}) %collective-permute-start.14) | collective-permute-done | bytes 589856 | tf_op jit(solution)/shard_map/ppermute | solution.py:50
  31.5 6.3 %collective-permute-done.6.refs_4_ = bf16[384,768]{1,0:T(8,128)(2,1)S(1)} collective-permute-done((bf16[384,768]{1,0:T(8,128)(2,1)S(1)}, bf16[384,768]{1,0:T(8,128)(2,1)S(1)}, u32[]{:S(2)}, u32[]{:S(2)}) %collective-permute-start.6) | collective-permute-done | bytes 589856 | tf_op jit(solution)/shard_map/ppermute | solution.py:50
  37.9 0.5 collective-permute-start.16
  38.4 0.1 collective-permute-start.17
  38.5 14.1 %all_to_all.20.part = s32[8,2,192]{2,1,0:T(2,128)S(1)} all-to-all(s32[8,2,192]{2,1,0:T(2,128)S(1)} %get-tuple-element.19), channel_id=1, replica_groups=mesh['x'=4,'h'=2,'z'=4,'c'=2,'l'=2] {'x','h'}, dimensions={0} | all-to-all | bytes 24576 | tf_op jit(solution)/shard_map/all_to_all | solution.py:414
  52.6 9.6 %all_to_all.21.table = s32[8,16,192]{2,1,0:T(8,128)S(1)} all-to-all(s32[8,16,192]{2,1,0:T(8,128)S(1)} %shard_map.68), channel_id=1, replica_groups=mesh['x'=4,'h'=2,'z'=4,'c'=2,'l'=2] {'z','l'}, dimensions={0} | all-to-all | bytes 196608 | tf_op jit(solution)/shard_map/all_to_all | solution.py:419
  62.2 1.0 shard_map.69
  63.2 1.9 %shard_map.70 = (bf16[1984,768]{1,0:T(8,128)(2,1)S(1)}, bf16[3584,768]{1,0:T(8,128)(2,1)S(1)}) custom-call(s32[24,128]{1,0:T(8,128)S(1)} %get-tuple-element.20.counts, f32[8,192]{1,0:T(8,128)S(1)} %get-tuple-element.22.ranks.row_ranks, bf16[384,768]{1,0:T(8,128)(2,1)S(1)} %get-tuple-element.23.refs_0_, bf16[384,768]{1,0:T(8,128)(2,1)S(1)} %collective-permute-done.3.refs_1_, ...), custom_call_target="tpu_custom_call" | custom-call | flops 1000000000 | bytes 1000000 | tf_op jit(solution)/shard_map/pallas_call | solution.py:433
  65.1 1.2 %shard_map.71 = (bf16[1984,768]{1,0:T(8,128)(2,1)S(1)}, bf16[3584,768]{1,0:T(8,128)(2,1)S(1)}) custom-call(s32[24,128]{1,0:T(8,128)S(1)} %get-tuple-element.20.counts, f32[8,192]{1,0:T(8,128)S(1)} %get-tuple-element.22.ranks.row_ranks, bf16[1984,768]{1,0:T(8,128)(2,1)S(1)} %get-tuple-element.24.refs_0_, ...), custom_call_target="tpu_custom_call", output_to_operand_aliasing={{0}: (2, {}), {1}: (3, {})} | custom-call | flops 1000000000 | bytes 1000000 | tf_op jit(solution)/shard_map/pallas_call | solution.py:433
  66.3 7.4 %shard_map.72 = (f32[128,1,384]{2,1,0:T(1,128)S(1)}, f32[1,1,384]{2,1,0:T(1,128)S(1)}) custom-call(s32[24,128]{1,0:T(8,128)S(1)} %get-tuple-element.20.counts, f32[192,128]{1,0:T(8,128)S(1)} %get-tuple-element.21.columns, bf16[1984,768]{1,0:T(8,128)(2,1)S(1)} %get-tuple-element.26.cap_v, bf16[3584,768]{1,0:T(8,128)(2,1)S(1)} %get-tuple-element.27.img_v), custom_call_target="tpu_custom_call" | custom-call | flops 4227858432 | bytes 7471104 | tf_op jit(solution)/shard_map/pallas_call | solution.py:442
  73.6 14.4 %all_to_all.22.parts = f32[128,1,384]{2,1,0:T(1,128)S(1)} all-to-all(f32[128,1,384]{2,1,0:T(1,128)S(1)} %get-tuple-element.28), channel_id=1, replica_groups=mesh['x'=4,'h'=2,'z'=4,'c'=2,'l'=2] {'x','h','z','c','l'}, dimensions={0} | all-to-all | bytes 393216 | tf_op jit(solution)/shard_map/all_to_all | solution.py:460
  88.1 0.9 shard_map.73
  89.0 13.9 %all_to_all.23 = f32[128,1,8]{2,1,0:T(1,128)S(1)} all-to-all(f32[128,1,8]{2,1,0:T(1,128)S(1)} %get-tuple-element.34), channel_id=1, replica_groups=mesh['x'=4,'h'=2,'z'=4,'c'=2,'l'=2] {'x','h','z','c','l'}, dimensions={0} | all-to-all | bytes 8192 | tf_op jit(solution)/shard_map/all_to_all | solution.py:469
  102.9 0.7 slice_reduce_fusion
  (18 shorter events, 0.1 us)
Async XLA Ops:
  0.6 2.5 %collective-permute-start = (bf16[192,768]{1,0:T(8,128)(2,1)}, bf16[192,768]{1,0:T(8,128)(2,1)S(1)}, u32[]{:S(2)}, u32[]{:S(2)}) collective-permute-start(bf16[192,768]{1,0:T(8,128)(2,1)} %param.4), channel_id=1, source_target_pairs={{0,2},{1,3},{2,0},{3,1},{4,6},{5,7},{6,4},{7,5},{8,10},{9,11},{10,... | collective-permute-start | bytes 884744 | tf_op jit(solution)/shard_map/ppermute | solution.py:50
  0.7 2.4 %collective-permute-start.1 = (bf16[192,768]{1,0:T(8,128)(2,1)}, bf16[192,768]{1,0:T(8,128)(2,1)S(1)}, u32[]{:S(2)}, u32[]{:S(2)}) collective-permute-start(bf16[192,768]{1,0:T(8,128)(2,1)} %param.5), channel_id=1, source_target_pairs={{0,2},{1,3},{2,0},{3,1},{4,6},{5,7},{6,4},{7,5},{8,10},{9,11},{10,... | collective-permute-start | bytes 884744 | tf_op jit(solution)/shard_map/ppermute | solution.py:50
  1.9 1.2 %collective-permute-start.2 = (s32[1,192]{1,0:T(1,128)S(1)}, s32[1,192]{1,0:T(1,128)S(1)}, u32[]{:S(2)}, u32[]{:S(2)}) collective-permute-start(s32[1,192]{1,0:T(1,128)S(1)} %bitcast.3), channel_id=1, source_target_pairs={{0,2},{1,3},{2,0},{3,1},{4,6},{5,7},{6,4},{7,5},{8,10},{9,11},{10,... | collective-permute-start | bytes 2312 | tf_op jit(solution)/shard_map/ppermute | solution.py:50
  3.5 10.0 %collective-permute-start.3 = (bf16[384,768]{1,0:T(8,128)(2,1)S(1)}, bf16[384,768]{1,0:T(8,128)(2,1)S(1)}, u32[]{:S(2)}, u32[]{:S(2)}) collective-permute-start(bf16[384,768]{1,0:T(8,128)(2,1)S(1)} %get-tuple-element.23.refs_0_), channel_id=1, source_target_pairs={{0,1},{1,0},{2,19},{3,18},{4,5},{5,4},{6,23},{7,22},{8,9},{9,8},{1... | collective-permute-start | bytes 1769480 | tf_op jit(solution)/shard_map/ppermute | solution.py:50
  5.3 12.4 %collective-permute-start.5 = (bf16[384,768]{1,0:T(8,128)(2,1)S(1)}, bf16[384,768]{1,0:T(8,128)(2,1)S(1)}, u32[]{:S(2)}, u32[]{:S(2)}) collective-permute-start(bf16[384,768]{1,0:T(8,128)(2,1)S(1)} %get-tuple-element.23.refs_0_), channel_id=1, source_target_pairs={{0,12},{1,13},{2,98},{3,99},{4,0},{5,1},{6,102},{7,103},{8,4},{9,5... | collective-permute-start | bytes 1769480 | tf_op jit(solution)/shard_map/ppermute | solution.py:50
  9.3 11.1 %collective-permute-start.4 = (bf16[384,768]{1,0:T(8,128)(2,1)S(1)}, bf16[384,768]{1,0:T(8,128)(2,1)S(1)}, u32[]{:S(2)}, u32[]{:S(2)}) collective-permute-start(bf16[384,768]{1,0:T(8,128)(2,1)S(1)} %get-tuple-element.23.refs_0_), channel_id=1, source_target_pairs={{0,4},{1,5},{2,34},{3,35},{4,8},{5,9},{6,38},{7,39},{8,12},{9,13},... | collective-permute-start | bytes 1769480 | tf_op jit(solution)/shard_map/ppermute | solution.py:50
  9.4 11.1 %collective-permute-start.8 = (bf16[384,768]{1,0:T(8,128)(2,1)S(1)}, bf16[384,768]{1,0:T(8,128)(2,1)S(1)}, u32[]{:S(2)}, u32[]{:S(2)}) collective-permute-start(bf16[384,768]{1,0:T(8,128)(2,1)S(1)} %get-tuple-element.23.refs_0_), channel_id=1, source_target_pairs={{0,2},{1,3},{2,0},{3,1},{4,6},{5,7},{6,4},{7,5},{8,10},{9,11},{10,... | collective-permute-start | bytes 1769480 | tf_op jit(solution)/shard_map/ppermute | solution.py:50
  13.5 11.6 %collective-permute-start.7 = (bf16[384,768]{1,0:T(8,128)(2,1)S(1)}, bf16[384,768]{1,0:T(8,128)(2,1)S(1)}, u32[]{:S(2)}, u32[]{:S(2)}) collective-permute-start(bf16[384,768]{1,0:T(8,128)(2,1)S(1)} %collective-permute-done.3.refs_1_), channel_id=1, source_target_pairs={{0,12},{1,13},{2,98},{3,99},{4,0},{5,1},{6,102},{7,103},{8,4},{9,5... | collective-permute-start | bytes 1769480 | tf_op jit(solution)/shard_map/ppermute | solution.py:50
  17.7 11.1 %collective-permute-start.11 = (bf16[384,768]{1,0:T(8,128)(2,1)S(1)}, bf16[384,768]{1,0:T(8,128)(2,1)S(1)}, u32[]{:S(2)}, u32[]{:S(2)}) collective-permute-start(bf16[384,768]{1,0:T(8,128)(2,1)S(1)} %collective-permute-done.5.refs_3_), channel_id=1, source_target_pairs={{0,2},{1,3},{2,0},{3,1},{4,6},{5,7},{6,4},{7,5},{8,10},{9,11},{10,... | collective-permute-start | bytes 1769480 | tf_op jit(solution)/shard_map/ppermute | solution.py:50
  20.4 11.1 %collective-permute-start.14 = (bf16[384,768]{1,0:T(8,128)(2,1)S(1)}, bf16[384,768]{1,0:T(8,128)(2,1)S(1)}, u32[]{:S(2)}, u32[]{:S(2)}) collective-permute-start(bf16[384,768]{1,0:T(8,128)(2,1)S(1)} %collective-permute-done.4.refs_2_), channel_id=1, source_target_pairs={{0,4},{1,5},{2,34},{3,35},{4,8},{5,9},{6,38},{7,39},{8,12},{9,13},... | collective-permute-start | bytes 1769480 | tf_op jit(solution)/shard_map/ppermute | solution.py:50
  20.4 17.4 %collective-permute-start.6 = (bf16[384,768]{1,0:T(8,128)(2,1)S(1)}, bf16[384,768]{1,0:T(8,128)(2,1)S(1)}, u32[]{:S(2)}, u32[]{:S(2)}) collective-permute-start(bf16[384,768]{1,0:T(8,128)(2,1)S(1)} %collective-permute-done.3.refs_1_), channel_id=1, source_target_pairs={{0,4},{1,5},{2,34},{3,35},{4,8},{5,9},{6,38},{7,39},{8,12},{9,13},... | collective-permute-start | bytes 1769480 | tf_op jit(solution)/shard_map/ppermute | solution.py:50
  20.5 17.4 %collective-permute-start.10 = (bf16[384,768]{1,0:T(8,128)(2,1)S(1)}, bf16[384,768]{1,0:T(8,128)(2,1)S(1)}, u32[]{:S(2)}, u32[]{:S(2)}) collective-permute-start(bf16[384,768]{1,0:T(8,128)(2,1)S(1)} %collective-permute-done.4.refs_2_), channel_id=1, source_target_pairs={{0,2},{1,3},{2,0},{3,1},{4,6},{5,7},{6,4},{7,5},{8,10},{9,11},{10,... | collective-permute-start | bytes 1769480 | tf_op jit(solution)/shard_map/ppermute | solution.py:50
  25.1 13.3 %collective-permute-start.15 = (bf16[384,768]{1,0:T(8,128)(2,1)S(1)}, bf16[384,768]{1,0:T(8,128)(2,1)S(1)}, u32[]{:S(2)}, u32[]{:S(2)}) collective-permute-start(bf16[384,768]{1,0:T(8,128)(2,1)S(1)} %collective-permute-done.7.refs_5_), channel_id=1, source_target_pairs={{0,12},{1,13},{2,98},{3,99},{4,0},{5,1},{6,102},{7,103},{8,4},{9,5... | collective-permute-start | bytes 1769480 | tf_op jit(solution)/shard_map/ppermute | solution.py:50
  28.8 34.4 %collective-permute-start.9 = (bf16[384,768]{1,0:T(8,128)(2,1)S(1)}, bf16[384,768]{1,0:T(8,128)(2,1)S(1)}, u32[]{:S(2)}, u32[]{:S(2)}) collective-permute-start(bf16[384,768]{1,0:T(8,128)(2,1)S(1)} %collective-permute-done.3.refs_1_), channel_id=1, source_target_pairs={{0,2},{1,3},{2,0},{3,1},{4,6},{5,7},{6,4},{7,5},{8,10},{9,11},{10,... | collective-permute-start | bytes 1769480 | tf_op jit(solution)/shard_map/ppermute | solution.py:50
  31.5 31.7 %collective-permute-start.13 = (bf16[384,768]{1,0:T(8,128)(2,1)S(1)}, bf16[384,768]{1,0:T(8,128)(2,1)S(1)}, u32[]{:S(2)}, u32[]{:S(2)}) collective-permute-start(bf16[384,768]{1,0:T(8,128)(2,1)S(1)} %collective-permute-done.7.refs_5_), channel_id=1, source_target_pairs={{0,2},{1,3},{2,0},{3,1},{4,6},{5,7},{6,4},{7,5},{8,10},{9,11},{10,... | collective-permute-start | bytes 1769480 | tf_op jit(solution)/shard_map/ppermute | solution.py:50
  37.9 25.4 %collective-permute-start.12 = (bf16[384,768]{1,0:T(8,128)(2,1)S(1)}, bf16[384,768]{1,0:T(8,128)(2,1)S(1)}, u32[]{:S(2)}, u32[]{:S(2)}) collective-permute-start(bf16[384,768]{1,0:T(8,128)(2,1)S(1)} %collective-permute-done.6.refs_4_), channel_id=1, source_target_pairs={{0,2},{1,3},{2,0},{3,1},{4,6},{5,7},{6,4},{7,5},{8,10},{9,11},{10,... | collective-permute-start | bytes 1769480 | tf_op jit(solution)/shard_map/ppermute | solution.py:50
  37.9 27.2 %collective-permute-start.16 = (bf16[384,768]{1,0:T(8,128)(2,1)S(1)}, bf16[384,768]{1,0:T(8,128)(2,1)S(1)}, u32[]{:S(2)}, u32[]{:S(2)}) collective-permute-start(bf16[384,768]{1,0:T(8,128)(2,1)S(1)} %collective-permute-done.14.refs_2_), channel_id=1, source_target_pairs={{0,2},{1,3},{2,0},{3,1},{4,6},{5,7},{6,4},{7,5},{8,10},{9,11},{10,... | collective-permute-start | bytes 1769480 | tf_op jit(solution)/shard_map/ppermute | solution.py:50
  38.4 26.7 %collective-permute-start.17 = (bf16[384,768]{1,0:T(8,128)(2,1)S(1)}, bf16[384,768]{1,0:T(8,128)(2,1)S(1)}, u32[]{:S(2)}, u32[]{:S(2)}) collective-permute-start(bf16[384,768]{1,0:T(8,128)(2,1)S(1)} %collective-permute-done.15.refs_3_), channel_id=1, source_target_pairs={{0,2},{1,3},{2,0},{3,1},{4,6},{5,7},{6,4},{7,5},{8,10},{9,11},{10,... | collective-permute-start | bytes 1769480 | tf_op jit(solution)/shard_map/ppermute | solution.py:50

commit v7 on v6

--- a/solution.py
+++ b/solution.py
@@ -19,7 +19,8 @@
 B = 192
 E = 768
 MET = ((0, 0), (0, 1), (3, 0), (1, 0), (3, 1), (1, 1), (2, 0), (2, 1))
-PARTS = ((0, 6), (6, 8))
+PARTS = ((0, 4), (4, 7))
+LATE = PARTS[-1][1]
 CAPS = len(MET)
 IMGS = 2 * len(MET)
 C = IMGS * B
@@ -229,9 +230,11 @@
 
 
 def score_kernel(
-    counts, columns, cap_v, img_v, out, own_row,
+    counts, columns, ranks, cap_in, img_in, carried, swapped, out, own_row, cap_v, img_v,
     t_v, pos_b, bias_b, rmax, rmatch, rsum, col_bias, cmax, cmatch, csum, lines_v, row_lines,
 ):
+    del cap_in, img_in
+    compact(counts, ranks, [carried], [swapped], cap_v, img_v, LATE)
     img_at = starts_of(counts, CAPS, IMGS)
     col_bias[...] = jnp.full((8, C + 384), LOW, F32)
     column = iota((8, 384), 1)
@@ -438,12 +441,15 @@
             input_output_aliases={2: 0, 3: 1} if part else {},
             **small(10, 10**9),
         )(counts, ranks, *buffers, *carried[first:last], *swapped[first:last])
-    cap_v, img_v = buffers
-    out, own_row = pl.pallas_call(
+    out, own_row, _, _ = pl.pallas_call(
         score_kernel,
-        out_shape=[shape((n, 1, 2 * B), F32) for n in (128, 1)],
-        in_specs=[SMEM] + [VMEM] * 3,
-        out_specs=[VMEM] * 2,
+        out_shape=[
+            *(shape((n, 1, 2 * B), F32) for n in (128, 1)),
+            shape((CAP_ROWS, E), BF16), shape((IMG_ROWS, E), BF16),
+        ],
+        in_specs=[SMEM] + [VMEM] * 6,
+        out_specs=[VMEM] * 4,
+        input_output_aliases={3: 2, 4: 3},
         scratch_shapes=[
             pltpu.VMEM((R, C), F32),
             *[pltpu.VMEM((R + RC, 128), F32)] * 5,
@@ -456,7 +462,7 @@
         cost_estimate=pl.CostEstimate(
             flops=R * C * E, bytes_accessed=2 * (R + C) * E, transcendentals=R * C
         ),
-    )(counts, columns, cap_v, img_v)
+    )(counts, columns, ranks, *buffers, carried[LATE], swapped[LATE])
     parts = lax.all_to_all(out, AXES, 0, 0, tiled=True)
     caption_loss, image_loss, total = pl.pallas_call(
         loss_kernel,

time: 105 us -> 105 us (level)
  waiting for transfers between devices: 20.6 us -> 15.3 us
  starting transfers between devices: 15.1 us -> 18.1 us
  blocking collectives: 52 us -> 54.4 us
    ppermute x18, waiting for transfers between devices: 20.6 us -> 15.3 us  [send(): return lax.ppermute(value, AXES, pairs)]
    ppermute x18, starting transfers between devices: 15.1 us -> 18.1 us  [send(): return lax.ppermute(value, AXES, pairs)]
    all_to_all x1, blocking collectives: 9.57 us -> 11.6 us  [step(): table = lax.all_to_all(part, ('z', 'l'), 0, 0, tiled=True)]
  transfers between devices with their start and end apart: 18 -> 18, of which waited for: 6 -> 5; matrix products, arithmetic and copies ran while one was open for 2% -> 2% of each run, Pallas kernels for 3% -> 4%
where the time goes in v7:
time: 105 us; the launch traced here: 104 us
  blocking collectives  54.4 us (52%)
  starting transfers between devices  18.1 us (17%)
  waiting for transfers between devices  15.3 us (15%)
  Pallas kernels  12.6 us (12%)
  other arithmetic  2.43 us (2%)
    ppermute x18, starting transfers between devices, send(): return lax.ppermute(value, AXES, pairs)  18.1 us
    ppermute x18, waiting for transfers between devices, send(): return lax.ppermute(value, AXES, pairs)  15.3 us
    all_to_all x1, blocking collectives, step(): parts = lax.all_to_all(out, AXES, 0, 0, tiled=True)  14.5 us
    all_to_all x1, blocking collectives, step(): part = lax.all_to_all(words, ('x', 'h'), 0, 0, tiled=True)  14.4 us
    all_to_all x1, blocking collectives, step(): totals = lax.all_to_all(total, AXES, 0, 0, tiled=True)  13.9 us
    all_to_all x1, blocking collectives, step(): table = lax.all_to_all(part, ('z', 'l'), 0, 0, tiled=True)  11.6 us
    pallas_call x1, Pallas kernels, step(): pl.pallas_call(score_kernel, out_shape=[*(shape((n, 1, 2 * B), F32) for n...  7.47 us
    pallas_call x2, Pallas kernels, step(): pl.pallas_call(functools.partial(compact_kernel, part), out_shape=[shape(...  2.76 us
  transfers between devices with their start and end apart: 18, of which 5 were waited for; matrix products, arithmetic and copies ran while one was open for 2% of the time, Pallas kernels for 4%

profile of v7, /device:TPU:0, one launch (start us, length us, event | category | flops | bytes accessed | tf_op | source)
XLA Modules:
  0.0 103.5 jit_solution(10633953855347299346)
XLA Ops:
  0.6 0.1 collective-permute-start
  0.7 0.5 collective-permute-start.1
  1.2 0.7 multiply_add_fusion
  1.9 0.1 collective-permute-start.2
  2.0 1.0 broadcast_select_fusion.own
  3.0 0.1 collective-permute-done.2.word_other
  3.1 0.4 shard_map.67
  3.5 1.8 %collective-permute-start.3 = (bf16[384,768]{1,0:T(8,128)(2,1)S(1)}, bf16[384,768]{1,0:T(8,128)(2,1)S(1)}, u32[]{:S(2)}, u32[]{:S(2)}) collective-permute-start(bf16[384,768]{1,0:T(8,128)(2,1)S(1)} %get-tuple-element.23.refs_0_), channel_id=1, source_target_pairs={{0,1},{1,0},{2,19},{3,18},{4,5},{5,4},{6,23},{7,22},{8,9},{9,8},{1... | collective-permute-start | bytes 1769480 | tf_op jit(solution)/shard_map/ppermute | solution.py:51
  5.3 1.9 %collective-permute-start.4 = (bf16[384,768]{1,0:T(8,128)(2,1)S(1)}, bf16[384,768]{1,0:T(8,128)(2,1)S(1)}, u32[]{:S(2)}, u32[]{:S(2)}) collective-permute-start(bf16[384,768]{1,0:T(8,128)(2,1)S(1)} %get-tuple-element.23.refs_0_), channel_id=1, source_target_pairs={{0,4},{1,5},{2,34},{3,35},{4,8},{5,9},{6,38},{7,39},{8,12},{9,13},... | collective-permute-start | bytes 1769480 | tf_op jit(solution)/shard_map/ppermute | solution.py:51
  7.2 2.1 %collective-permute-start.5 = (bf16[384,768]{1,0:T(8,128)(2,1)S(1)}, bf16[384,768]{1,0:T(8,128)(2,1)S(1)}, u32[]{:S(2)}, u32[]{:S(2)}) collective-permute-start(bf16[384,768]{1,0:T(8,128)(2,1)S(1)} %get-tuple-element.23.refs_0_), channel_id=1, source_target_pairs={{0,12},{1,13},{2,98},{3,99},{4,0},{5,1},{6,102},{7,103},{8,4},{9,5... | collective-permute-start | bytes 1769480 | tf_op jit(solution)/shard_map/ppermute | solution.py:51
  9.4 0.2 collective-permute-start.6
  9.5 4.0 %collective-permute-done.3.refs_1_ = bf16[384,768]{1,0:T(8,128)(2,1)S(1)} collective-permute-done((bf16[384,768]{1,0:T(8,128)(2,1)S(1)}, bf16[384,768]{1,0:T(8,128)(2,1)S(1)}, u32[]{:S(2)}, u32[]{:S(2)}) %collective-permute-start.3) | collective-permute-done | bytes 589856 | tf_op jit(solution)/shard_map/ppermute | solution.py:51
  13.5 4.2 %collective-permute-start.11 = (bf16[384,768]{1,0:T(8,128)(2,1)S(1)}, bf16[384,768]{1,0:T(8,128)(2,1)S(1)}, u32[]{:S(2)}, u32[]{:S(2)}) collective-permute-start(bf16[384,768]{1,0:T(8,128)(2,1)S(1)} %collective-permute-done.3.refs_1_), channel_id=1, source_target_pairs={{0,12},{1,13},{2,98},{3,99},{4,0},{5,1},{6,102},{7,103},{8,4},{9,5... | collective-permute-start | bytes 1769480 | tf_op jit(solution)/shard_map/ppermute | solution.py:51
  17.7 0.5 collective-permute-start.8
  18.2 0.8 collective-permute-start.10
  19.0 1.6 %collective-permute-start.12 = (bf16[384,768]{1,0:T(8,128)(2,1)S(1)}, bf16[384,768]{1,0:T(8,128)(2,1)S(1)}, u32[]{:S(2)}, u32[]{:S(2)}) collective-permute-start(bf16[384,768]{1,0:T(8,128)(2,1)S(1)} %collective-permute-done.4.refs_2_), channel_id=1, source_target_pairs={{0,4},{1,5},{2,34},{3,35},{4,8},{5,9},{6,38},{7,39},{8,12},{9,13},... | collective-permute-start | bytes 1769480 | tf_op jit(solution)/shard_map/ppermute | solution.py:51
  20.7 4.4 %collective-permute-done.11.refs_3_ = bf16[384,768]{1,0:T(8,128)(2,1)S(1)} collective-permute-done((bf16[384,768]{1,0:T(8,128)(2,1)S(1)}, bf16[384,768]{1,0:T(8,128)(2,1)S(1)}, u32[]{:S(2)}, u32[]{:S(2)}) %collective-permute-start.11) | collective-permute-done | bytes 589856 | tf_op jit(solution)/shard_map/ppermute | solution.py:51
  25.1 3.7 %collective-permute-start.16 = (bf16[384,768]{1,0:T(8,128)(2,1)S(1)}, bf16[384,768]{1,0:T(8,128)(2,1)S(1)}, u32[]{:S(2)}, u32[]{:S(2)}) collective-permute-start(bf16[384,768]{1,0:T(8,128)(2,1)S(1)} %collective-permute-done.11.refs_3_), channel_id=1, source_target_pairs={{0,12},{1,13},{2,98},{3,99},{4,0},{5,1},{6,102},{7,103},{8,4},{9,5... | collective-permute-start | bytes 1769480 | tf_op jit(solution)/shard_map/ppermute | solution.py:51
  28.8 0.5 collective-permute-start.14
  29.3 0.1 collective-permute-start.13
  29.4 6.2 %collective-permute-done.12.refs_4_ = bf16[384,768]{1,0:T(8,128)(2,1)S(1)} collective-permute-done((bf16[384,768]{1,0:T(8,128)(2,1)S(1)}, bf16[384,768]{1,0:T(8,128)(2,1)S(1)}, u32[]{:S(2)}, u32[]{:S(2)}) %collective-permute-start.12) | collective-permute-done | bytes 589856 | tf_op jit(solution)/shard_map/ppermute | solution.py:51
  35.6 0.6 collective-permute-done.16.carried
  36.2 14.4 %all_to_all.20.part = s32[8,2,192]{2,1,0:T(2,128)S(1)} all-to-all(s32[8,2,192]{2,1,0:T(2,128)S(1)} %get-tuple-element.19), channel_id=1, replica_groups=mesh['x'=4,'h'=2,'z'=4,'c'=2,'l'=2] {'x','h'}, dimensions={0} | all-to-all | bytes 24576 | tf_op jit(solution)/shard_map/all_to_all | solution.py:417
  50.6 11.6 %all_to_all.21.table = s32[8,16,192]{2,1,0:T(8,128)S(1)} all-to-all(s32[8,16,192]{2,1,0:T(8,128)S(1)} %shard_map.68), channel_id=1, replica_groups=mesh['x'=4,'h'=2,'z'=4,'c'=2,'l'=2] {'z','l'}, dimensions={0} | all-to-all | bytes 196608 | tf_op jit(solution)/shard_map/all_to_all | solution.py:422
  62.2 1.0 shard_map.69
  63.2 1.5 %shard_map.70 = (bf16[1984,768]{1,0:T(8,128)(2,1)S(1)}, bf16[3584,768]{1,0:T(8,128)(2,1)S(1)}) custom-call(s32[24,128]{1,0:T(8,128)S(1)} %get-tuple-element.20.counts, f32[8,192]{1,0:T(8,128)S(1)} %get-tuple-element.22.ranks.row_ranks, bf16[384,768]{1,0:T(8,128)(2,1)S(1)} %get-tuple-element.23.refs_0_, bf16[384,768]{1,0:T(8,128)(2,1)S(1)} %collective-permute-done.3.refs_1_, ...), custom_call_target="tpu_custom_call" | custom-call | flops 1000000000 | bytes 1000000 | tf_op jit(solution)/shard_map/pallas_call | solution.py:436
  64.7 1.3 %shard_map.71 = (bf16[1984,768]{1,0:T(8,128)(2,1)S(1)}, bf16[3584,768]{1,0:T(8,128)(2,1)S(1)}) custom-call(s32[24,128]{1,0:T(8,128)S(1)} %get-tuple-element.20.counts, f32[8,192]{1,0:T(8,128)S(1)} %get-tuple-element.22.ranks.row_ranks, bf16[1984,768]{1,0:T(8,128)(2,1)S(1)} %get-tuple-element.24.refs_0_, ...), custom_call_target="tpu_custom_call", output_to_operand_aliasing={{0}: (2, {}), {1}: (3, {})} | custom-call | flops 1000000000 | bytes 1000000 | tf_op jit(solution)/shard_map/pallas_call | solution.py:436
  66.0 7.5 %shard_map.72 = (f32[128,1,384]{2,1,0:T(1,128)S(1)}, f32[1,1,384]{2,1,0:T(1,128)S(1)}, bf16[1984,768]{1,0:T(8,128)(2,1)S(1)}, bf16[3584,768]{1,0:T(8,128)(2,1)S(1)}) custom-call(s32[24,128]{1,0:T(8,128)S(1)} %get-tuple-element.20.counts, f32[192,128]{1,0:T(8,128)S(1)} %get-tuple-element.21.columns, ...), custom_call_target="tpu_custom_call", output_to_operand_aliasing={{2}: (3, {}), {3}: (4, {})} | custom-call | flops 4227858432 | bytes 7471104 | tf_op jit(solution)/shard_map/pallas_call | solution.py:444
  73.5 14.5 %all_to_all.22.parts = f32[128,1,384]{2,1,0:T(1,128)S(1)} all-to-all(f32[128,1,384]{2,1,0:T(1,128)S(1)} %get-tuple-element.28), channel_id=1, replica_groups=mesh['x'=4,'h'=2,'z'=4,'c'=2,'l'=2] {'x','h','z','c','l'}, dimensions={0} | all-to-all | bytes 393216 | tf_op jit(solution)/shard_map/all_to_all | solution.py:466
  88.0 0.9 shard_map.73
  88.9 13.9 %all_to_all.23 = f32[128,1,8]{2,1,0:T(1,128)S(1)} all-to-all(f32[128,1,8]{2,1,0:T(1,128)S(1)} %get-tuple-element.34), channel_id=1, replica_groups=mesh['x'=4,'h'=2,'z'=4,'c'=2,'l'=2] {'x','h','z','c','l'}, dimensions={0} | all-to-all | bytes 8192 | tf_op jit(solution)/shard_map/all_to_all | solution.py:475
  102.8 0.7 slice_reduce_fusion
  (18 shorter events, 0.1 us)
Async XLA Ops:
  0.6 2.5 %collective-permute-start = (bf16[192,768]{1,0:T(8,128)(2,1)}, bf16[192,768]{1,0:T(8,128)(2,1)S(1)}, u32[]{:S(2)}, u32[]{:S(2)}) collective-permute-start(bf16[192,768]{1,0:T(8,128)(2,1)} %param.4), channel_id=1, source_target_pairs={{0,2},{1,3},{2,0},{3,1},{4,6},{5,7},{6,4},{7,5},{8,10},{9,11},{10,... | collective-permute-start | bytes 884744 | tf_op jit(solution)/shard_map/ppermute | solution.py:51
  0.7 2.4 %collective-permute-start.1 = (bf16[192,768]{1,0:T(8,128)(2,1)}, bf16[192,768]{1,0:T(8,128)(2,1)S(1)}, u32[]{:S(2)}, u32[]{:S(2)}) collective-permute-start(bf16[192,768]{1,0:T(8,128)(2,1)} %param.5), channel_id=1, source_target_pairs={{0,2},{1,3},{2,0},{3,1},{4,6},{5,7},{6,4},{7,5},{8,10},{9,11},{10,... | collective-permute-start | bytes 884744 | tf_op jit(solution)/shard_map/ppermute | solution.py:51
  1.9 1.2 %collective-permute-start.2 = (s32[1,192]{1,0:T(1,128)S(1)}, s32[1,192]{1,0:T(1,128)S(1)}, u32[]{:S(2)}, u32[]{:S(2)}) collective-permute-start(s32[1,192]{1,0:T(1,128)S(1)} %bitcast.3), channel_id=1, source_target_pairs={{0,2},{1,3},{2,0},{3,1},{4,6},{5,7},{6,4},{7,5},{8,10},{9,11},{10,... | collective-permute-start | bytes 2312 | tf_op jit(solution)/shard_map/ppermute | solution.py:51
  3.5 10.0 %collective-permute-start.3 = (bf16[384,768]{1,0:T(8,128)(2,1)S(1)}, bf16[384,768]{1,0:T(8,128)(2,1)S(1)}, u32[]{:S(2)}, u32[]{:S(2)}) collective-permute-start(bf16[384,768]{1,0:T(8,128)(2,1)S(1)} %get-tuple-element.23.refs_0_), channel_id=1, source_target_pairs={{0,1},{1,0},{2,19},{3,18},{4,5},{5,4},{6,23},{7,22},{8,9},{9,8},{1... | collective-permute-start | bytes 1769480 | tf_op jit(solution)/shard_map/ppermute | solution.py:51
  5.3 12.4 %collective-permute-start.4 = (bf16[384,768]{1,0:T(8,128)(2,1)S(1)}, bf16[384,768]{1,0:T(8,128)(2,1)S(1)}, u32[]{:S(2)}, u32[]{:S(2)}) collective-permute-start(bf16[384,768]{1,0:T(8,128)(2,1)S(1)} %get-tuple-element.23.refs_0_), channel_id=1, source_target_pairs={{0,4},{1,5},{2,34},{3,35},{4,8},{5,9},{6,38},{7,39},{8,12},{9,13},... | collective-permute-start | bytes 1769480 | tf_op jit(solution)/shard_map/ppermute | solution.py:51
  7.2 10.9 %collective-permute-start.5 = (bf16[384,768]{1,0:T(8,128)(2,1)S(1)}, bf16[384,768]{1,0:T(8,128)(2,1)S(1)}, u32[]{:S(2)}, u32[]{:S(2)}) collective-permute-start(bf16[384,768]{1,0:T(8,128)(2,1)S(1)} %get-tuple-element.23.refs_0_), channel_id=1, source_target_pairs={{0,12},{1,13},{2,98},{3,99},{4,0},{5,1},{6,102},{7,103},{8,4},{9,5... | collective-permute-start | bytes 1769480 | tf_op jit(solution)/shard_map/ppermute | solution.py:51
  9.4 9.7 %collective-permute-start.6 = (bf16[384,768]{1,0:T(8,128)(2,1)S(1)}, bf16[384,768]{1,0:T(8,128)(2,1)S(1)}, u32[]{:S(2)}, u32[]{:S(2)}) collective-permute-start(bf16[384,768]{1,0:T(8,128)(2,1)S(1)} %get-tuple-element.23.refs_0_), channel_id=1, source_target_pairs={{0,2},{1,3},{2,0},{3,1},{4,6},{5,7},{6,4},{7,5},{8,10},{9,11},{10,... | collective-permute-start | bytes 1769480 | tf_op jit(solution)/shard_map/ppermute | solution.py:51
  13.5 11.6 %collective-permute-start.11 = (bf16[384,768]{1,0:T(8,128)(2,1)S(1)}, bf16[384,768]{1,0:T(8,128)(2,1)S(1)}, u32[]{:S(2)}, u32[]{:S(2)}) collective-permute-start(bf16[384,768]{1,0:T(8,128)(2,1)S(1)} %collective-permute-done.3.refs_1_), channel_id=1, source_target_pairs={{0,12},{1,13},{2,98},{3,99},{4,0},{5,1},{6,102},{7,103},{8,4},{9,5... | collective-permute-start | bytes 1769480 | tf_op jit(solution)/shard_map/ppermute | solution.py:51
  17.7 11.1 %collective-permute-start.7 = (bf16[384,768]{1,0:T(8,128)(2,1)S(1)}, bf16[384,768]{1,0:T(8,128)(2,1)S(1)}, u32[]{:S(2)}, u32[]{:S(2)}) collective-permute-start(bf16[384,768]{1,0:T(8,128)(2,1)S(1)} %collective-permute-done.3.refs_1_), channel_id=1, source_target_pairs={{0,2},{1,3},{2,0},{3,1},{4,6},{5,7},{6,4},{7,5},{8,10},{9,11},{10,... | collective-permute-start | bytes 1769480 | tf_op jit(solution)/shard_map/ppermute | solution.py:51
  17.7 11.1 %collective-permute-start.8 = (bf16[384,768]{1,0:T(8,128)(2,1)S(1)}, bf16[384,768]{1,0:T(8,128)(2,1)S(1)}, u32[]{:S(2)}, u32[]{:S(2)}) collective-permute-start(bf16[384,768]{1,0:T(8,128)(2,1)S(1)} %collective-permute-done.4.refs_2_), channel_id=1, source_target_pairs={{0,2},{1,3},{2,0},{3,1},{4,6},{5,7},{6,4},{7,5},{8,10},{9,11},{10,... | collective-permute-start | bytes 1769480 | tf_op jit(solution)/shard_map/ppermute | solution.py:51
  18.2 11.1 %collective-permute-start.10 = (bf16[384,768]{1,0:T(8,128)(2,1)S(1)}, bf16[384,768]{1,0:T(8,128)(2,1)S(1)}, u32[]{:S(2)}, u32[]{:S(2)}) collective-permute-start(bf16[384,768]{1,0:T(8,128)(2,1)S(1)} %collective-permute-done.3.refs_1_), channel_id=1, source_target_pairs={{0,4},{1,5},{2,34},{3,35},{4,8},{5,9},{6,38},{7,39},{8,12},{9,13},... | collective-permute-start | bytes 1769480 | tf_op jit(solution)/shard_map/ppermute | solution.py:51
  19.0 16.6 %collective-permute-start.12 = (bf16[384,768]{1,0:T(8,128)(2,1)S(1)}, bf16[384,768]{1,0:T(8,128)(2,1)S(1)}, u32[]{:S(2)}, u32[]{:S(2)}) collective-permute-start(bf16[384,768]{1,0:T(8,128)(2,1)S(1)} %collective-permute-done.4.refs_2_), channel_id=1, source_target_pairs={{0,4},{1,5},{2,34},{3,35},{4,8},{5,9},{6,38},{7,39},{8,12},{9,13},... | collective-permute-start | bytes 1769480 | tf_op jit(solution)/shard_map/ppermute | solution.py:51
  25.1 11.1 %collective-permute-start.16 = (bf16[384,768]{1,0:T(8,128)(2,1)S(1)}, bf16[384,768]{1,0:T(8,128)(2,1)S(1)}, u32[]{:S(2)}, u32[]{:S(2)}) collective-permute-start(bf16[384,768]{1,0:T(8,128)(2,1)S(1)} %collective-permute-done.11.refs_3_), channel_id=1, source_target_pairs={{0,12},{1,13},{2,98},{3,99},{4,0},{5,1},{6,102},{7,103},{8,4},{9,5... | collective-permute-start | bytes 1769480 | tf_op jit(solution)/shard_map/ppermute | solution.py:51
  28.8 34.4 %collective-permute-start.9 = (bf16[384,768]{1,0:T(8,128)(2,1)S(1)}, bf16[384,768]{1,0:T(8,128)(2,1)S(1)}, u32[]{:S(2)}, u32[]{:S(2)}) collective-permute-start(bf16[384,768]{1,0:T(8,128)(2,1)S(1)} %collective-permute-done.5.refs_3_), channel_id=1, source_target_pairs={{0,2},{1,3},{2,0},{3,1},{4,6},{5,7},{6,4},{7,5},{8,10},{9,11},{10,... | collective-permute-start | bytes 1769480 | tf_op jit(solution)/shard_map/ppermute | solution.py:51
  28.8 35.9 %collective-permute-start.14 = (bf16[384,768]{1,0:T(8,128)(2,1)S(1)}, bf16[384,768]{1,0:T(8,128)(2,1)S(1)}, u32[]{:S(2)}, u32[]{:S(2)}) collective-permute-start(bf16[384,768]{1,0:T(8,128)(2,1)S(1)} %collective-permute-done.11.refs_3_), channel_id=1, source_target_pairs={{0,2},{1,3},{2,0},{3,1},{4,6},{5,7},{6,4},{7,5},{8,10},{9,11},{10,... | collective-permute-start | bytes 1769480 | tf_op jit(solution)/shard_map/ppermute | solution.py:51
  29.3 35.4 %collective-permute-start.13 = (bf16[384,768]{1,0:T(8,128)(2,1)S(1)}, bf16[384,768]{1,0:T(8,128)(2,1)S(1)}, u32[]{:S(2)}, u32[]{:S(2)}) collective-permute-start(bf16[384,768]{1,0:T(8,128)(2,1)S(1)} %collective-permute-done.10.refs_2_), channel_id=1, source_target_pairs={{0,2},{1,3},{2,0},{3,1},{4,6},{5,7},{6,4},{7,5},{8,10},{9,11},{10,... | collective-permute-start | bytes 1769480 | tf_op jit(solution)/shard_map/ppermute | solution.py:51
  35.6 29.1 %collective-permute-start.15 = (bf16[384,768]{1,0:T(8,128)(2,1)S(1)}, bf16[384,768]{1,0:T(8,128)(2,1)S(1)}, u32[]{:S(2)}, u32[]{:S(2)}) collective-permute-start(bf16[384,768]{1,0:T(8,128)(2,1)S(1)} %collective-permute-done.12.refs_4_), channel_id=1, source_target_pairs={{0,2},{1,3},{2,0},{3,1},{4,6},{5,7},{6,4},{7,5},{8,10},{9,11},{10,... | collective-permute-start | bytes 1769480 | tf_op jit(solution)/shard_map/ppermute | solution.py:51
  36.2 29.8 %collective-permute-start.17 = (bf16[384,768]{1,0:T(8,128)(2,1)S(1)}, bf16[384,768]{1,0:T(8,128)(2,1)S(1)}, u32[]{:S(2)}, u32[]{:S(2)}) collective-permute-start(bf16[384,768]{1,0:T(8,128)(2,1)S(1)} %collective-permute-done.16.carried), channel_id=1, source_target_pairs={{0,2},{1,3},{2,0},{3,1},{4,6},{5,7},{6,4},{7,5},{8,10},{9,11},{10,... | collective-permute-start | bytes 1769480 | tf_op jit(solution)/shard_map/ppermute | solution.py:51

commit v8 on v7

--- a/solution.py
+++ b/solution.py
@@ -19,7 +19,7 @@
 B = 192
 E = 768
 MET = ((0, 0), (0, 1), (3, 0), (1, 0), (3, 1), (1, 1), (2, 0), (2, 1))
-PARTS = ((0, 4), (4, 7))
+PARTS = ((0, 4), (4, 6))
 LATE = PARTS[-1][1]
 CAPS = len(MET)
 IMGS = 2 * len(MET)
@@ -31,7 +31,7 @@
 COUNTS = (2, 4, 5, 6, 7, 8, 10, 12)
 TAIL = 2 * NC
 IMG_ROWS = C + TAIL
-PIECE = 32
+PIECE = 64
 SPAN = 7 * 128
 GRAIN = 16
 OK_BIT = 15
@@ -230,11 +230,12 @@
 
 
 def score_kernel(
-    counts, columns, ranks, cap_in, img_in, carried, swapped, out, own_row, cap_v, img_v,
+    counts, columns, ranks, cap_in, img_in, c1, c3, c1_other, c3_other,
+    out, own_row, cap_v, img_v,
     t_v, pos_b, bias_b, rmax, rmatch, rsum, col_bias, cmax, cmatch, csum, lines_v, row_lines,
 ):
     del cap_in, img_in
-    compact(counts, ranks, [carried], [swapped], cap_v, img_v, LATE)
+    compact(counts, ranks, [c1, c3], [c1_other, c3_other], cap_v, img_v, LATE)
     img_at = starts_of(counts, CAPS, IMGS)
     col_bias[...] = jnp.full((8, C + 384), LOW, F32)
     column = iota((8, 384), 1)
@@ -385,6 +386,10 @@
     both = jnp.sum(caption, axis=1, keepdims=True) + jnp.sum(image, axis=1, keepdims=True)
     share = both / (2.0 * real[0:1, 0:1])
     total[...] = jnp.broadcast_to(share, (128, 8)).reshape(128, 1, 8)
+
+
+def sum_kernel(totals, loss):
+    loss[...] = jnp.sum(totals[...].reshape(128, 8)[:, 0:1], axis=0, keepdims=True)
 
 
 def small(mib, flops):
@@ -447,7 +452,7 @@
             *(shape((n, 1, 2 * B), F32) for n in (128, 1)),
             shape((CAP_ROWS, E), BF16), shape((IMG_ROWS, E), BF16),
         ],
-        in_specs=[SMEM] + [VMEM] * 6,
+        in_specs=[SMEM] + [VMEM] * 8,
         out_specs=[VMEM] * 4,
         input_output_aliases={3: 2, 4: 3},
         scratch_shapes=[
@@ -462,7 +467,7 @@
         cost_estimate=pl.CostEstimate(
             flops=R * C * E, bytes_accessed=2 * (R + C) * E, transcendentals=R * C
         ),
-    )(counts, columns, ranks, *buffers, carried[LATE], swapped[LATE])
+    )(counts, columns, ranks, *buffers, *carried[LATE:], *swapped[LATE:])
     parts = lax.all_to_all(out, AXES, 0, 0, tiled=True)
     caption_loss, image_loss, total = pl.pallas_call(
         loss_kernel,
@@ -473,7 +478,11 @@
         **small(4, 10**8),
     )(parts, own_row, ranks, image_ranks, real)
     totals = lax.all_to_all(total, AXES, 0, 0, tiled=True)
-    return caption_loss.reshape(B), image_loss.reshape(B), jnp.sum(totals[:, 0, 0])
+    loss = pl.pallas_call(
+        sum_kernel, out_shape=shape((1, 1), F32), in_specs=[VMEM], out_specs=VMEM,
+        **small(4, 10**6),
+    )(totals)
+    return caption_loss.reshape(B), image_loss.reshape(B), loss.reshape(())
 
 
 def solution(mesh):

time: 105 us -> 104 us (level)
  no operation moved by 1% of the time
where the time goes in v8:
time: 104 us; the launch traced here: 103 us
  blocking collectives  54.4 us (52%)
  starting transfers between devices  18.1 us (17%)
  waiting for transfers between devices  15.3 us (15%)
  Pallas kernels  13.1 us (13%)
  other arithmetic  1.69 us (2%)
    ppermute x18, starting transfers between devices, send(): return lax.ppermute(value, AXES, pairs)  18.1 us
    ppermute x18, waiting for transfers between devices, send(): return lax.ppermute(value, AXES, pairs)  15.3 us
    all_to_all x1, blocking collectives, step(): parts = lax.all_to_all(out, AXES, 0, 0, tiled=True)  14.5 us
    all_to_all x1, blocking collectives, step(): part = lax.all_to_all(words, ('x', 'h'), 0, 0, tiled=True)  14.4 us
    all_to_all x1, blocking collectives, step(): totals = lax.all_to_all(total, AXES, 0, 0, tiled=True)  13.9 us
    all_to_all x1, blocking collectives, step(): table = lax.all_to_all(part, ('z', 'l'), 0, 0, tiled=True)  11.6 us
    pallas_call x1, Pallas kernels, step(): pl.pallas_call(score_kernel, out_shape=[*(shape((n, 1, 2 * B), F32) for n...  7.47 us
    pallas_call x2, Pallas kernels, step(): pl.pallas_call(functools.partial(compact_kernel, part), out_shape=[shape(...  2.64 us
  transfers between devices with their start and end apart: 18, of which 5 were waited for; matrix products, arithmetic and copies ran while one was open for 2% of the time, Pallas kernels for 4%

profile of v8, /device:TPU:0, one launch (start us, length us, event | category | flops | bytes accessed | tf_op | source)
XLA Modules:
  0.0 103.3 jit_solution(3479076327544340103)
XLA Ops:
  0.6 0.1 collective-permute-start
  0.7 0.5 collective-permute-start.1
  1.2 0.7 multiply_add_fusion
  1.9 0.1 collective-permute-start.2
  2.0 1.0 broadcast_select_fusion.own
  3.0 0.1 collective-permute-done.2.word_other
  3.1 0.4 shard_map.67
  3.5 1.8 %collective-permute-start.3 = (bf16[384,768]{1,0:T(8,128)(2,1)S(1)}, bf16[384,768]{1,0:T(8,128)(2,1)S(1)}, u32[]{:S(2)}, u32[]{:S(2)}) collective-permute-start(bf16[384,768]{1,0:T(8,128)(2,1)S(1)} %get-tuple-element.23.refs_0_), channel_id=1, source_target_pairs={{0,1},{1,0},{2,19},{3,18},{4,5},{5,4},{6,23},{7,22},{8,9},{9,8},{1... | collective-permute-start | bytes 1769480 | tf_op jit(solution)/shard_map/ppermute | solution.py:51
  5.3 1.9 %collective-permute-start.4 = (bf16[384,768]{1,0:T(8,128)(2,1)S(1)}, bf16[384,768]{1,0:T(8,128)(2,1)S(1)}, u32[]{:S(2)}, u32[]{:S(2)}) collective-permute-start(bf16[384,768]{1,0:T(8,128)(2,1)S(1)} %get-tuple-element.23.refs_0_), channel_id=1, source_target_pairs={{0,4},{1,5},{2,34},{3,35},{4,8},{5,9},{6,38},{7,39},{8,12},{9,13},... | collective-permute-start | bytes 1769480 | tf_op jit(solution)/shard_map/ppermute | solution.py:51
  7.2 2.1 %collective-permute-start.5 = (bf16[384,768]{1,0:T(8,128)(2,1)S(1)}, bf16[384,768]{1,0:T(8,128)(2,1)S(1)}, u32[]{:S(2)}, u32[]{:S(2)}) collective-permute-start(bf16[384,768]{1,0:T(8,128)(2,1)S(1)} %get-tuple-element.23.refs_0_), channel_id=1, source_target_pairs={{0,12},{1,13},{2,98},{3,99},{4,0},{5,1},{6,102},{7,103},{8,4},{9,5... | collective-permute-start | bytes 1769480 | tf_op jit(solution)/shard_map/ppermute | solution.py:51
  9.4 0.2 collective-permute-start.6
  9.5 4.0 %collective-permute-done.3.refs_1_ = bf16[384,768]{1,0:T(8,128)(2,1)S(1)} collective-permute-done((bf16[384,768]{1,0:T(8,128)(2,1)S(1)}, bf16[384,768]{1,0:T(8,128)(2,1)S(1)}, u32[]{:S(2)}, u32[]{:S(2)}) %collective-permute-start.3) | collective-permute-done | bytes 589856 | tf_op jit(solution)/shard_map/ppermute | solution.py:51
  13.5 4.2 %collective-permute-start.11 = (bf16[384,768]{1,0:T(8,128)(2,1)S(1)}, bf16[384,768]{1,0:T(8,128)(2,1)S(1)}, u32[]{:S(2)}, u32[]{:S(2)}) collective-permute-start(bf16[384,768]{1,0:T(8,128)(2,1)S(1)} %collective-permute-done.3.refs_1_), channel_id=1, source_target_pairs={{0,12},{1,13},{2,98},{3,99},{4,0},{5,1},{6,102},{7,103},{8,4},{9,5... | collective-permute-start | bytes 1769480 | tf_op jit(solution)/shard_map/ppermute | solution.py:51
  17.7 0.5 collective-permute-start.8
  18.2 0.8 collective-permute-start.10
  19.0 1.6 %collective-permute-start.14 = (bf16[384,768]{1,0:T(8,128)(2,1)S(1)}, bf16[384,768]{1,0:T(8,128)(2,1)S(1)}, u32[]{:S(2)}, u32[]{:S(2)}) collective-permute-start(bf16[384,768]{1,0:T(8,128)(2,1)S(1)} %collective-permute-done.4.refs_2_), channel_id=1, source_target_pairs={{0,4},{1,5},{2,34},{3,35},{4,8},{5,9},{6,38},{7,39},{8,12},{9,13},... | collective-permute-start | bytes 1769480 | tf_op jit(solution)/shard_map/ppermute | solution.py:51
  20.7 4.4 %collective-permute-done.11.refs_3_ = bf16[384,768]{1,0:T(8,128)(2,1)S(1)} collective-permute-done((bf16[384,768]{1,0:T(8,128)(2,1)S(1)}, bf16[384,768]{1,0:T(8,128)(2,1)S(1)}, u32[]{:S(2)}, u32[]{:S(2)}) %collective-permute-start.11) | collective-permute-done | bytes 589856 | tf_op jit(solution)/shard_map/ppermute | solution.py:51
  25.1 3.7 %collective-permute-start.15 = (bf16[384,768]{1,0:T(8,128)(2,1)S(1)}, bf16[384,768]{1,0:T(8,128)(2,1)S(1)}, u32[]{:S(2)}, u32[]{:S(2)}) collective-permute-start(bf16[384,768]{1,0:T(8,128)(2,1)S(1)} %collective-permute-done.11.refs_3_), channel_id=1, source_target_pairs={{0,12},{1,13},{2,98},{3,99},{4,0},{5,1},{6,102},{7,103},{8,4},{9,5... | collective-permute-start | bytes 1769480 | tf_op jit(solution)/shard_map/ppermute | solution.py:51
  28.8 0.5 collective-permute-start.13
  29.3 0.1 collective-permute-start.12
  29.4 6.2 %collective-permute-done.14.c1 = bf16[384,768]{1,0:T(8,128)(2,1)S(1)} collective-permute-done((bf16[384,768]{1,0:T(8,128)(2,1)S(1)}, bf16[384,768]{1,0:T(8,128)(2,1)S(1)}, u32[]{:S(2)}, u32[]{:S(2)}) %collective-permute-start.14) | collective-permute-done | bytes 589856 | tf_op jit(solution)/shard_map/ppermute | solution.py:51
  35.6 0.6 collective-permute-done.15.c3
  36.2 14.4 %all_to_all.20.part = s32[8,2,192]{2,1,0:T(2,128)S(1)} all-to-all(s32[8,2,192]{2,1,0:T(2,128)S(1)} %get-tuple-element.19), channel_id=1, replica_groups=mesh['x'=4,'h'=2,'z'=4,'c'=2,'l'=2] {'x','h'}, dimensions={0} | all-to-all | bytes 24576 | tf_op jit(solution)/shard_map/all_to_all | solution.py:422
  50.6 11.6 %all_to_all.21.table = s32[8,16,192]{2,1,0:T(8,128)S(1)} all-to-all(s32[8,16,192]{2,1,0:T(8,128)S(1)} %shard_map.68), channel_id=1, replica_groups=mesh['x'=4,'h'=2,'z'=4,'c'=2,'l'=2] {'z','l'}, dimensions={0} | all-to-all | bytes 196608 | tf_op jit(solution)/shard_map/all_to_all | solution.py:427
  62.2 1.0 shard_map.69
  63.2 1.5 %shard_map.70 = (bf16[1984,768]{1,0:T(8,128)(2,1)S(1)}, bf16[3584,768]{1,0:T(8,128)(2,1)S(1)}) custom-call(s32[24,128]{1,0:T(8,128)S(1)} %get-tuple-element.20.counts, f32[8,192]{1,0:T(8,128)S(1)} %get-tuple-element.22.ranks.row_ranks, bf16[384,768]{1,0:T(8,128)(2,1)S(1)} %get-tuple-element.23.refs_0_, bf16[384,768]{1,0:T(8,128)(2,1)S(1)} %collective-permute-done.3.refs_1_, ...), custom_call_target="tpu_custom_call" | custom-call | flops 1000000000 | bytes 1000000 | tf_op jit(solution)/shard_map/pallas_call | solution.py:441
  64.7 1.1 %shard_map.71 = (bf16[1984,768]{1,0:T(8,128)(2,1)S(1)}, bf16[3584,768]{1,0:T(8,128)(2,1)S(1)}) custom-call(s32[24,128]{1,0:T(8,128)S(1)} %get-tuple-element.20.counts, f32[8,192]{1,0:T(8,128)S(1)} %get-tuple-element.22.ranks.row_ranks, bf16[1984,768]{1,0:T(8,128)(2,1)S(1)} %get-tuple-element.24.refs_0_, ...), custom_call_target="tpu_custom_call", output_to_operand_aliasing={{0}: (2, {}), {1}: (3, {})} | custom-call | flops 1000000000 | bytes 1000000 | tf_op jit(solution)/shard_map/pallas_call | solution.py:441
  65.9 7.5 %shard_map.72 = (f32[128,1,384]{2,1,0:T(1,128)S(1)}, f32[1,1,384]{2,1,0:T(1,128)S(1)}, bf16[1984,768]{1,0:T(8,128)(2,1)S(1)}, bf16[3584,768]{1,0:T(8,128)(2,1)S(1)}) custom-call(s32[24,128]{1,0:T(8,128)S(1)} %get-tuple-element.20.counts, f32[192,128]{1,0:T(8,128)S(1)} %get-tuple-element.21.columns, ...), custom_call_target="tpu_custom_call", output_to_operand_aliasing={{2}: (3, {}), {3}: (4, {})} | custom-call | flops 4227858432 | bytes 7471104 | tf_op jit(solution)/shard_map/pallas_call | solution.py:449
  73.4 14.5 %all_to_all.22.parts = f32[128,1,384]{2,1,0:T(1,128)S(1)} all-to-all(f32[128,1,384]{2,1,0:T(1,128)S(1)} %get-tuple-element.28), channel_id=1, replica_groups=mesh['x'=4,'h'=2,'z'=4,'c'=2,'l'=2] {'x','h','z','c','l'}, dimensions={0} | all-to-all | bytes 393216 | tf_op jit(solution)/shard_map/all_to_all | solution.py:471
  87.9 0.9 shard_map.73
  88.8 13.9 %all_to_all.23.totals = f32[128,1,8]{2,1,0:T(1,128)S(1)} all-to-all(f32[128,1,8]{2,1,0:T(1,128)S(1)} %get-tuple-element.34), channel_id=1, replica_groups=mesh['x'=4,'h'=2,'z'=4,'c'=2,'l'=2] {'x','h','z','c','l'}, dimensions={0} | all-to-all | bytes 8192 | tf_op jit(solution)/shard_map/all_to_all | solution.py:480
  102.7 0.6 shard_map.74
  (18 shorter events, 0.1 us)
Async XLA Ops:
  0.6 2.5 %collective-permute-start = (bf16[192,768]{1,0:T(8,128)(2,1)}, bf16[192,768]{1,0:T(8,128)(2,1)S(1)}, u32[]{:S(2)}, u32[]{:S(2)}) collective-permute-start(bf16[192,768]{1,0:T(8,128)(2,1)} %param.4), channel_id=1, source_target_pairs={{0,2},{1,3},{2,0},{3,1},{4,6},{5,7},{6,4},{7,5},{8,10},{9,11},{10,... | collective-permute-start | bytes 884744 | tf_op jit(solution)/shard_map/ppermute | solution.py:51
  0.7 2.4 %collective-permute-start.1 = (bf16[192,768]{1,0:T(8,128)(2,1)}, bf16[192,768]{1,0:T(8,128)(2,1)S(1)}, u32[]{:S(2)}, u32[]{:S(2)}) collective-permute-start(bf16[192,768]{1,0:T(8,128)(2,1)} %param.5), channel_id=1, source_target_pairs={{0,2},{1,3},{2,0},{3,1},{4,6},{5,7},{6,4},{7,5},{8,10},{9,11},{10,... | collective-permute-start | bytes 884744 | tf_op jit(solution)/shard_map/ppermute | solution.py:51
  1.9 1.2 %collective-permute-start.2 = (s32[1,192]{1,0:T(1,128)S(1)}, s32[1,192]{1,0:T(1,128)S(1)}, u32[]{:S(2)}, u32[]{:S(2)}) collective-permute-start(s32[1,192]{1,0:T(1,128)S(1)} %bitcast.4), channel_id=1, source_target_pairs={{0,2},{1,3},{2,0},{3,1},{4,6},{5,7},{6,4},{7,5},{8,10},{9,11},{10,... | collective-permute-start | bytes 2312 | tf_op jit(solution)/shard_map/ppermute | solution.py:51
  3.5 10.0 %collective-permute-start.3 = (bf16[384,768]{1,0:T(8,128)(2,1)S(1)}, bf16[384,768]{1,0:T(8,128)(2,1)S(1)}, u32[]{:S(2)}, u32[]{:S(2)}) collective-permute-start(bf16[384,768]{1,0:T(8,128)(2,1)S(1)} %get-tuple-element.23.refs_0_), channel_id=1, source_target_pairs={{0,1},{1,0},{2,19},{3,18},{4,5},{5,4},{6,23},{7,22},{8,9},{9,8},{1... | collective-permute-start | bytes 1769480 | tf_op jit(solution)/shard_map/ppermute | solution.py:51
  5.3 12.4 %collective-permute-start.4 = (bf16[384,768]{1,0:T(8,128)(2,1)S(1)}, bf16[384,768]{1,0:T(8,128)(2,1)S(1)}, u32[]{:S(2)}, u32[]{:S(2)}) collective-permute-start(bf16[384,768]{1,0:T(8,128)(2,1)S(1)} %get-tuple-element.23.refs_0_), channel_id=1, source_target_pairs={{0,4},{1,5},{2,34},{3,35},{4,8},{5,9},{6,38},{7,39},{8,12},{9,13},... | collective-permute-start | bytes 1769480 | tf_op jit(solution)/shard_map/ppermute | solution.py:51
  7.2 10.9 %collective-permute-start.5 = (bf16[384,768]{1,0:T(8,128)(2,1)S(1)}, bf16[384,768]{1,0:T(8,128)(2,1)S(1)}, u32[]{:S(2)}, u32[]{:S(2)}) collective-permute-start(bf16[384,768]{1,0:T(8,128)(2,1)S(1)} %get-tuple-element.23.refs_0_), channel_id=1, source_target_pairs={{0,12},{1,13},{2,98},{3,99},{4,0},{5,1},{6,102},{7,103},{8,4},{9,5... | collective-permute-start | bytes 1769480 | tf_op jit(solution)/shard_map/ppermute | solution.py:51
  9.4 9.7 %collective-permute-start.6 = (bf16[384,768]{1,0:T(8,128)(2,1)S(1)}, bf16[384,768]{1,0:T(8,128)(2,1)S(1)}, u32[]{:S(2)}, u32[]{:S(2)}) collective-permute-start(bf16[384,768]{1,0:T(8,128)(2,1)S(1)} %get-tuple-element.23.refs_0_), channel_id=1, source_target_pairs={{0,2},{1,3},{2,0},{3,1},{4,6},{5,7},{6,4},{7,5},{8,10},{9,11},{10,... | collective-permute-start | bytes 1769480 | tf_op jit(solution)/shard_map/ppermute | solution.py:51
  13.5 11.6 %collective-permute-start.11 = (bf16[384,768]{1,0:T(8,128)(2,1)S(1)}, bf16[384,768]{1,0:T(8,128)(2,1)S(1)}, u32[]{:S(2)}, u32[]{:S(2)}) collective-permute-start(bf16[384,768]{1,0:T(8,128)(2,1)S(1)} %collective-permute-done.3.refs_1_), channel_id=1, source_target_pairs={{0,12},{1,13},{2,98},{3,99},{4,0},{5,1},{6,102},{7,103},{8,4},{9,5... | collective-permute-start | bytes 1769480 | tf_op jit(solution)/shard_map/ppermute | solution.py:51
  17.7 11.1 %collective-permute-start.7 = (bf16[384,768]{1,0:T(8,128)(2,1)S(1)}, bf16[384,768]{1,0:T(8,128)(2,1)S(1)}, u32[]{:S(2)}, u32[]{:S(2)}) collective-permute-start(bf16[384,768]{1,0:T(8,128)(2,1)S(1)} %collective-permute-done.3.refs_1_), channel_id=1, source_target_pairs={{0,2},{1,3},{2,0},{3,1},{4,6},{5,7},{6,4},{7,5},{8,10},{9,11},{10,... | collective-permute-start | bytes 1769480 | tf_op jit(solution)/shard_map/ppermute | solution.py:51
  17.7 11.1 %collective-permute-start.8 = (bf16[384,768]{1,0:T(8,128)(2,1)S(1)}, bf16[384,768]{1,0:T(8,128)(2,1)S(1)}, u32[]{:S(2)}, u32[]{:S(2)}) collective-permute-start(bf16[384,768]{1,0:T(8,128)(2,1)S(1)} %collective-permute-done.4.refs_2_), channel_id=1, source_target_pairs={{0,2},{1,3},{2,0},{3,1},{4,6},{5,7},{6,4},{7,5},{8,10},{9,11},{10,... | collective-permute-start | bytes 1769480 | tf_op jit(solution)/shard_map/ppermute | solution.py:51
  18.2 11.1 %collective-permute-start.10 = (bf16[384,768]{1,0:T(8,128)(2,1)S(1)}, bf16[384,768]{1,0:T(8,128)(2,1)S(1)}, u32[]{:S(2)}, u32[]{:S(2)}) collective-permute-start(bf16[384,768]{1,0:T(8,128)(2,1)S(1)} %collective-permute-done.3.refs_1_), channel_id=1, source_target_pairs={{0,4},{1,5},{2,34},{3,35},{4,8},{5,9},{6,38},{7,39},{8,12},{9,13},... | collective-permute-start | bytes 1769480 | tf_op jit(solution)/shard_map/ppermute | solution.py:51
  19.0 16.6 %collective-permute-start.14 = (bf16[384,768]{1,0:T(8,128)(2,1)S(1)}, bf16[384,768]{1,0:T(8,128)(2,1)S(1)}, u32[]{:S(2)}, u32[]{:S(2)}) collective-permute-start(bf16[384,768]{1,0:T(8,128)(2,1)S(1)} %collective-permute-done.4.refs_2_), channel_id=1, source_target_pairs={{0,4},{1,5},{2,34},{3,35},{4,8},{5,9},{6,38},{7,39},{8,12},{9,13},... | collective-permute-start | bytes 1769480 | tf_op jit(solution)/shard_map/ppermute | solution.py:51
  25.1 11.1 %collective-permute-start.15 = (bf16[384,768]{1,0:T(8,128)(2,1)S(1)}, bf16[384,768]{1,0:T(8,128)(2,1)S(1)}, u32[]{:S(2)}, u32[]{:S(2)}) collective-permute-start(bf16[384,768]{1,0:T(8,128)(2,1)S(1)} %collective-permute-done.11.refs_3_), channel_id=1, source_target_pairs={{0,12},{1,13},{2,98},{3,99},{4,0},{5,1},{6,102},{7,103},{8,4},{9,5... | collective-permute-start | bytes 1769480 | tf_op jit(solution)/shard_map/ppermute | solution.py:51
  28.8 34.4 %collective-permute-start.9 = (bf16[384,768]{1,0:T(8,128)(2,1)S(1)}, bf16[384,768]{1,0:T(8,128)(2,1)S(1)}, u32[]{:S(2)}, u32[]{:S(2)}) collective-permute-start(bf16[384,768]{1,0:T(8,128)(2,1)S(1)} %collective-permute-done.5.refs_3_), channel_id=1, source_target_pairs={{0,2},{1,3},{2,0},{3,1},{4,6},{5,7},{6,4},{7,5},{8,10},{9,11},{10,... | collective-permute-start | bytes 1769480 | tf_op jit(solution)/shard_map/ppermute | solution.py:51
  28.8 35.9 %collective-permute-start.13 = (bf16[384,768]{1,0:T(8,128)(2,1)S(1)}, bf16[384,768]{1,0:T(8,128)(2,1)S(1)}, u32[]{:S(2)}, u32[]{:S(2)}) collective-permute-start(bf16[384,768]{1,0:T(8,128)(2,1)S(1)} %collective-permute-done.11.refs_3_), channel_id=1, source_target_pairs={{0,2},{1,3},{2,0},{3,1},{4,6},{5,7},{6,4},{7,5},{8,10},{9,11},{10,... | collective-permute-start | bytes 1769480 | tf_op jit(solution)/shard_map/ppermute | solution.py:51
  29.3 35.4 %collective-permute-start.12 = (bf16[384,768]{1,0:T(8,128)(2,1)S(1)}, bf16[384,768]{1,0:T(8,128)(2,1)S(1)}, u32[]{:S(2)}, u32[]{:S(2)}) collective-permute-start(bf16[384,768]{1,0:T(8,128)(2,1)S(1)} %collective-permute-done.10.refs_2_), channel_id=1, source_target_pairs={{0,2},{1,3},{2,0},{3,1},{4,6},{5,7},{6,4},{7,5},{8,10},{9,11},{10,... | collective-permute-start | bytes 1769480 | tf_op jit(solution)/shard_map/ppermute | solution.py:51
  35.6 30.3 %collective-permute-start.16 = (bf16[384,768]{1,0:T(8,128)(2,1)S(1)}, bf16[384,768]{1,0:T(8,128)(2,1)S(1)}, u32[]{:S(2)}, u32[]{:S(2)}) collective-permute-start(bf16[384,768]{1,0:T(8,128)(2,1)S(1)} %collective-permute-done.14.c1), channel_id=1, source_target_pairs={{0,2},{1,3},{2,0},{3,1},{4,6},{5,7},{6,4},{7,5},{8,10},{9,11},{10,... | collective-permute-start | bytes 1769480 | tf_op jit(solution)/shard_map/ppermute | solution.py:51
  36.2 29.7 %collective-permute-start.17 = (bf16[384,768]{1,0:T(8,128)(2,1)S(1)}, bf16[384,768]{1,0:T(8,128)(2,1)S(1)}, u32[]{:S(2)}, u32[]{:S(2)}) collective-permute-start(bf16[384,768]{1,0:T(8,128)(2,1)S(1)} %collective-permute-done.15.c3), channel_id=1, source_target_pairs={{0,2},{1,3},{2,0},{3,1},{4,6},{5,7},{6,4},{7,5},{8,10},{9,11},{10,... | collective-permute-start | bytes 1769480 | tf_op jit(solution)/shard_map/ppermute | solution.py:51
